TPU v7x, 128 devices: a whole 4x4x4 slice. The times are simulated.
128 devices in a mesh: gx: 8 (over y, z_lo), gz: 16 (over z_hi, x, core).
Axes of the slice: x: 4, y: 4, z: 4 (z_hi: 2, z_lo: 2; z = z_hi * 2 + z_lo), core: 2. Of those that a mesh axis runs over, the one named last changes fastest.
Arguments:
- sources: float32 [16, 8, 8, 1280, 128], P('gz', 'gx'), may hold values from -6 to 6
- green: float32 [16, 8, 1280, 1280], P('gz', 'gx'), may hold values from -0.2 to 1.2
- probe: float32 [16, 8, 1024, 1280], P('gz', 'gx'), may hold values from -0.0625 to 0.0625
- batch_pick: int32 [8, 23], replicated, may hold values from 0 to 7
- owner_map: int32 [16, 512], P('gz'), may hold values from 0 to 511, each once within a row
Outputs:
- outgoing: float32 [16, 8, 1280, 1024], P('gz', 'gx')
- receiver_data: float32 [16, 2, 512, 1024], P('gz', None, 'gx')
Inputs may be any that keep to these rules, and one draw needn't show every extreme that they name: Each row of owner_map holds every receiver once; slot q belongs to the column q // (512 // 8).
All inputs are finite; a program needn't handle non-finite values.
Results may differ from a plain program's by a relative error of at most 0.00013.
Values sent between devices are 32-bit elements; how exact they have to be, the bound alone decides.
No kernel may reach another device: no remote copies, remote signals or barrier semaphores. Data moves between devices by JAX's collectives and lax.ppermute only.
A program may use at most 128 MiB of HBM per device.

v0:
```python
import jax
import jax.numpy as jnp
from jax import lax
from jax.sharding import PartitionSpec as P


def passed_along(value, axis, steps):
    count = lax.axis_size(axis)
    first, last = (max(0, -steps), min(count, count - steps))
    return lax.ppermute(value, axis, [(source, source + steps) for source in range(first, last)])


def split_up(x, dim, count):
    before, after = (x.shape[:dim], x.shape[dim + 1 :])
    return jnp.moveaxis(x.reshape(*before, count, -1, *after), dim, 0)


def sum_at_owner(x, axis, dim):
    parts = split_up(x, dim, lax.axis_size(axis))
    arrived = lax.all_to_all(parts, axis, split_axis=0, concat_axis=0, tiled=True)
    return arrived.sum(axis=0)


def local(sources, green, probe, batch_pick, owner_map):
    column = lax.axis_index("gx")
    row = lax.axis_index("gz")
    diag = row + column
    operator = green[0, 0]
    local_sources = sources[0, 0]
    trace = operator.shape[0]
    shots = local_sources.shape[2]
    window = batch_pick.shape[0]
    total = window * shots
    units = total // shots
    steps = units + lax.axis_size("gx") + lax.axis_size("gz") - 2

    def advance(step, carry):
        upper, lefter, traces = carry
        unit = step - diag
        active = jnp.logical_and(unit >= 0, unit < units)
        start = jnp.clip(unit, 0, units - 1) * shots
        batch = start // shots
        chosen = batch_pick[batch, diag]
        source_set = lax.dynamic_index_in_dim(local_sources, chosen, 0, keepdims=False)

        def work(stored):
            inflow = source_set + 0.5 * (upper + lefter)
            result = jnp.dot(
                operator,
                inflow,
                precision=lax.Precision.HIGHEST,
                preferred_element_type=jnp.float32,
            )
            return (result, lax.dynamic_update_slice_in_dim(stored, result, start, 1))

        def skip(stored):
            return (jnp.zeros((trace, shots), jnp.float32), stored)

        result, traces = lax.cond(active, work, skip, traces)
        lower = passed_along(result, "gz", 1)
        righter = passed_along(result, "gx", 1)
        return (lower, righter, traces)

    blank = jnp.zeros((trace, shots), jnp.float32)
    start_traces = jnp.zeros((trace, total), jnp.float32)
    upper, lefter, traces = lax.fori_loop(0, steps, advance, (blank, blank, start_traces))
    partial_value = jnp.dot(
        probe[0, 0], traces, precision=lax.Precision.HIGHEST, preferred_element_type=jnp.float32
    )
    receivers = owner_map.shape[1]
    partial_value = partial_value.reshape(2, receivers, total)
    ordered = jnp.take(partial_value, owner_map[0], axis=1)
    shared = sum_at_owner(ordered, "gx", 1)
    return (traces[None, None], shared[None])


def solution(mesh):
    return jax.shard_map(
        local,
        mesh=mesh,
        in_specs=(
            P("gz", "gx", None, None, None),
            P("gz", "gx", None, None),
            P("gz", "gx", None, None),
            P(),
            P("gz", None),
        ),
        out_specs=(P("gz", "gx", None, None), P("gz", None, "gx", None)),
        check_vma=False,
    )
```

profile of v0, /device:TPU:0, one launch (start us, length us, event | category | flops | bytes accessed | tf_op | source)
XLA Modules:
  0.0 1048.6 jit_solution(5266626794905340231)
XLA Ops:
  3.4 917.0 %while.22 = (s32[]{:T(128)}, f32[1280,128]{0,1:T(8,128)S(1)}, f32[1280,128]{0,1:T(8,128)S(1)}, f32[1280,1024]{0,1:T(8,128)}, s32[]{:T(128)}, /*index=5*/s32[8,23...) while((s32[]{:T(128)}, f32[1280,128]{0,1:T(8,128)S(1)}, ...), condition=%wide.region_3.4_spmd, body=%wide.region_0.3_spmd.sunk | while | flops 2517073920 | bytes 18350752 | solution.py:66
  3.4 16.3 %conditional.2 = (f32[1280,128]{0,1:T(8,128)}, f32[1280,1024]{0,1:T(8,128)}) conditional(s32[]{:T(128)} %convert_element_type.11, f32[1280,1024]{0,1:T(8,128)} %get-tuple-element.577, (s32[]{:T(128)}, pred[]{:T(512)}, pred[]{:T(512)}, s32[]{:T(128)}, s32[8,23]{1,0:T(8,128)}, /*index=5*/s32[]{:T(128)}, f32[8,1280,128]{2,1,0:T(8,128)}, ...), branch_computations={%region_1.1_spmd, %region_2.2_spmd.clone} | conditional | flops 2517073920 | bytes 13107479 | solution.py:59
  7.1 9.5 convolution_bitcast_fusion
  22.9 10.3 collective-permute-done.1
  33.2 16.3 %conditional.2 = (f32[1280,128]{0,1:T(8,128)}, f32[1280,1024]{0,1:T(8,128)}) conditional(s32[]{:T(128)} %convert_element_type.11, f32[1280,1024]{0,1:T(8,128)} %get-tuple-element.577, (s32[]{:T(128)}, pred[]{:T(512)}, pred[]{:T(512)}, s32[]{:T(128)}, s32[8,23]{1,0:T(8,128)}, /*index=5*/s32[]{:T(128)}, f32[8,1280,128]{2,1,0:T(8,128)}, ...), branch_computations={%region_1.1_spmd, %region_2.2_spmd.clone} | conditional | flops 2517073920 | bytes 13107479 | solution.py:59
  36.9 9.5 convolution_bitcast_fusion
  55.1 15.4 %collective-permute-done.1 = f32[1280,128]{0,1:T(8,128)S(1)} collective-permute-done((f32[1280,128]{0,1:T(8,128)}, f32[1280,128]{0,1:T(8,128)S(1)}, u32[]{:S(2)}, u32[]{:S(2)}) %collective-permute-start.1) | collective-permute-done | bytes 655392 | tf_op jit(solution)/shard_map/while/body/eval_jaxpr/ppermute | solution.py:10
  70.5 16.3 %conditional.2 = (f32[1280,128]{0,1:T(8,128)}, f32[1280,1024]{0,1:T(8,128)}) conditional(s32[]{:T(128)} %convert_element_type.11, f32[1280,1024]{0,1:T(8,128)} %get-tuple-element.577, (s32[]{:T(128)}, pred[]{:T(512)}, pred[]{:T(512)}, s32[]{:T(128)}, s32[8,23]{1,0:T(8,128)}, /*index=5*/s32[]{:T(128)}, f32[8,1280,128]{2,1,0:T(8,128)}, ...), branch_computations={%region_1.1_spmd, %region_2.2_spmd.clone} | conditional | flops 2517073920 | bytes 13107479 | solution.py:59
  74.2 9.5 convolution_bitcast_fusion
  92.5 8.3 collective-permute-done.1
  100.8 16.3 %conditional.2 = (f32[1280,128]{0,1:T(8,128)}, f32[1280,1024]{0,1:T(8,128)}) conditional(s32[]{:T(128)} %convert_element_type.11, f32[1280,1024]{0,1:T(8,128)} %get-tuple-element.577, (s32[]{:T(128)}, pred[]{:T(512)}, pred[]{:T(512)}, s32[]{:T(128)}, s32[8,23]{1,0:T(8,128)}, /*index=5*/s32[]{:T(128)}, f32[8,1280,128]{2,1,0:T(8,128)}, ...), branch_computations={%region_1.1_spmd, %region_2.2_spmd.clone} | conditional | flops 2517073920 | bytes 13107479 | solution.py:59
  104.5 9.5 convolution_bitcast_fusion
  122.7 15.4 %collective-permute-done.1 = f32[1280,128]{0,1:T(8,128)S(1)} collective-permute-done((f32[1280,128]{0,1:T(8,128)}, f32[1280,128]{0,1:T(8,128)S(1)}, u32[]{:S(2)}, u32[]{:S(2)}) %collective-permute-start.1) | collective-permute-done | bytes 655392 | tf_op jit(solution)/shard_map/while/body/eval_jaxpr/ppermute | solution.py:10
  138.1 16.3 %conditional.2 = (f32[1280,128]{0,1:T(8,128)}, f32[1280,1024]{0,1:T(8,128)}) conditional(s32[]{:T(128)} %convert_element_type.11, f32[1280,1024]{0,1:T(8,128)} %get-tuple-element.577, (s32[]{:T(128)}, pred[]{:T(512)}, pred[]{:T(512)}, s32[]{:T(128)}, s32[8,23]{1,0:T(8,128)}, /*index=5*/s32[]{:T(128)}, f32[8,1280,128]{2,1,0:T(8,128)}, ...), branch_computations={%region_1.1_spmd, %region_2.2_spmd.clone} | conditional | flops 2517073920 | bytes 13107479 | solution.py:59
  141.8 9.5 convolution_bitcast_fusion
  160.0 8.3 collective-permute-done.1
  168.4 16.3 %conditional.2 = (f32[1280,128]{0,1:T(8,128)}, f32[1280,1024]{0,1:T(8,128)}) conditional(s32[]{:T(128)} %convert_element_type.11, f32[1280,1024]{0,1:T(8,128)} %get-tuple-element.577, (s32[]{:T(128)}, pred[]{:T(512)}, pred[]{:T(512)}, s32[]{:T(128)}, s32[8,23]{1,0:T(8,128)}, /*index=5*/s32[]{:T(128)}, f32[8,1280,128]{2,1,0:T(8,128)}, ...), branch_computations={%region_1.1_spmd, %region_2.2_spmd.clone} | conditional | flops 2517073920 | bytes 13107479 | solution.py:59
  172.1 9.5 convolution_bitcast_fusion
  190.3 15.4 %collective-permute-done.1 = f32[1280,128]{0,1:T(8,128)S(1)} collective-permute-done((f32[1280,128]{0,1:T(8,128)}, f32[1280,128]{0,1:T(8,128)S(1)}, u32[]{:S(2)}, u32[]{:S(2)}) %collective-permute-start.1) | collective-permute-done | bytes 655392 | tf_op jit(solution)/shard_map/while/body/eval_jaxpr/ppermute | solution.py:10
  205.7 16.3 %conditional.2 = (f32[1280,128]{0,1:T(8,128)}, f32[1280,1024]{0,1:T(8,128)}) conditional(s32[]{:T(128)} %convert_element_type.11, f32[1280,1024]{0,1:T(8,128)} %get-tuple-element.577, (s32[]{:T(128)}, pred[]{:T(512)}, pred[]{:T(512)}, s32[]{:T(128)}, s32[8,23]{1,0:T(8,128)}, /*index=5*/s32[]{:T(128)}, f32[8,1280,128]{2,1,0:T(8,128)}, ...), branch_computations={%region_1.1_spmd, %region_2.2_spmd.clone} | conditional | flops 2517073920 | bytes 13107479 | solution.py:59
  209.4 9.5 convolution_bitcast_fusion
  227.6 10.3 collective-permute-done.1
  237.9 16.0 %conditional.2 = (f32[1280,128]{0,1:T(8,128)}, f32[1280,1024]{0,1:T(8,128)}) conditional(s32[]{:T(128)} %convert_element_type.11, f32[1280,1024]{0,1:T(8,128)} %get-tuple-element.577, (s32[]{:T(128)}, pred[]{:T(512)}, pred[]{:T(512)}, s32[]{:T(128)}, s32[8,23]{1,0:T(8,128)}, /*index=5*/s32[]{:T(128)}, f32[8,1280,128]{2,1,0:T(8,128)}, ...), branch_computations={%region_1.1_spmd, %region_2.2_spmd.clone} | conditional | flops 2517073920 | bytes 13107479 | solution.py:59
  241.6 9.5 convolution_bitcast_fusion
  259.9 10.1 collective-permute-done.1
  275.5 16.2 %collective-permute-start.1 = (f32[1280,128]{0,1:T(8,128)}, f32[1280,128]{0,1:T(8,128)S(1)}, u32[]{:S(2)}, u32[]{:S(2)}) collective-permute-start(f32[1280,128]{0,1:T(8,128)} %get-tuple-element.554), channel_id=1, source_target_pairs={{0,16},{16,32},{32,48},{48,64},{64,80},{80,96},{96,112},{1,17},{17... | collective-permute-start | bytes 1966088 | tf_op jit(solution)/shard_map/while/body/eval_jaxpr/ppermute | solution.py:10
  291.7 10.4 collective-permute-done.1
  304.3 18.7 %collective-permute-start.1 = (f32[1280,128]{0,1:T(8,128)}, f32[1280,128]{0,1:T(8,128)S(1)}, u32[]{:S(2)}, u32[]{:S(2)}) collective-permute-start(f32[1280,128]{0,1:T(8,128)} %get-tuple-element.554), channel_id=1, source_target_pairs={{0,16},{16,32},{32,48},{48,64},{64,80},{80,96},{96,112},{1,17},{17... | collective-permute-start | bytes 1966088 | tf_op jit(solution)/shard_map/while/body/eval_jaxpr/ppermute | solution.py:10
  323.1 20.4 %collective-permute-done.1 = f32[1280,128]{0,1:T(8,128)S(1)} collective-permute-done((f32[1280,128]{0,1:T(8,128)}, f32[1280,128]{0,1:T(8,128)S(1)}, u32[]{:S(2)}, u32[]{:S(2)}) %collective-permute-start.1) | collective-permute-done | bytes 655392 | tf_op jit(solution)/shard_map/while/body/eval_jaxpr/ppermute | solution.py:10
  350.6 22.0 %collective-permute-done.1 = f32[1280,128]{0,1:T(8,128)S(1)} collective-permute-done((f32[1280,128]{0,1:T(8,128)}, f32[1280,128]{0,1:T(8,128)S(1)}, u32[]{:S(2)}, u32[]{:S(2)}) %collective-permute-start.1) | collective-permute-done | bytes 655392 | tf_op jit(solution)/shard_map/while/body/eval_jaxpr/ppermute | solution.py:10
  375.1 10.3 collective-permute-start.1
  385.4 21.1 %collective-permute-done.1 = f32[1280,128]{0,1:T(8,128)S(1)} collective-permute-done((f32[1280,128]{0,1:T(8,128)}, f32[1280,128]{0,1:T(8,128)S(1)}, u32[]{:S(2)}, u32[]{:S(2)}) %collective-permute-start.1) | collective-permute-done | bytes 655392 | tf_op jit(solution)/shard_map/while/body/eval_jaxpr/ppermute | solution.py:10
  408.7 7.2 collective-permute-start.1
  415.9 21.4 %collective-permute-done.1 = f32[1280,128]{0,1:T(8,128)S(1)} collective-permute-done((f32[1280,128]{0,1:T(8,128)}, f32[1280,128]{0,1:T(8,128)S(1)}, u32[]{:S(2)}, u32[]{:S(2)}) %collective-permute-start.1) | collective-permute-done | bytes 655392 | tf_op jit(solution)/shard_map/while/body/eval_jaxpr/ppermute | solution.py:10
  439.5 8.6 collective-permute-start.1
  448.1 20.9 %collective-permute-done.1 = f32[1280,128]{0,1:T(8,128)S(1)} collective-permute-done((f32[1280,128]{0,1:T(8,128)}, f32[1280,128]{0,1:T(8,128)S(1)}, u32[]{:S(2)}, u32[]{:S(2)}) %collective-permute-start.1) | collective-permute-done | bytes 655392 | tf_op jit(solution)/shard_map/while/body/eval_jaxpr/ppermute | solution.py:10
  475.6 20.6 %collective-permute-done.1 = f32[1280,128]{0,1:T(8,128)S(1)} collective-permute-done((f32[1280,128]{0,1:T(8,128)}, f32[1280,128]{0,1:T(8,128)S(1)}, u32[]{:S(2)}, u32[]{:S(2)}) %collective-permute-start.1) | collective-permute-done | bytes 655392 | tf_op jit(solution)/shard_map/while/body/eval_jaxpr/ppermute | solution.py:10
  498.4 10.6 %collective-permute-start.1 = (f32[1280,128]{0,1:T(8,128)}, f32[1280,128]{0,1:T(8,128)S(1)}, u32[]{:S(2)}, u32[]{:S(2)}) collective-permute-start(f32[1280,128]{0,1:T(8,128)} %get-tuple-element.554), channel_id=1, source_target_pairs={{0,16},{16,32},{32,48},{48,64},{64,80},{80,96},{96,112},{1,17},{17... | collective-permute-start | bytes 1966088 | tf_op jit(solution)/shard_map/while/body/eval_jaxpr/ppermute | solution.py:10
  509.0 19.1 %collective-permute-done.1 = f32[1280,128]{0,1:T(8,128)S(1)} collective-permute-done((f32[1280,128]{0,1:T(8,128)}, f32[1280,128]{0,1:T(8,128)S(1)}, u32[]{:S(2)}, u32[]{:S(2)}) %collective-permute-start.1) | collective-permute-done | bytes 655392 | tf_op jit(solution)/shard_map/while/body/eval_jaxpr/ppermute | solution.py:10
  534.6 19.2 %collective-permute-done.1 = f32[1280,128]{0,1:T(8,128)S(1)} collective-permute-done((f32[1280,128]{0,1:T(8,128)}, f32[1280,128]{0,1:T(8,128)S(1)}, u32[]{:S(2)}, u32[]{:S(2)}) %collective-permute-start.1) | collective-permute-done | bytes 655392 | tf_op jit(solution)/shard_map/while/body/eval_jaxpr/ppermute | solution.py:10
  556.0 10.9 %collective-permute-start.1 = (f32[1280,128]{0,1:T(8,128)}, f32[1280,128]{0,1:T(8,128)S(1)}, u32[]{:S(2)}, u32[]{:S(2)}) collective-permute-start(f32[1280,128]{0,1:T(8,128)} %get-tuple-element.554), channel_id=1, source_target_pairs={{0,16},{16,32},{32,48},{48,64},{64,80},{80,96},{96,112},{1,17},{17... | collective-permute-start | bytes 1966088 | tf_op jit(solution)/shard_map/while/body/eval_jaxpr/ppermute | solution.py:10
  567.0 20.3 %collective-permute-done.1 = f32[1280,128]{0,1:T(8,128)S(1)} collective-permute-done((f32[1280,128]{0,1:T(8,128)}, f32[1280,128]{0,1:T(8,128)S(1)}, u32[]{:S(2)}, u32[]{:S(2)}) %collective-permute-start.1) | collective-permute-done | bytes 655392 | tf_op jit(solution)/shard_map/while/body/eval_jaxpr/ppermute | solution.py:10
  593.9 20.1 %collective-permute-done.1 = f32[1280,128]{0,1:T(8,128)S(1)} collective-permute-done((f32[1280,128]{0,1:T(8,128)}, f32[1280,128]{0,1:T(8,128)S(1)}, u32[]{:S(2)}, u32[]{:S(2)}) %collective-permute-start.1) | collective-permute-done | bytes 655392 | tf_op jit(solution)/shard_map/while/body/eval_jaxpr/ppermute | solution.py:10
  616.2 16.1 %collective-permute-start.1 = (f32[1280,128]{0,1:T(8,128)}, f32[1280,128]{0,1:T(8,128)S(1)}, u32[]{:S(2)}, u32[]{:S(2)}) collective-permute-start(f32[1280,128]{0,1:T(8,128)} %get-tuple-element.554), channel_id=1, source_target_pairs={{0,16},{16,32},{32,48},{48,64},{64,80},{80,96},{96,112},{1,17},{17... | collective-permute-start | bytes 1966088 | tf_op jit(solution)/shard_map/while/body/eval_jaxpr/ppermute | solution.py:10
  632.3 17.6 %collective-permute-done.1 = f32[1280,128]{0,1:T(8,128)S(1)} collective-permute-done((f32[1280,128]{0,1:T(8,128)}, f32[1280,128]{0,1:T(8,128)S(1)}, u32[]{:S(2)}, u32[]{:S(2)}) %collective-permute-start.1) | collective-permute-done | bytes 655392 | tf_op jit(solution)/shard_map/while/body/eval_jaxpr/ppermute | solution.py:10
  659.2 18.7 %collective-permute-done.1 = f32[1280,128]{0,1:T(8,128)S(1)} collective-permute-done((f32[1280,128]{0,1:T(8,128)}, f32[1280,128]{0,1:T(8,128)S(1)}, u32[]{:S(2)}, u32[]{:S(2)}) %collective-permute-start.1) | collective-permute-done | bytes 655392 | tf_op jit(solution)/shard_map/while/body/eval_jaxpr/ppermute | solution.py:10
  685.6 19.0 %collective-permute-done.1 = f32[1280,128]{0,1:T(8,128)S(1)} collective-permute-done((f32[1280,128]{0,1:T(8,128)}, f32[1280,128]{0,1:T(8,128)S(1)}, u32[]{:S(2)}, u32[]{:S(2)}) %collective-permute-start.1) | collective-permute-done | bytes 655392 | tf_op jit(solution)/shard_map/while/body/eval_jaxpr/ppermute | solution.py:10
  706.9 9.9 collective-permute-start.1
  716.8 14.0 %collective-permute-done.1 = f32[1280,128]{0,1:T(8,128)S(1)} collective-permute-done((f32[1280,128]{0,1:T(8,128)}, f32[1280,128]{0,1:T(8,128)S(1)}, u32[]{:S(2)}, u32[]{:S(2)}) %collective-permute-start.1) | collective-permute-done | bytes 655392 | tf_op jit(solution)/shard_map/while/body/eval_jaxpr/ppermute | solution.py:10
  738.7 20.2 %collective-permute-done.1 = f32[1280,128]{0,1:T(8,128)S(1)} collective-permute-done((f32[1280,128]{0,1:T(8,128)}, f32[1280,128]{0,1:T(8,128)S(1)}, u32[]{:S(2)}, u32[]{:S(2)}) %collective-permute-start.1) | collective-permute-done | bytes 655392 | tf_op jit(solution)/shard_map/while/body/eval_jaxpr/ppermute | solution.py:10
  761.1 12.1 %collective-permute-start.1 = (f32[1280,128]{0,1:T(8,128)}, f32[1280,128]{0,1:T(8,128)S(1)}, u32[]{:S(2)}, u32[]{:S(2)}) collective-permute-start(f32[1280,128]{0,1:T(8,128)} %get-tuple-element.554), channel_id=1, source_target_pairs={{0,16},{16,32},{32,48},{48,64},{64,80},{80,96},{96,112},{1,17},{17... | collective-permute-start | bytes 1966088 | tf_op jit(solution)/shard_map/while/body/eval_jaxpr/ppermute | solution.py:10
  773.2 13.1 %collective-permute-done.1 = f32[1280,128]{0,1:T(8,128)S(1)} collective-permute-done((f32[1280,128]{0,1:T(8,128)}, f32[1280,128]{0,1:T(8,128)S(1)}, u32[]{:S(2)}, u32[]{:S(2)}) %collective-permute-start.1) | collective-permute-done | bytes 655392 | tf_op jit(solution)/shard_map/while/body/eval_jaxpr/ppermute | solution.py:10
  788.5 8.4 collective-permute-start.1
  796.9 20.5 %collective-permute-done.1 = f32[1280,128]{0,1:T(8,128)S(1)} collective-permute-done((f32[1280,128]{0,1:T(8,128)}, f32[1280,128]{0,1:T(8,128)S(1)}, u32[]{:S(2)}, u32[]{:S(2)}) %collective-permute-start.1) | collective-permute-done | bytes 655392 | tf_op jit(solution)/shard_map/while/body/eval_jaxpr/ppermute | solution.py:10
  824.8 15.6 %collective-permute-done.1 = f32[1280,128]{0,1:T(8,128)S(1)} collective-permute-done((f32[1280,128]{0,1:T(8,128)}, f32[1280,128]{0,1:T(8,128)S(1)}, u32[]{:S(2)}, u32[]{:S(2)}) %collective-permute-start.1) | collective-permute-done | bytes 655392 | tf_op jit(solution)/shard_map/while/body/eval_jaxpr/ppermute | solution.py:10
  843.2 9.7 collective-permute-start.1
  852.9 20.1 %collective-permute-done.1 = f32[1280,128]{0,1:T(8,128)S(1)} collective-permute-done((f32[1280,128]{0,1:T(8,128)}, f32[1280,128]{0,1:T(8,128)S(1)}, u32[]{:S(2)}, u32[]{:S(2)}) %collective-permute-start.1) | collective-permute-done | bytes 655392 | tf_op jit(solution)/shard_map/while/body/eval_jaxpr/ppermute | solution.py:10
  880.6 13.9 %collective-permute-done.1 = f32[1280,128]{0,1:T(8,128)S(1)} collective-permute-done((f32[1280,128]{0,1:T(8,128)}, f32[1280,128]{0,1:T(8,128)S(1)}, u32[]{:S(2)}, u32[]{:S(2)}) %collective-permute-start.1) | collective-permute-done | bytes 655392 | tf_op jit(solution)/shard_map/while/body/eval_jaxpr/ppermute | solution.py:10
  896.7 10.6 %collective-permute-start.1 = (f32[1280,128]{0,1:T(8,128)}, f32[1280,128]{0,1:T(8,128)S(1)}, u32[]{:S(2)}, u32[]{:S(2)}) collective-permute-start(f32[1280,128]{0,1:T(8,128)} %get-tuple-element.554), channel_id=1, source_target_pairs={{0,16},{16,32},{32,48},{48,64},{64,80},{80,96},{96,112},{1,17},{17... | collective-permute-start | bytes 1966088 | tf_op jit(solution)/shard_map/while/body/eval_jaxpr/ppermute | solution.py:10
  907.4 13.0 %collective-permute-done.1 = f32[1280,128]{0,1:T(8,128)S(1)} collective-permute-done((f32[1280,128]{0,1:T(8,128)}, f32[1280,128]{0,1:T(8,128)S(1)}, u32[]{:S(2)}, u32[]{:S(2)}) %collective-permute-start.1) | collective-permute-done | bytes 655392 | tf_op jit(solution)/shard_map/while/body/eval_jaxpr/ppermute | solution.py:10
  920.4 20.2 %fusion.6 = f32[1024,1024]{0,1:T(8,128)S(1)} fusion(f32[1280,1024]{0,1:T(8,128)} %get-tuple-element.409, f32[1,1,1024,1280]{3,2,1,0:T(8,128)} %param.11), kind=kOutput, calls=%fused_computation.9 | convolution fusion | flops 16106127360 | bytes 14680064 | tf_op jit(solution)/shard_map/dot_general | solution.py:67
  947.1 22.2 %gather_fusion = f32[512,2,1024]{2,1,0:T(2,128)} fusion(f32[2,512,1024]{2,0,1:T(2,128)} %copy.17, s32[1024]{0:T(1024)S(1)} %pad_clamp_fusion), kind=kCustom, calls=%fused_computation | custom fusion | bytes 8390656 | tf_op jit(solution)/shard_map/jit(_take)/gather | solution.py:72
  975.1 9.9 all-to-all-start
  990.8 53.0 %all-to-all-done = f32[8,2,64,1024]{3,1,2,0:T(2,128)} async-done(((f32[8,2,64,1024]{3,1,2,0:T(2,128)}), f32[8,2,64,1024]{3,1,2,0:T(2,128)}, u32[]{:S(2)}, u32[]{:S(2)}) %all-to-all-start) | async-done | bytes 4194336 | tf_op jit(solution)/shard_map/all_to_all | solution.py:20
  (169 shorter events, 225.6 us)
Async XLA Ops:
  19.7 3.2 collective-permute-start
  21.0 12.2 %collective-permute-start.1 = (f32[1280,128]{0,1:T(8,128)}, f32[1280,128]{0,1:T(8,128)S(1)}, u32[]{:S(2)}, u32[]{:S(2)}) collective-permute-start(f32[1280,128]{0,1:T(8,128)} %get-tuple-element.554), channel_id=1, source_target_pairs={{0,16},{16,32},{32,48},{48,64},{64,80},{80,96},{96,112},{1,17},{17... | collective-permute-start | bytes 1966088 | tf_op jit(solution)/shard_map/while/body/eval_jaxpr/ppermute | solution.py:10
  49.5 5.6 collective-permute-start
  50.8 19.7 %collective-permute-start.1 = (f32[1280,128]{0,1:T(8,128)}, f32[1280,128]{0,1:T(8,128)S(1)}, u32[]{:S(2)}, u32[]{:S(2)}) collective-permute-start(f32[1280,128]{0,1:T(8,128)} %get-tuple-element.554), channel_id=1, source_target_pairs={{0,16},{16,32},{32,48},{48,64},{64,80},{80,96},{96,112},{1,17},{17... | collective-permute-start | bytes 1966088 | tf_op jit(solution)/shard_map/while/body/eval_jaxpr/ppermute | solution.py:10
  86.8 5.7 collective-permute-start
  88.1 12.7 %collective-permute-start.1 = (f32[1280,128]{0,1:T(8,128)}, f32[1280,128]{0,1:T(8,128)S(1)}, u32[]{:S(2)}, u32[]{:S(2)}) collective-permute-start(f32[1280,128]{0,1:T(8,128)} %get-tuple-element.554), channel_id=1, source_target_pairs={{0,16},{16,32},{32,48},{48,64},{64,80},{80,96},{96,112},{1,17},{17... | collective-permute-start | bytes 1966088 | tf_op jit(solution)/shard_map/while/body/eval_jaxpr/ppermute | solution.py:10
  117.1 5.7 collective-permute-start
  118.4 19.7 %collective-permute-start.1 = (f32[1280,128]{0,1:T(8,128)}, f32[1280,128]{0,1:T(8,128)S(1)}, u32[]{:S(2)}, u32[]{:S(2)}) collective-permute-start(f32[1280,128]{0,1:T(8,128)} %get-tuple-element.554), channel_id=1, source_target_pairs={{0,16},{16,32},{32,48},{48,64},{64,80},{80,96},{96,112},{1,17},{17... | collective-permute-start | bytes 1966088 | tf_op jit(solution)/shard_map/while/body/eval_jaxpr/ppermute | solution.py:10
  154.4 5.7 collective-permute-start
  155.7 12.7 %collective-permute-start.1 = (f32[1280,128]{0,1:T(8,128)}, f32[1280,128]{0,1:T(8,128)S(1)}, u32[]{:S(2)}, u32[]{:S(2)}) collective-permute-start(f32[1280,128]{0,1:T(8,128)} %get-tuple-element.554), channel_id=1, source_target_pairs={{0,16},{16,32},{32,48},{48,64},{64,80},{80,96},{96,112},{1,17},{17... | collective-permute-start | bytes 1966088 | tf_op jit(solution)/shard_map/while/body/eval_jaxpr/ppermute | solution.py:10
  184.7 5.6 collective-permute-start
  186.0 19.7 %collective-permute-start.1 = (f32[1280,128]{0,1:T(8,128)}, f32[1280,128]{0,1:T(8,128)S(1)}, u32[]{:S(2)}, u32[]{:S(2)}) collective-permute-start(f32[1280,128]{0,1:T(8,128)} %get-tuple-element.554), channel_id=1, source_target_pairs={{0,16},{16,32},{32,48},{48,64},{64,80},{80,96},{96,112},{1,17},{17... | collective-permute-start | bytes 1966088 | tf_op jit(solution)/shard_map/while/body/eval_jaxpr/ppermute | solution.py:10
  221.9 5.7 collective-permute-start
  223.3 14.7 %collective-permute-start.1 = (f32[1280,128]{0,1:T(8,128)}, f32[1280,128]{0,1:T(8,128)S(1)}, u32[]{:S(2)}, u32[]{:S(2)}) collective-permute-start(f32[1280,128]{0,1:T(8,128)} %get-tuple-element.554), channel_id=1, source_target_pairs={{0,16},{16,32},{32,48},{48,64},{64,80},{80,96},{96,112},{1,17},{17... | collective-permute-start | bytes 1966088 | tf_op jit(solution)/shard_map/while/body/eval_jaxpr/ppermute | solution.py:10
  254.0 5.9 collective-permute-start
  255.3 14.7 %collective-permute-start.1 = (f32[1280,128]{0,1:T(8,128)}, f32[1280,128]{0,1:T(8,128)S(1)}, u32[]{:S(2)}, u32[]{:S(2)}) collective-permute-start(f32[1280,128]{0,1:T(8,128)} %get-tuple-element.554), channel_id=1, source_target_pairs={{0,16},{16,32},{32,48},{48,64},{64,80},{80,96},{96,112},{1,17},{17... | collective-permute-start | bytes 1966088 | tf_op jit(solution)/shard_map/while/body/eval_jaxpr/ppermute | solution.py:10
  270.9 20.8 %collective-permute-start = (f32[1280,128]{0,1:T(8,128)}, f32[1280,128]{0,1:T(8,128)S(1)}, u32[]{:S(2)}, u32[]{:S(2)}) collective-permute-start(f32[1280,128]{0,1:T(8,128)} %get-tuple-element.554), channel_id=1, source_target_pairs={{0,1},{1,2},{2,3},{3,4},{4,5},{5,6},{6,7},{7,8},{8,9},{9,10},{10,1... | collective-permute-start | bytes 1966088 | tf_op jit(solution)/shard_map/while/body/eval_jaxpr/ppermute | solution.py:10
  275.5 26.6 %collective-permute-start.1 = (f32[1280,128]{0,1:T(8,128)}, f32[1280,128]{0,1:T(8,128)S(1)}, u32[]{:S(2)}, u32[]{:S(2)}) collective-permute-start(f32[1280,128]{0,1:T(8,128)} %get-tuple-element.554), channel_id=1, source_target_pairs={{0,16},{16,32},{32,48},{48,64},{64,80},{80,96},{96,112},{1,17},{17... | collective-permute-start | bytes 1966088 | tf_op jit(solution)/shard_map/while/body/eval_jaxpr/ppermute | solution.py:10
  303.0 20.1 %collective-permute-start = (f32[1280,128]{0,1:T(8,128)}, f32[1280,128]{0,1:T(8,128)S(1)}, u32[]{:S(2)}, u32[]{:S(2)}) collective-permute-start(f32[1280,128]{0,1:T(8,128)} %get-tuple-element.554), channel_id=1, source_target_pairs={{0,1},{1,2},{2,3},{3,4},{4,5},{5,6},{6,7},{7,8},{8,9},{9,10},{10,1... | collective-permute-start | bytes 1966088 | tf_op jit(solution)/shard_map/while/body/eval_jaxpr/ppermute | solution.py:10
  304.3 39.1 %collective-permute-start.1 = (f32[1280,128]{0,1:T(8,128)}, f32[1280,128]{0,1:T(8,128)S(1)}, u32[]{:S(2)}, u32[]{:S(2)}) collective-permute-start(f32[1280,128]{0,1:T(8,128)} %get-tuple-element.554), channel_id=1, source_target_pairs={{0,16},{16,32},{32,48},{48,64},{64,80},{80,96},{96,112},{1,17},{17... | collective-permute-start | bytes 1966088 | tf_op jit(solution)/shard_map/while/body/eval_jaxpr/ppermute | solution.py:10
  344.3 6.3 collective-permute-start
  346.3 26.3 %collective-permute-start.1 = (f32[1280,128]{0,1:T(8,128)}, f32[1280,128]{0,1:T(8,128)S(1)}, u32[]{:S(2)}, u32[]{:S(2)}) collective-permute-start(f32[1280,128]{0,1:T(8,128)} %get-tuple-element.554), channel_id=1, source_target_pairs={{0,16},{16,32},{32,48},{48,64},{64,80},{80,96},{96,112},{1,17},{17... | collective-permute-start | bytes 1966088 | tf_op jit(solution)/shard_map/while/body/eval_jaxpr/ppermute | solution.py:10
  373.5 11.9 %collective-permute-start = (f32[1280,128]{0,1:T(8,128)}, f32[1280,128]{0,1:T(8,128)S(1)}, u32[]{:S(2)}, u32[]{:S(2)}) collective-permute-start(f32[1280,128]{0,1:T(8,128)} %get-tuple-element.554), channel_id=1, source_target_pairs={{0,1},{1,2},{2,3},{3,4},{4,5},{5,6},{6,7},{7,8},{8,9},{9,10},{10,1... | collective-permute-start | bytes 1966088 | tf_op jit(solution)/shard_map/while/body/eval_jaxpr/ppermute | solution.py:10
  375.1 31.4 %collective-permute-start.1 = (f32[1280,128]{0,1:T(8,128)}, f32[1280,128]{0,1:T(8,128)S(1)}, u32[]{:S(2)}, u32[]{:S(2)}) collective-permute-start(f32[1280,128]{0,1:T(8,128)} %get-tuple-element.554), channel_id=1, source_target_pairs={{0,16},{16,32},{32,48},{48,64},{64,80},{80,96},{96,112},{1,17},{17... | collective-permute-start | bytes 1966088 | tf_op jit(solution)/shard_map/while/body/eval_jaxpr/ppermute | solution.py:10
  407.4 8.5 collective-permute-start
  408.7 28.6 %collective-permute-start.1 = (f32[1280,128]{0,1:T(8,128)}, f32[1280,128]{0,1:T(8,128)S(1)}, u32[]{:S(2)}, u32[]{:S(2)}) collective-permute-start(f32[1280,128]{0,1:T(8,128)} %get-tuple-element.554), channel_id=1, source_target_pairs={{0,16},{16,32},{32,48},{48,64},{64,80},{80,96},{96,112},{1,17},{17... | collective-permute-start | bytes 1966088 | tf_op jit(solution)/shard_map/while/body/eval_jaxpr/ppermute | solution.py:10
  438.2 10.0 collective-permute-start
  439.5 29.5 %collective-permute-start.1 = (f32[1280,128]{0,1:T(8,128)}, f32[1280,128]{0,1:T(8,128)S(1)}, u32[]{:S(2)}, u32[]{:S(2)}) collective-permute-start(f32[1280,128]{0,1:T(8,128)} %get-tuple-element.554), channel_id=1, source_target_pairs={{0,16},{16,32},{32,48},{48,64},{64,80},{80,96},{96,112},{1,17},{17... | collective-permute-start | bytes 1966088 | tf_op jit(solution)/shard_map/while/body/eval_jaxpr/ppermute | solution.py:10
  469.9 5.7 collective-permute-start
  471.2 24.9 %collective-permute-start.1 = (f32[1280,128]{0,1:T(8,128)}, f32[1280,128]{0,1:T(8,128)S(1)}, u32[]{:S(2)}, u32[]{:S(2)}) collective-permute-start(f32[1280,128]{0,1:T(8,128)} %get-tuple-element.554), channel_id=1, source_target_pairs={{0,16},{16,32},{32,48},{48,64},{64,80},{80,96},{96,112},{1,17},{17... | collective-permute-start | bytes 1966088 | tf_op jit(solution)/shard_map/while/body/eval_jaxpr/ppermute | solution.py:10
  497.0 11.9 %collective-permute-start = (f32[1280,128]{0,1:T(8,128)}, f32[1280,128]{0,1:T(8,128)S(1)}, u32[]{:S(2)}, u32[]{:S(2)}) collective-permute-start(f32[1280,128]{0,1:T(8,128)} %get-tuple-element.554), channel_id=1, source_target_pairs={{0,1},{1,2},{2,3},{3,4},{4,5},{5,6},{6,7},{7,8},{8,9},{9,10},{10,1... | collective-permute-start | bytes 1966088 | tf_op jit(solution)/shard_map/while/body/eval_jaxpr/ppermute | solution.py:10
  498.4 29.7 %collective-permute-start.1 = (f32[1280,128]{0,1:T(8,128)}, f32[1280,128]{0,1:T(8,128)S(1)}, u32[]{:S(2)}, u32[]{:S(2)}) collective-permute-start(f32[1280,128]{0,1:T(8,128)} %get-tuple-element.554), channel_id=1, source_target_pairs={{0,16},{16,32},{32,48},{48,64},{64,80},{80,96},{96,112},{1,17},{17... | collective-permute-start | bytes 1966088 | tf_op jit(solution)/shard_map/while/body/eval_jaxpr/ppermute | solution.py:10
  528.9 5.7 collective-permute-start
  530.3 23.6 %collective-permute-start.1 = (f32[1280,128]{0,1:T(8,128)}, f32[1280,128]{0,1:T(8,128)S(1)}, u32[]{:S(2)}, u32[]{:S(2)}) collective-permute-start(f32[1280,128]{0,1:T(8,128)} %get-tuple-element.554), channel_id=1, source_target_pairs={{0,16},{16,32},{32,48},{48,64},{64,80},{80,96},{96,112},{1,17},{17... | collective-permute-start | bytes 1966088 | tf_op jit(solution)/shard_map/while/body/eval_jaxpr/ppermute | solution.py:10
  554.7 12.3 %collective-permute-start = (f32[1280,128]{0,1:T(8,128)}, f32[1280,128]{0,1:T(8,128)S(1)}, u32[]{:S(2)}, u32[]{:S(2)}) collective-permute-start(f32[1280,128]{0,1:T(8,128)} %get-tuple-element.554), channel_id=1, source_target_pairs={{0,1},{1,2},{2,3},{3,4},{4,5},{5,6},{6,7},{7,8},{8,9},{9,10},{10,1... | collective-permute-start | bytes 1966088 | tf_op jit(solution)/shard_map/while/body/eval_jaxpr/ppermute | solution.py:10
  556.0 31.3 %collective-permute-start.1 = (f32[1280,128]{0,1:T(8,128)}, f32[1280,128]{0,1:T(8,128)S(1)}, u32[]{:S(2)}, u32[]{:S(2)}) collective-permute-start(f32[1280,128]{0,1:T(8,128)} %get-tuple-element.554), channel_id=1, source_target_pairs={{0,16},{16,32},{32,48},{48,64},{64,80},{80,96},{96,112},{1,17},{17... | collective-permute-start | bytes 1966088 | tf_op jit(solution)/shard_map/while/body/eval_jaxpr/ppermute | solution.py:10
  588.2 5.7 collective-permute-start
  589.5 24.4 %collective-permute-start.1 = (f32[1280,128]{0,1:T(8,128)}, f32[1280,128]{0,1:T(8,128)S(1)}, u32[]{:S(2)}, u32[]{:S(2)}) collective-permute-start(f32[1280,128]{0,1:T(8,128)} %get-tuple-element.554), channel_id=1, source_target_pairs={{0,16},{16,32},{32,48},{48,64},{64,80},{80,96},{96,112},{1,17},{17... | collective-permute-start | bytes 1966088 | tf_op jit(solution)/shard_map/while/body/eval_jaxpr/ppermute | solution.py:10
  614.8 17.4 %collective-permute-start = (f32[1280,128]{0,1:T(8,128)}, f32[1280,128]{0,1:T(8,128)S(1)}, u32[]{:S(2)}, u32[]{:S(2)}) collective-permute-start(f32[1280,128]{0,1:T(8,128)} %get-tuple-element.554), channel_id=1, source_target_pairs={{0,1},{1,2},{2,3},{3,4},{4,5},{5,6},{6,7},{7,8},{8,9},{9,10},{10,1... | collective-permute-start | bytes 1966088 | tf_op jit(solution)/shard_map/while/body/eval_jaxpr/ppermute | solution.py:10
  616.2 33.7 %collective-permute-start.1 = (f32[1280,128]{0,1:T(8,128)}, f32[1280,128]{0,1:T(8,128)S(1)}, u32[]{:S(2)}, u32[]{:S(2)}) collective-permute-start(f32[1280,128]{0,1:T(8,128)} %get-tuple-element.554), channel_id=1, source_target_pairs={{0,16},{16,32},{32,48},{48,64},{64,80},{80,96},{96,112},{1,17},{17... | collective-permute-start | bytes 1966088 | tf_op jit(solution)/shard_map/while/body/eval_jaxpr/ppermute | solution.py:10
  650.7 8.5 collective-permute-start
  652.0 25.8 %collective-permute-start.1 = (f32[1280,128]{0,1:T(8,128)}, f32[1280,128]{0,1:T(8,128)S(1)}, u32[]{:S(2)}, u32[]{:S(2)}) collective-permute-start(f32[1280,128]{0,1:T(8,128)} %get-tuple-element.554), channel_id=1, source_target_pairs={{0,16},{16,32},{32,48},{48,64},{64,80},{80,96},{96,112},{1,17},{17... | collective-permute-start | bytes 1966088 | tf_op jit(solution)/shard_map/while/body/eval_jaxpr/ppermute | solution.py:10
  678.7 6.9 collective-permute-start
  680.0 24.6 %collective-permute-start.1 = (f32[1280,128]{0,1:T(8,128)}, f32[1280,128]{0,1:T(8,128)S(1)}, u32[]{:S(2)}, u32[]{:S(2)}) collective-permute-start(f32[1280,128]{0,1:T(8,128)} %get-tuple-element.554), channel_id=1, source_target_pairs={{0,16},{16,32},{32,48},{48,64},{64,80},{80,96},{96,112},{1,17},{17... | collective-permute-start | bytes 1966088 | tf_op jit(solution)/shard_map/while/body/eval_jaxpr/ppermute | solution.py:10
  705.6 11.3 %collective-permute-start = (f32[1280,128]{0,1:T(8,128)}, f32[1280,128]{0,1:T(8,128)S(1)}, u32[]{:S(2)}, u32[]{:S(2)}) collective-permute-start(f32[1280,128]{0,1:T(8,128)} %get-tuple-element.554), channel_id=1, source_target_pairs={{0,1},{1,2},{2,3},{3,4},{4,5},{5,6},{6,7},{7,8},{8,9},{9,10},{10,1... | collective-permute-start | bytes 1966088 | tf_op jit(solution)/shard_map/while/body/eval_jaxpr/ppermute | solution.py:10
  706.9 24.0 %collective-permute-start.1 = (f32[1280,128]{0,1:T(8,128)}, f32[1280,128]{0,1:T(8,128)S(1)}, u32[]{:S(2)}, u32[]{:S(2)}) collective-permute-start(f32[1280,128]{0,1:T(8,128)} %get-tuple-element.554), channel_id=1, source_target_pairs={{0,16},{16,32},{32,48},{48,64},{64,80},{80,96},{96,112},{1,17},{17... | collective-permute-start | bytes 1966088 | tf_op jit(solution)/shard_map/while/body/eval_jaxpr/ppermute | solution.py:10
  731.7 6.9 collective-permute-start
  733.1 25.8 %collective-permute-start.1 = (f32[1280,128]{0,1:T(8,128)}, f32[1280,128]{0,1:T(8,128)S(1)}, u32[]{:S(2)}, u32[]{:S(2)}) collective-permute-start(f32[1280,128]{0,1:T(8,128)} %get-tuple-element.554), channel_id=1, source_target_pairs={{0,16},{16,32},{32,48},{48,64},{64,80},{80,96},{96,112},{1,17},{17... | collective-permute-start | bytes 1966088 | tf_op jit(solution)/shard_map/while/body/eval_jaxpr/ppermute | solution.py:10
  759.8 13.4 %collective-permute-start = (f32[1280,128]{0,1:T(8,128)}, f32[1280,128]{0,1:T(8,128)S(1)}, u32[]{:S(2)}, u32[]{:S(2)}) collective-permute-start(f32[1280,128]{0,1:T(8,128)} %get-tuple-element.554), channel_id=1, source_target_pairs={{0,1},{1,2},{2,3},{3,4},{4,5},{5,6},{6,7},{7,8},{8,9},{9,10},{10,1... | collective-permute-start | bytes 1966088 | tf_op jit(solution)/shard_map/while/body/eval_jaxpr/ppermute | solution.py:10
  761.1 25.2 %collective-permute-start.1 = (f32[1280,128]{0,1:T(8,128)}, f32[1280,128]{0,1:T(8,128)S(1)}, u32[]{:S(2)}, u32[]{:S(2)}) collective-permute-start(f32[1280,128]{0,1:T(8,128)} %get-tuple-element.554), channel_id=1, source_target_pairs={{0,16},{16,32},{32,48},{48,64},{64,80},{80,96},{96,112},{1,17},{17... | collective-permute-start | bytes 1966088 | tf_op jit(solution)/shard_map/while/body/eval_jaxpr/ppermute | solution.py:10
  787.2 9.7 collective-permute-start
  788.5 28.9 %collective-permute-start.1 = (f32[1280,128]{0,1:T(8,128)}, f32[1280,128]{0,1:T(8,128)S(1)}, u32[]{:S(2)}, u32[]{:S(2)}) collective-permute-start(f32[1280,128]{0,1:T(8,128)} %get-tuple-element.554), channel_id=1, source_target_pairs={{0,16},{16,32},{32,48},{48,64},{64,80},{80,96},{96,112},{1,17},{17... | collective-permute-start | bytes 1966088 | tf_op jit(solution)/shard_map/while/body/eval_jaxpr/ppermute | solution.py:10
  818.3 6.5 collective-permute-start
  819.6 20.8 %collective-permute-start.1 = (f32[1280,128]{0,1:T(8,128)}, f32[1280,128]{0,1:T(8,128)S(1)}, u32[]{:S(2)}, u32[]{:S(2)}) collective-permute-start(f32[1280,128]{0,1:T(8,128)} %get-tuple-element.554), channel_id=1, source_target_pairs={{0,16},{16,32},{32,48},{48,64},{64,80},{80,96},{96,112},{1,17},{17... | collective-permute-start | bytes 1966088 | tf_op jit(solution)/shard_map/while/body/eval_jaxpr/ppermute | solution.py:10
  841.3 11.6 %collective-permute-start = (f32[1280,128]{0,1:T(8,128)}, f32[1280,128]{0,1:T(8,128)S(1)}, u32[]{:S(2)}, u32[]{:S(2)}) collective-permute-start(f32[1280,128]{0,1:T(8,128)} %get-tuple-element.554), channel_id=1, source_target_pairs={{0,1},{1,2},{2,3},{3,4},{4,5},{5,6},{6,7},{7,8},{8,9},{9,10},{10,1... | collective-permute-start | bytes 1966088 | tf_op jit(solution)/shard_map/while/body/eval_jaxpr/ppermute | solution.py:10
  843.2 29.7 %collective-permute-start.1 = (f32[1280,128]{0,1:T(8,128)}, f32[1280,128]{0,1:T(8,128)S(1)}, u32[]{:S(2)}, u32[]{:S(2)}) collective-permute-start(f32[1280,128]{0,1:T(8,128)} %get-tuple-element.554), channel_id=1, source_target_pairs={{0,16},{16,32},{32,48},{48,64},{64,80},{80,96},{96,112},{1,17},{17... | collective-permute-start | bytes 1966088 | tf_op jit(solution)/shard_map/while/body/eval_jaxpr/ppermute | solution.py:10
  873.9 6.7 collective-permute-start
  875.8 18.7 %collective-permute-start.1 = (f32[1280,128]{0,1:T(8,128)}, f32[1280,128]{0,1:T(8,128)S(1)}, u32[]{:S(2)}, u32[]{:S(2)}) collective-permute-start(f32[1280,128]{0,1:T(8,128)} %get-tuple-element.554), channel_id=1, source_target_pairs={{0,16},{16,32},{32,48},{48,64},{64,80},{80,96},{96,112},{1,17},{17... | collective-permute-start | bytes 1966088 | tf_op jit(solution)/shard_map/while/body/eval_jaxpr/ppermute | solution.py:10
  895.4 12.0 %collective-permute-start = (f32[1280,128]{0,1:T(8,128)}, f32[1280,128]{0,1:T(8,128)S(1)}, u32[]{:S(2)}, u32[]{:S(2)}) collective-permute-start(f32[1280,128]{0,1:T(8,128)} %get-tuple-element.554), channel_id=1, source_target_pairs={{0,1},{1,2},{2,3},{3,4},{4,5},{5,6},{6,7},{7,8},{8,9},{9,10},{10,1... | collective-permute-start | bytes 1966088 | tf_op jit(solution)/shard_map/while/body/eval_jaxpr/ppermute | solution.py:10
  896.7 23.6 %collective-permute-start.1 = (f32[1280,128]{0,1:T(8,128)}, f32[1280,128]{0,1:T(8,128)S(1)}, u32[]{:S(2)}, u32[]{:S(2)}) collective-permute-start(f32[1280,128]{0,1:T(8,128)} %get-tuple-element.554), channel_id=1, source_target_pairs={{0,16},{16,32},{32,48},{48,64},{64,80},{80,96},{96,112},{1,17},{17... | collective-permute-start | bytes 1966088 | tf_op jit(solution)/shard_map/while/body/eval_jaxpr/ppermute | solution.py:10
  940.5 5.3 copy-start
  975.1 68.7 %all-to-all-start = ((f32[8,2,64,1024]{3,1,2,0:T(2,128)}), f32[8,2,64,1024]{3,1,2,0:T(2,128)}, u32[]{:S(2)}, u32[]{:S(2)}) async-start(f32[8,2,64,1024]{3,1,2,0:T(2,128)} %select_bitcast_fusion), calls=%async_computation | async-start | bytes 8388608 | tf_op jit(solution)/shard_map/all_to_all | solution.py:20
where the time goes:
time: 1050 us
  waiting for transfers between devices  548 us (52%)
  starting transfers between devices  281 us (27%)
  matrix products  96 us (9%)
  local copies, waits for them, and re-layouts  95.3 us (9%)
  loops' own time  16.6 us (2%)
    ppermute x60, waiting for transfers between devices, passed_along(): lax.ppermute(value, axis, [(source, source + steps) for source in range(f...  495 us
    ppermute x60, starting transfers between devices, passed_along(): lax.ppermute(value, axis, [(source, source + steps) for source in range(f...  272 us
    dot_general x8, matrix products, work(): jnp.dot(operator, inflow, precision=lax.Precision.HIGHEST, preferred_elem...  75.9 us
    all_to_all x1, waiting for transfers between devices, sum_at_owner(): lax.all_to_all(parts, axis, split_axis=0, concat_axis=0, tiled=True)  53 us
    dynamic_update_slice x8, local copies, waits for them, and re-layouts, work(): return (result, lax.dynamic_update_slice_in_dim(stored, result, start, 1))  24.6 us
    another operation x40, local copies, waits for them, and re-layouts  23 us
    gather x1, local copies, waits for them, and re-layouts, local(): ordered = jnp.take(partial_value, owner_map[0], axis=1)  22.2 us
  transfers between devices with their start and end apart: 61, of which 32 were waited for; matrix products, arithmetic and copies ran while one was open for 1% of the time, Pallas kernels for 0%

commit v1 on v0

v1 whole, which is shorter than its diff:
```python
import functools

import jax
import jax.numpy as jnp
from jax import lax
from jax.experimental import pallas as pl
from jax.experimental.pallas import tpu as pltpu
from jax.sharding import PartitionSpec as P


UNIT = 32
SKEW = 2
VMEM = pltpu.MemorySpace.VMEM
SMEM = pltpu.MemorySpace.SMEM


def passed_along(value, axis, steps):
    count = lax.axis_size(axis)
    return lax.ppermute(value, axis, [(place, place + steps) for place in range(count - steps)])


def swapped(value, axis):
    count = lax.axis_size(axis)
    return lax.ppermute(value, axis, [(place, place ^ 1) for place in range(count)])


def pick_kernel(picks, sources, theirs, sems):
    count = theirs.shape[0]
    copies = [pltpu.make_async_copy(sources.at[picks[1, place]], theirs.at[place], sems.at[place]) for place in range(count)]
    for copy in copies:
        copy.start()
    for copy in copies:
        copy.wait()


def picked(picks, sources):
    count = picks.shape[1]
    return pl.pallas_call(
        pick_kernel,
        out_shape=pltpu.VMEM((count,) + sources.shape[1:], sources.dtype),
        in_specs=[pl.BlockSpec(memory_space=SMEM), pl.BlockSpec(memory_space=pl.ANY)],
        out_specs=pl.BlockSpec(memory_space=VMEM),
        scratch_shapes=[pltpu.SemaphoreType.DMA((count,))],
        compiler_params=pltpu.CompilerParams(vmem_limit_bytes=4 * 1024 * 1024),
        name="pick",
    )(picks, sources)


def split(x):
    high = x.astype(jnp.bfloat16)
    low = (x - high.astype(jnp.float32)).astype(jnp.bfloat16)
    return high, low


def fill(slot, green, slab_copies, pairs, inputs, rows, slabs, row_sems):
    trace = green.shape[0]
    chunk = rows.shape[1]
    steps = trace // chunk
    shots = slabs.shape[2]

    def row_copy(step):
        place = pl.ds(pl.multiple_of(step * chunk, chunk), chunk)
        return pltpu.make_async_copy(green.at[place], rows.at[step % 2], row_sems.at[step % 2])

    row_copy(0).start()
    for copy in slab_copies:
        copy.start()

    def one_chunk(step, nothing):
        @pl.when(step + 1 < steps)
        def _():
            row_copy(step + 1).start()

        row_copy(step).wait()
        high, low = split(rows[step % 2].T)
        pairs[slot, :, pl.ds(pl.multiple_of(step * chunk, chunk), chunk)] = high
        pairs[slot, :, pl.ds(pl.multiple_of(trace + step * chunk, chunk), chunk)] = low
        return nothing

    lax.fori_loop(0, steps, one_chunk, 0)
    for place, copy in enumerate(slab_copies):
        copy.wait()
        inputs[slot, pl.ds(place * shots, shots), :] = slabs[place].T


def own_kernel(core, picks, green, sources, pairs, inputs, store, rows, slabs, row_sems, slab_sems):
    del store
    copies = [pltpu.make_async_copy(sources.at[picks[0, place]], slabs.at[place], slab_sems.at[place]) for place in range(slabs.shape[0])]
    fill(core[0], green, copies, pairs, inputs, rows, slabs, row_sems)


def other_kernel(core, green, theirs, pairs_in, inputs_in, pairs, inputs, rows, slabs, row_sems, slab_sems):
    del pairs_in, inputs_in
    copies = [pltpu.make_async_copy(theirs.at[place], slabs.at[place], slab_sems.at[place]) for place in range(slabs.shape[0])]
    fill(1 - core[0], green, copies, pairs, inputs, rows, slabs, row_sems)


def fill_scratch(trace, count, shots):
    return [
        pltpu.VMEM((2, 128, trace), jnp.float32),
        pltpu.VMEM((count, trace, shots), jnp.float32),
        pltpu.SemaphoreType.DMA((2,)),
        pltpu.SemaphoreType.DMA((count,)),
    ]


def own_side(core, picks, green, sources):
    trace = green.shape[0]
    count = picks.shape[1]
    shots = sources.shape[2]
    columns = count * shots
    scalar = pl.BlockSpec(memory_space=SMEM)
    anywhere = pl.BlockSpec(memory_space=pl.ANY)
    inside = pl.BlockSpec(memory_space=VMEM)
    return pl.pallas_call(
        own_kernel,
        out_shape=(
            pltpu.VMEM((2, trace, 2 * trace), jnp.bfloat16),
            pltpu.VMEM((2, columns, trace), jnp.float32),
            pltpu.VMEM((2, columns, trace), jnp.float32),
        ),
        in_specs=[scalar, scalar, anywhere, anywhere],
        out_specs=(inside,) * 3,
        scratch_shapes=fill_scratch(trace, count, shots),
        compiler_params=pltpu.CompilerParams(vmem_limit_bytes=12 * 1024 * 1024),
        name="own",
    )(core, picks, green, sources)


def other_side(core, green, theirs, pairs, inputs):
    count, trace, shots = theirs.shape
    scalar = pl.BlockSpec(memory_space=SMEM)
    anywhere = pl.BlockSpec(memory_space=pl.ANY)
    inside = pl.BlockSpec(memory_space=VMEM)
    return pl.pallas_call(
        other_kernel,
        out_shape=(pltpu.VMEM(pairs.shape, pairs.dtype), pltpu.VMEM(inputs.shape, inputs.dtype)),
        in_specs=[scalar, anywhere, anywhere, inside, inside],
        out_specs=(inside,) * 2,
        input_output_aliases={3: 0, 4: 1},
        scratch_shapes=fill_scratch(trace, count, shots),
        compiler_params=pltpu.CompilerParams(vmem_limit_bytes=12 * 1024 * 1024),
        name="other",
    )(core, green, theirs, pairs, inputs)


def sweep_kernel(step, units, base, pairs, inputs, upper, lefter, stored, right, lower, store, above, both):
    del stored
    unit = step - base[0]
    size, trace = upper.shape
    block = 640

    @pl.when(jnp.logical_and(unit >= 0, unit < units))
    def _():
        spot = pl.ds(pl.multiple_of(jnp.clip(unit, 0, units - 1) * size, size), size)
        above[...] = upper[...]

        def one_row(row, nothing):
            high, low = split(inputs[row, spot, :] + 0.5 * (above[...] + lefter[row]))
            both[:size, :] = high
            both[size:, :] = low

            def one_block(number, nothing):
                start = pl.multiple_of(number * block, block)
                contract = (((1,), (0,)), ((), ()))
                most = lax.dot_general(both[...], pairs[row, :, pl.ds(start, block)], contract, preferred_element_type=jnp.float32)
                rest = lax.dot_general(both[:size, :], pairs[row, :, pl.ds(trace + start, block)], contract, preferred_element_type=jnp.float32)
                value = most[:size] + (most[size:] + rest)
                above[:, pl.ds(start, block)] = value
                right[row, :, pl.ds(start, block)] = value
                store[row, spot, pl.ds(start, block)] = value
                return nothing

            return lax.fori_loop(0, trace // block, one_block, nothing)

        lax.fori_loop(0, 2, one_row, 0)
        lower[...] = above[...]


def swept(step, units, base, pairs, inputs, upper, lefter, store):
    inside = pl.BlockSpec(memory_space=VMEM)
    return pl.pallas_call(
        functools.partial(sweep_kernel, step, units),
        out_shape=(
            pltpu.VMEM(lefter.shape, jnp.float32),
            pltpu.VMEM(upper.shape, jnp.float32),
            pltpu.VMEM(store.shape, jnp.float32),
        ),
        in_specs=[pl.BlockSpec(memory_space=SMEM)] + [inside] * 5,
        out_specs=(inside,) * 3,
        input_output_aliases={5: 2},
        scratch_shapes=[pltpu.VMEM(upper.shape, jnp.float32), pltpu.VMEM((2 * upper.shape[0], upper.shape[1]), jnp.bfloat16)],
        compiler_params=pltpu.CompilerParams(vmem_limit_bytes=8 * 1024 * 1024),
        name="sweep",
    )(base, pairs, inputs, upper, lefter, store)


def release_kernel(core, store, own, other, sems):
    copies = (
        pltpu.make_async_copy(store.at[1 - core[0]], other, sems.at[0]),
        pltpu.make_async_copy(store.at[core[0]], own, sems.at[1]),
    )
    for copy in copies:
        copy.start()
    for copy in copies:
        copy.wait()


def released(core, store):
    shape = jax.ShapeDtypeStruct(store.shape[1:], store.dtype)
    anywhere = pl.BlockSpec(memory_space=pl.ANY)
    return pl.pallas_call(
        release_kernel,
        out_shape=(shape, shape),
        in_specs=[pl.BlockSpec(memory_space=SMEM), pl.BlockSpec(memory_space=VMEM)],
        out_specs=(anywhere, anywhere),
        scratch_shapes=[pltpu.SemaphoreType.DMA((2,))],
        compiler_params=pltpu.CompilerParams(vmem_limit_bytes=8 * 1024 * 1024),
        name="release",
    )(core, store)


def order_kernel(*refs):
    gate, places, probe, high, low, whole, sem = refs[:3] + refs[-4:]

    @pl.when(gate[0] > 0)
    def _():
        copy = pltpu.make_async_copy(probe, whole, sem)
        copy.start()
        receivers = places.shape[0]
        slots = lax.broadcasted_iota(jnp.int32, (receivers, receivers), 1)
        chosen = jnp.where(slots == places[...], 1.0, 0.0).astype(jnp.bfloat16)
        copy.wait()
        for component in range(whole.shape[0] // receivers):
            span = pl.ds(component * receivers, receivers)
            first, second = split(whole[span, :])
            high[span, :] = jnp.dot(chosen, first, preferred_element_type=jnp.float32).astype(jnp.bfloat16)
            low[span, :] = jnp.dot(chosen, second, preferred_element_type=jnp.float32).astype(jnp.bfloat16)


def ordered(gate, places, probe, before=None):
    inside = pl.BlockSpec(memory_space=VMEM)
    shape = pltpu.VMEM(probe.shape, jnp.bfloat16)
    more = () if before is None else tuple(before)
    return pl.pallas_call(
        order_kernel,
        out_shape=(shape, shape),
        in_specs=[pl.BlockSpec(memory_space=SMEM), inside, pl.BlockSpec(memory_space=pl.ANY)] + [inside] * len(more),
        out_specs=(inside, inside),
        input_output_aliases={3 + number: number for number in range(len(more))},
        scratch_shapes=[pltpu.VMEM(probe.shape, jnp.float32), pltpu.SemaphoreType.DMA],
        compiler_params=pltpu.CompilerParams(vmem_limit_bytes=16 * 1024 * 1024),
        name="order",
    )(gate, places, probe, *more)


def gather_kernel(traces, high, low, *refs):
    straight, partial_value, turned, sem = refs[-4:]
    columns, _ = traces.shape
    block = 256
    copies = []
    for number in range(columns // block):
        span = pl.ds(number * block, block)
        turned[:, span] = traces[span, :].T
        copies.append(pltpu.make_async_copy(turned.at[:, span], straight.at[:, span], sem.at[number]))
        copies[-1].start()
        first, second = split(turned[:, span])
        half = high.shape[0] // 2

        def one_component(component, nothing, span=span, first=first, second=second):
            rows = pl.ds(pl.multiple_of(component * half, half), half)
            value = jnp.dot(high[rows, :], first, preferred_element_type=jnp.float32)
            value += jnp.dot(high[rows, :], second, preferred_element_type=jnp.float32)
            value += jnp.dot(low[rows, :], first, preferred_element_type=jnp.float32)
            partial_value[:, component, :, span] = value.reshape(partial_value.shape[0], partial_value.shape[2], block)
            return nothing

        for component in range(2):
            one_component(component, 0)
    for copy in copies:
        copy.wait()


def gathered(traces, high, low, owners):
    columns, trace = traces.shape
    inside = pl.BlockSpec(memory_space=VMEM)
    anywhere = pl.BlockSpec(memory_space=pl.ANY)
    return pl.pallas_call(
        gather_kernel,
        out_shape=(
            jax.ShapeDtypeStruct((trace, columns), jnp.float32),
            jax.ShapeDtypeStruct((owners, 2, high.shape[0] // (2 * owners), columns), jnp.float32),
        ),
        in_specs=[inside] * 3,
        out_specs=(anywhere, inside),
        scratch_shapes=[pltpu.VMEM((trace, columns), jnp.float32), pltpu.SemaphoreType.DMA((columns // 256,))],
        compiler_params=pltpu.CompilerParams(vmem_limit_bytes=24 * 1024 * 1024),
        name="gather",
    )(traces, high, low)


def local(sources, green, probe, batch_pick, owner_map):
    column = lax.axis_index("gx")
    row = lax.axis_index("gz")
    columns = lax.axis_size("gx")
    rows = lax.axis_size("gz")
    core = lax.bitwise_and(row, 1)
    chip_diag = lax.shift_right_logical(row, 1) + column
    operator = green[0, 0]
    trace = operator.shape[0]
    window = batch_pick.shape[0]
    half = window // 2
    shots = sources.shape[4]
    units = half * shots // UNIT
    steps = units + SKEW * (columns + rows // 2 - 2)
    receivers = owner_map.shape[1]

    other_operator = swapped(operator, "gz")
    on_diag = lax.dynamic_index_in_dim(batch_pick, row + column, 1, keepdims=False).reshape(2, half)
    picks = jnp.where(core == 0, on_diag, on_diag[::-1])
    theirs = swapped(picked(picks, sources[0, 0]), "gz")
    core_word = core.astype(jnp.int32).reshape(1)
    pairs, inputs, store = own_side(core_word, picks, operator, sources[0, 0])
    pairs, inputs = other_side(core_word, other_operator, theirs, pairs, inputs)

    places = owner_map.reshape(receivers, 1)
    late = (chip_diag < 2).astype(jnp.int32).reshape(1)
    high, low = ordered(1 - late, places, probe[0, 0])

    base = (SKEW * chip_diag).astype(jnp.int32).reshape(1)
    uppers = [jnp.zeros((UNIT, trace), jnp.float32)] * SKEW
    lefters = [jnp.zeros((2, UNIT, trace), jnp.float32)] * SKEW
    for step in range(steps):
        right, lower, store = swept(step, units, base, pairs, inputs, uppers[step], lefters[step], store)
        if step + SKEW < steps:
            lefters.append(passed_along(right, "gx", 1))
            uppers.append(passed_along(lower, "gz", 2))
        if step == steps - 4:
            high, low = ordered(late, places, probe[0, 0], (high, low))

    own_traces, other_traces = released(core_word, store)
    arrived = swapped(other_traces, "gz")
    own_straight, own_partial = gathered(own_traces, high, low, columns)
    own_sums = lax.all_to_all(own_partial, "gx", split_axis=0, concat_axis=0, tiled=True)
    far_straight, far_partial = gathered(arrived, high, low, columns)
    far_sums = lax.all_to_all(far_partial, "gx", split_axis=0, concat_axis=0, tiled=True)
    own_sum = own_sums.sum(axis=0)
    far_sum = far_sums.sum(axis=0)

    def in_order(own, far):
        return jnp.where(core == 0, jnp.concatenate([own, far], -1), jnp.concatenate([far, own], -1))

    return (in_order(own_straight, far_straight)[None, None], in_order(own_sum, far_sum)[None])


def solution(mesh):
    return jax.shard_map(
        local,
        mesh=mesh,
        in_specs=(
            P("gz", "gx", None, None, None),
            P("gz", "gx", None, None),
            P("gz", "gx", None, None),
            P(),
            P("gz", None),
        ),
        out_specs=(P("gz", "gx", None, None), P("gz", None, "gx", None)),
        check_vma=False,
    )
```

time: 1050 us -> 617 us (0.59)
  waiting for transfers between devices: 548 us -> 176 us
  matrix products: 96 us -> 0 us
  Pallas kernels: 0 us -> 80.7 us
  local copies, waits for them, and re-layouts: 95.3 us -> 48 us
  loops' own time: 16.6 us -> 0 us
    ppermute x60 -> x87, waiting for transfers between devices: 495 us -> 132 us  [the longest x84 132 us: passed_along(): lax.ppermute(value, axis, [(place, place + steps) for place in range(coun...]
    dot_general x9 -> x0, matrix products: 96 us -> none  [the longest x8 75.9 us: work(): jnp.dot(operator, inflow, precision=lax.Precision.HIGHEST, preferred_elem...]
    pallas_call x0 -> x52, Pallas kernels: none -> 80.7 us  [the longest x44 44.2 us: swept(): pl.pallas_call(functools.partial(sweep_kernel, step, units), out_shape=(p...]
    unnamed x4 -> x48, local copies, waits for them, and re-layouts: 1.47 us -> 47.5 us
    dynamic_update_slice x8 -> x0, local copies, waits for them, and re-layouts: 24.6 us -> none  [work(): return (result, lax.dynamic_update_slice_in_dim(stored, result, start, 1))]
    another operation x40 -> x0, local copies, waits for them, and re-layouts: 23 us -> none
    gather x1 -> x0, local copies, waits for them, and re-layouts: 22.2 us -> none  [local(): ordered = jnp.take(partial_value, owner_map[0], axis=1)]
    another operation x31 -> x0, loops' own time: 16.6 us -> none  [the longest x30 15.8 us: advance(): result, traces = lax.cond(active, work, skip, traces)]
  transfers between devices with their start and end apart: 61 -> 89, of which waited for: 32 -> 46; matrix products, arithmetic and copies ran while one was open for 1% -> 1% of each run, Pallas kernels for 0% -> 11%
where the time goes in v1:
time: 617 us; the launch traced here: 605 us
  starting transfers between devices  289 us (47%)
  waiting for transfers between devices  176 us (29%)
  Pallas kernels  80.7 us (13%)
  local copies, waits for them, and re-layouts  48 us (8%)
  other arithmetic  9.9 us (2%)
    ppermute x84, starting transfers between devices, passed_along(): lax.ppermute(value, axis, [(place, place + steps) for place in range(coun...  274 us
    ppermute x84, waiting for transfers between devices, passed_along(): lax.ppermute(value, axis, [(place, place + steps) for place in range(coun...  132 us
    unnamed x48, local copies, waits for them, and re-layouts  47.5 us
    pallas_call x44, Pallas kernels, swept(): pl.pallas_call(functools.partial(sweep_kernel, step, units), out_shape=(p...  44.2 us
    all_to_all x1, waiting for transfers between devices, local(): lax.all_to_all(far_partial, 'gx', split_axis=0, concat_axis=0, tiled=True)  23.7 us
    all_to_all x1, waiting for transfers between devices, local(): lax.all_to_all(own_partial, 'gx', split_axis=0, concat_axis=0, tiled=True)  20.6 us
  transfers between devices with their start and end apart: 89, of which 46 were waited for; matrix products, arithmetic and copies ran while one was open for 1% of the time, Pallas kernels for 11%

profile of v1, /device:TPU:0, one launch (start us, length us, event | category | flops | bytes accessed | tf_op | source)
XLA Modules:
  0.0 605.4 jit_solution(6927645746134579358)
XLA Ops:
  12.5 7.3 %own.1 = (bf16[2,1280,2560]{2,1,0:T(8,128)(2,1)S(1)}, f32[2,512,1280]{2,1,0:T(8,128)S(1)}, f32[2,512,1280]{2,1,0:T(8,128)S(1)}) custom-call(s32[1]{0:T(128)} %bitcast.core, s32[2,4]{1,0:T(2,128)S(1)} %broadcast_select_fusion.picks, f32[1280,1280]{1,0:T(8,128)S(1)} %bitcast.16, f32[8,1280,128]{2,1,0:T(8,128)S(1)} %bitcast.12), custom_call_target="tpu_custom_call" | custom-call | tf_op jit(solution)/shard_map/own/pallas_call | solution.py:115
  19.9 4.7 copy-done.2
  29.3 4.7 copy-done.3
  36.5 9.0 %other.1 = (bf16[2,1280,2560]{2,1,0:T(8,128)(2,1)S(1)}, f32[2,512,1280]{2,1,0:T(8,128)S(1)}) custom-call(s32[1]{0:T(128)} %bitcast.core, f32[1280,1280]{1,0:T(8,128)} %collective-permute-done.green, f32[4,1280,128]{2,1,0:T(8,128)S(1)} %collective-permute-done.1.theirs, ...), custom_call_target="tpu_custom_call", output_to_operand_aliasing={{0}: (3, {}), {1}: (4, {})} | custom-call | tf_op jit(solution)/shard_map/other/pallas_call | solution.py:135
  45.5 4.7 copy-done.4
  50.3 4.7 copy-done.5
  72.0 3.8 collective-permute-start.9
  75.8 5.3 collective-permute-done.3.lefter
  83.7 4.4 collective-permute-start.7
  97.6 4.6 collective-permute-start.13
  104.8 4.2 collective-permute-start.11
  119.6 4.5 collective-permute-start.17
  126.8 4.4 collective-permute-start.15
  141.9 4.4 collective-permute-start.21
  152.4 4.4 collective-permute-start.19
  173.5 4.4 collective-permute-start.23
  184.7 6.2 %collective-permute-start.29 = (f32[2,32,1280]{2,1,0:T(8,128)S(1)}, f32[2,32,1280]{2,1,0:T(8,128)S(1)}, u32[]{:S(2)}, u32[]{:S(2)}) collective-permute-start(f32[2,32,1280]{2,1,0:T(8,128)S(1)} %get-tuple-element.190), channel_id=1, source_target_pairs={{0,16},{16,32},{32,48},{48,64},{64,80},{80,96},{96,112},{1,17},{17... | collective-permute-start | bytes 983048 | tf_op jit(solution)/shard_map/ppermute | solution.py:19
  195.0 5.5 collective-permute-start.27
  207.2 5.3 collective-permute-start.33
  215.5 5.4 collective-permute-start.31
  226.3 8.3 %collective-permute-start.37 = (f32[2,32,1280]{2,1,0:T(8,128)S(1)}, f32[2,32,1280]{2,1,0:T(8,128)S(1)}, u32[]{:S(2)}, u32[]{:S(2)}) collective-permute-start(f32[2,32,1280]{2,1,0:T(8,128)S(1)} %get-tuple-element.202), channel_id=1, source_target_pairs={{0,16},{16,32},{32,48},{48,64},{64,80},{80,96},{96,112},{1,17},{17... | collective-permute-start | bytes 983048 | tf_op jit(solution)/shard_map/ppermute | solution.py:19
  234.6 6.8 %collective-permute-start.35 = (f32[2,32,1280]{2,1,0:T(8,128)S(1)}, f32[2,32,1280]{2,1,0:T(8,128)S(1)}, u32[]{:S(2)}, u32[]{:S(2)}) collective-permute-start(f32[2,32,1280]{2,1,0:T(8,128)S(1)} %get-tuple-element.200), channel_id=1, source_target_pairs={{0,16},{16,32},{32,48},{48,64},{64,80},{80,96},{96,112},{1,17},{17... | collective-permute-start | bytes 983048 | tf_op jit(solution)/shard_map/ppermute | solution.py:19
  241.4 4.4 collective-permute-start.36
  248.6 6.5 %collective-permute-start.41 = (f32[2,32,1280]{2,1,0:T(8,128)S(1)}, f32[2,32,1280]{2,1,0:T(8,128)S(1)}, u32[]{:S(2)}, u32[]{:S(2)}) collective-permute-start(f32[2,32,1280]{2,1,0:T(8,128)S(1)} %get-tuple-element.208), channel_id=1, source_target_pairs={{0,16},{16,32},{32,48},{48,64},{64,80},{80,96},{96,112},{1,17},{17... | collective-permute-start | bytes 983048 | tf_op jit(solution)/shard_map/ppermute | solution.py:19
  255.2 4.8 collective-permute-start.39
  260.0 7.0 %collective-permute-start.40 = (f32[32,1280]{1,0:T(8,128)S(1)}, f32[32,1280]{1,0:T(8,128)S(1)}, u32[]{:S(2)}, u32[]{:S(2)}) collective-permute-start(f32[32,1280]{1,0:T(8,128)S(1)} %get-tuple-element.207), channel_id=1, source_target_pairs={{0,2},{1,3},{2,4},{3,5},{4,6},{5,7},{6,8},{7,9},{8,10},{9,11},{10,... | collective-permute-start | bytes 491528 | tf_op jit(solution)/shard_map/ppermute | solution.py:19
  275.7 4.4 collective-permute-start.43
  280.1 6.6 %collective-permute-start.44 = (f32[32,1280]{1,0:T(8,128)S(1)}, f32[32,1280]{1,0:T(8,128)S(1)}, u32[]{:S(2)}, u32[]{:S(2)}) collective-permute-start(f32[32,1280]{1,0:T(8,128)S(1)} %get-tuple-element.213), channel_id=1, source_target_pairs={{0,2},{1,3},{2,4},{3,5},{4,6},{5,7},{6,8},{7,9},{8,10},{9,11},{10,... | collective-permute-start | bytes 491528 | tf_op jit(solution)/shard_map/ppermute | solution.py:19
  286.7 4.5 collective-permute-start.42
  291.3 6.2 %collective-permute-start.49 = (f32[2,32,1280]{2,1,0:T(8,128)S(1)}, f32[2,32,1280]{2,1,0:T(8,128)S(1)}, u32[]{:S(2)}, u32[]{:S(2)}) collective-permute-start(f32[2,32,1280]{2,1,0:T(8,128)S(1)} %get-tuple-element.220), channel_id=1, source_target_pairs={{0,16},{16,32},{32,48},{48,64},{64,80},{80,96},{96,112},{1,17},{17... | collective-permute-start | bytes 983048 | tf_op jit(solution)/shard_map/ppermute | solution.py:19
  297.5 5.3 collective-permute-start.47
  304.4 4.0 collective-permute-start.46
  308.4 3.8 collective-permute-done.49.lefter
  312.2 4.5 collective-permute-start.53
  316.8 6.1 %collective-permute-done.47.lefter = f32[2,32,1280]{2,1,0:T(8,128)S(1)} collective-permute-done((f32[2,32,1280]{2,1,0:T(8,128)S(1)}, f32[2,32,1280]{2,1,0:T(8,128)S(1)}, u32[]{:S(2)}, u32[]{:S(2)}) %collective-permute-start.47) | collective-permute-done | bytes 327712 | tf_op jit(solution)/shard_map/ppermute | solution.py:19
  322.9 4.4 collective-permute-start.51
  331.4 6.4 %collective-permute-start.57 = (f32[2,32,1280]{2,1,0:T(8,128)S(1)}, f32[2,32,1280]{2,1,0:T(8,128)S(1)}, u32[]{:S(2)}, u32[]{:S(2)}) collective-permute-start(f32[2,32,1280]{2,1,0:T(8,128)S(1)} %get-tuple-element.232), channel_id=1, source_target_pairs={{0,16},{16,32},{32,48},{48,64},{64,80},{80,96},{96,112},{1,17},{17... | collective-permute-start | bytes 983048 | tf_op jit(solution)/shard_map/ppermute | solution.py:19
  337.8 6.1 %collective-permute-done.51.lefter = f32[2,32,1280]{2,1,0:T(8,128)S(1)} collective-permute-done((f32[2,32,1280]{2,1,0:T(8,128)S(1)}, f32[2,32,1280]{2,1,0:T(8,128)S(1)}, u32[]{:S(2)}, u32[]{:S(2)}) %collective-permute-start.51) | collective-permute-done | bytes 327712 | tf_op jit(solution)/shard_map/ppermute | solution.py:19
  343.9 4.4 collective-permute-start.55
  352.5 5.4 collective-permute-done.57.lefter
  357.9 4.5 collective-permute-start.61
  365.0 4.4 collective-permute-start.59
  373.5 5.5 collective-permute-done.61.lefter
  379.1 4.4 collective-permute-start.65
  386.2 4.4 collective-permute-start.63
  394.8 5.4 collective-permute-done.65.lefter
  400.1 4.4 collective-permute-start.69
  404.5 7.7 %collective-permute-done.63.lefter = f32[2,32,1280]{2,1,0:T(8,128)S(1)} collective-permute-done((f32[2,32,1280]{2,1,0:T(8,128)S(1)}, f32[2,32,1280]{2,1,0:T(8,128)S(1)}, u32[]{:S(2)}, u32[]{:S(2)}) %collective-permute-start.63) | collective-permute-done | bytes 327712 | tf_op jit(solution)/shard_map/ppermute | solution.py:19
  412.3 6.3 %collective-permute-start.67 = (f32[2,32,1280]{2,1,0:T(8,128)S(1)}, f32[2,32,1280]{2,1,0:T(8,128)S(1)}, u32[]{:S(2)}, u32[]{:S(2)}) collective-permute-start(f32[2,32,1280]{2,1,0:T(8,128)S(1)} %get-tuple-element.248), channel_id=1, source_target_pairs={{0,16},{16,32},{32,48},{48,64},{64,80},{80,96},{96,112},{1,17},{17... | collective-permute-start | bytes 983048 | tf_op jit(solution)/shard_map/ppermute | solution.py:19
  425.8 9.4 %collective-permute-done.67.lefter = f32[2,32,1280]{2,1,0:T(8,128)S(1)} collective-permute-done((f32[2,32,1280]{2,1,0:T(8,128)S(1)}, f32[2,32,1280]{2,1,0:T(8,128)S(1)}, u32[]{:S(2)}, u32[]{:S(2)}) %collective-permute-start.67) | collective-permute-done | bytes 327712 | tf_op jit(solution)/shard_map/ppermute | solution.py:19
  435.2 4.4 collective-permute-start.71
  446.7 9.6 %collective-permute-done.71.lefter = f32[2,32,1280]{2,1,0:T(8,128)S(1)} collective-permute-done((f32[2,32,1280]{2,1,0:T(8,128)S(1)}, f32[2,32,1280]{2,1,0:T(8,128)S(1)}, u32[]{:S(2)}, u32[]{:S(2)}) %collective-permute-start.71) | collective-permute-done | bytes 327712 | tf_op jit(solution)/shard_map/ppermute | solution.py:19
  456.3 4.4 collective-permute-start.75
  468.2 9.1 %collective-permute-done.75.lefter = f32[2,32,1280]{2,1,0:T(8,128)S(1)} collective-permute-done((f32[2,32,1280]{2,1,0:T(8,128)S(1)}, f32[2,32,1280]{2,1,0:T(8,128)S(1)}, u32[]{:S(2)}, u32[]{:S(2)}) %collective-permute-start.75) | collective-permute-done | bytes 327712 | tf_op jit(solution)/shard_map/ppermute | solution.py:19
  477.4 4.4 collective-permute-start.79
  487.8 4.5 collective-permute-start.85
  494.9 4.4 collective-permute-start.83
  515.4 5.2 gather.2
  525.0 10.1 %all-to-all-start = ((f32[8,2,64,512]{3,2,1,0:T(8,128)}), f32[8,2,64,512]{3,2,1,0:T(8,128)}, u32[]{:S(2)}, u32[]{:S(2)}) async-start(f32[8,2,64,512]{3,2,1,0:T(8,128)} %copy-done.22), calls=%async_computation | async-start | bytes 4194304 | tf_op jit(solution)/shard_map/all_to_all | solution.py:344
  536.8 6.9 %gather.3 = (f32[1280,512]{1,0:T(8,128)S(1)}, f32[8,2,64,512]{3,2,1,0:T(8,128)S(1)}) custom-call(f32[512,1280]{1,0:T(8,128)} %collective-permute-done.86.traces, bf16[1024,1280]{1,0:T(8,128)(2,1)S(1)} %get-tuple-element.281.high, bf16[1024,1280]{1,0:T(8,128)(2,1)S(1)} %copy-done.11), custom_call_target="tpu_custom_call" | custom-call | tf_op jit(solution)/shard_map/gather/pallas_call | solution.py:288
  546.7 20.6 %all-to-all-done = f32[8,2,64,512]{3,2,1,0:T(8,128)} async-done(((f32[8,2,64,512]{3,2,1,0:T(8,128)}), f32[8,2,64,512]{3,2,1,0:T(8,128)}, u32[]{:S(2)}, u32[]{:S(2)}) %all-to-all-start) | async-done | bytes 2097184 | tf_op jit(solution)/shard_map/all_to_all | solution.py:344
  567.3 4.3 all-to-all-start.1
  573.5 5.4 maximum_select_fusion
  578.9 23.7 %all-to-all-done.1 = f32[8,2,64,512]{3,2,1,0:T(8,128)} async-done(((f32[8,2,64,512]{3,2,1,0:T(8,128)}), f32[8,2,64,512]{3,2,1,0:T(8,128)}, u32[]{:S(2)}, u32[]{:S(2)}) %all-to-all-start.1) | async-done | bytes 2097184 | tf_op jit(solution)/shard_map/all_to_all | solution.py:346
  (225 shorter events, 218.0 us)
Async XLA Ops:
  0.6 28.7 %collective-permute-start = (f32[1280,1280]{1,0:T(8,128)}, f32[1280,1280]{1,0:T(8,128)}, u32[]{:S(2)}, u32[]{:S(2)}) collective-permute-start(f32[1280,1280]{1,0:T(8,128)} %bitcast.15), channel_id=1, source_target_pairs={{0,1},{1,0},{2,3},{3,2},{4,5},{5,4},{6,7},{7,6},{8,9},{9,8},{10,11... | collective-permute-start | bytes 19660808 | tf_op jit(solution)/shard_map/ppermute | solution.py:24
  7.1 22.2 %collective-permute-start.1 = (f32[4,1280,128]{2,1,0:T(8,128)}, f32[4,1280,128]{2,1,0:T(8,128)S(1)}, u32[]{:S(2)}, u32[]{:S(2)}) collective-permute-start(f32[4,1280,128]{2,1,0:T(8,128)} %pick.1), channel_id=1, source_target_pairs={{0,1},{1,0},{2,3},{3,2},{4,5},{5,4},{6,7},{7,6},{8,9},{9,8},{10,11... | collective-permute-start | bytes 7864328 | tf_op jit(solution)/shard_map/ppermute | solution.py:24
  57.6 11.7 %collective-permute-start.5 = (f32[2,32,1280]{2,1,0:T(8,128)S(1)}, f32[2,32,1280]{2,1,0:T(8,128)S(1)}, u32[]{:S(2)}, u32[]{:S(2)}) collective-permute-start(f32[2,32,1280]{2,1,0:T(8,128)S(1)} %get-tuple-element.154), channel_id=1, source_target_pairs={{0,16},{16,32},{32,48},{48,64},{64,80},{80,96},{96,112},{1,17},{17... | collective-permute-start | bytes 983048 | tf_op jit(solution)/shard_map/ppermute | solution.py:19
  61.6 19.5 %collective-permute-start.3 = (f32[2,32,1280]{2,1,0:T(8,128)S(1)}, f32[2,32,1280]{2,1,0:T(8,128)S(1)}, u32[]{:S(2)}, u32[]{:S(2)}) collective-permute-start(f32[2,32,1280]{2,1,0:T(8,128)S(1)} %get-tuple-element.152), channel_id=1, source_target_pairs={{0,16},{16,32},{32,48},{48,64},{64,80},{80,96},{96,112},{1,17},{17... | collective-permute-start | bytes 983048 | tf_op jit(solution)/shard_map/ppermute | solution.py:19
  65.4 10.4 %collective-permute-start.2 = (f32[32,1280]{1,0:T(8,128)S(1)}, f32[32,1280]{1,0:T(8,128)S(1)}, u32[]{:S(2)}, u32[]{:S(2)}) collective-permute-start(f32[32,1280]{1,0:T(8,128)S(1)} %get-tuple-element.151), channel_id=1, source_target_pairs={{0,2},{1,3},{2,4},{3,5},{4,6},{5,7},{6,8},{7,9},{8,10},{9,11},{10,... | collective-permute-start | bytes 491528 | tf_op jit(solution)/shard_map/ppermute | solution.py:19
  72.0 23.0 %collective-permute-start.9 = (f32[2,32,1280]{2,1,0:T(8,128)S(1)}, f32[2,32,1280]{2,1,0:T(8,128)S(1)}, u32[]{:S(2)}, u32[]{:S(2)}) collective-permute-start(f32[2,32,1280]{2,1,0:T(8,128)S(1)} %get-tuple-element.160), channel_id=1, source_target_pairs={{0,16},{16,32},{32,48},{48,64},{64,80},{80,96},{96,112},{1,17},{17... | collective-permute-start | bytes 983048 | tf_op jit(solution)/shard_map/ppermute | solution.py:19
  83.7 18.5 %collective-permute-start.7 = (f32[2,32,1280]{2,1,0:T(8,128)S(1)}, f32[2,32,1280]{2,1,0:T(8,128)S(1)}, u32[]{:S(2)}, u32[]{:S(2)}) collective-permute-start(f32[2,32,1280]{2,1,0:T(8,128)S(1)} %get-tuple-element.158), channel_id=1, source_target_pairs={{0,16},{16,32},{32,48},{48,64},{64,80},{80,96},{96,112},{1,17},{17... | collective-permute-start | bytes 983048 | tf_op jit(solution)/shard_map/ppermute | solution.py:19
  89.4 12.7 %collective-permute-start.6 = (f32[32,1280]{1,0:T(8,128)S(1)}, f32[32,1280]{1,0:T(8,128)S(1)}, u32[]{:S(2)}, u32[]{:S(2)}) collective-permute-start(f32[32,1280]{1,0:T(8,128)S(1)} %get-tuple-element.157), channel_id=1, source_target_pairs={{0,2},{1,3},{2,4},{3,5},{4,6},{5,7},{6,8},{7,9},{8,10},{9,11},{10,... | collective-permute-start | bytes 491528 | tf_op jit(solution)/shard_map/ppermute | solution.py:19
  97.6 19.4 %collective-permute-start.13 = (f32[2,32,1280]{2,1,0:T(8,128)S(1)}, f32[2,32,1280]{2,1,0:T(8,128)S(1)}, u32[]{:S(2)}, u32[]{:S(2)}) collective-permute-start(f32[2,32,1280]{2,1,0:T(8,128)S(1)} %get-tuple-element.166), channel_id=1, source_target_pairs={{0,16},{16,32},{32,48},{48,64},{64,80},{80,96},{96,112},{1,17},{17... | collective-permute-start | bytes 983048 | tf_op jit(solution)/shard_map/ppermute | solution.py:19
  104.8 19.4 %collective-permute-start.11 = (f32[2,32,1280]{2,1,0:T(8,128)S(1)}, f32[2,32,1280]{2,1,0:T(8,128)S(1)}, u32[]{:S(2)}, u32[]{:S(2)}) collective-permute-start(f32[2,32,1280]{2,1,0:T(8,128)S(1)} %get-tuple-element.164), channel_id=1, source_target_pairs={{0,16},{16,32},{32,48},{48,64},{64,80},{80,96},{96,112},{1,17},{17... | collective-permute-start | bytes 983048 | tf_op jit(solution)/shard_map/ppermute | solution.py:19
  110.3 13.9 %collective-permute-start.10 = (f32[32,1280]{1,0:T(8,128)S(1)}, f32[32,1280]{1,0:T(8,128)S(1)}, u32[]{:S(2)}, u32[]{:S(2)}) collective-permute-start(f32[32,1280]{1,0:T(8,128)S(1)} %get-tuple-element.163), channel_id=1, source_target_pairs={{0,2},{1,3},{2,4},{3,5},{4,6},{5,7},{6,8},{7,9},{8,10},{9,11},{10,... | collective-permute-start | bytes 491528 | tf_op jit(solution)/shard_map/ppermute | solution.py:19
  119.6 19.6 %collective-permute-start.17 = (f32[2,32,1280]{2,1,0:T(8,128)S(1)}, f32[2,32,1280]{2,1,0:T(8,128)S(1)}, u32[]{:S(2)}, u32[]{:S(2)}) collective-permute-start(f32[2,32,1280]{2,1,0:T(8,128)S(1)} %get-tuple-element.172), channel_id=1, source_target_pairs={{0,16},{16,32},{32,48},{48,64},{64,80},{80,96},{96,112},{1,17},{17... | collective-permute-start | bytes 983048 | tf_op jit(solution)/shard_map/ppermute | solution.py:19
  126.8 23.0 %collective-permute-start.15 = (f32[2,32,1280]{2,1,0:T(8,128)S(1)}, f32[2,32,1280]{2,1,0:T(8,128)S(1)}, u32[]{:S(2)}, u32[]{:S(2)}) collective-permute-start(f32[2,32,1280]{2,1,0:T(8,128)S(1)} %get-tuple-element.170), channel_id=1, source_target_pairs={{0,16},{16,32},{32,48},{48,64},{64,80},{80,96},{96,112},{1,17},{17... | collective-permute-start | bytes 983048 | tf_op jit(solution)/shard_map/ppermute | solution.py:19
  132.5 13.8 %collective-permute-start.14 = (f32[32,1280]{1,0:T(8,128)S(1)}, f32[32,1280]{1,0:T(8,128)S(1)}, u32[]{:S(2)}, u32[]{:S(2)}) collective-permute-start(f32[32,1280]{1,0:T(8,128)S(1)} %get-tuple-element.169), channel_id=1, source_target_pairs={{0,2},{1,3},{2,4},{3,5},{4,6},{5,7},{6,8},{7,9},{8,10},{9,11},{10,... | collective-permute-start | bytes 491528 | tf_op jit(solution)/shard_map/ppermute | solution.py:19
  141.9 19.1 %collective-permute-start.21 = (f32[2,32,1280]{2,1,0:T(8,128)S(1)}, f32[2,32,1280]{2,1,0:T(8,128)S(1)}, u32[]{:S(2)}, u32[]{:S(2)}) collective-permute-start(f32[2,32,1280]{2,1,0:T(8,128)S(1)} %get-tuple-element.178), channel_id=1, source_target_pairs={{0,16},{16,32},{32,48},{48,64},{64,80},{80,96},{96,112},{1,17},{17... | collective-permute-start | bytes 983048 | tf_op jit(solution)/shard_map/ppermute | solution.py:19
  152.4 18.4 %collective-permute-start.19 = (f32[2,32,1280]{2,1,0:T(8,128)S(1)}, f32[2,32,1280]{2,1,0:T(8,128)S(1)}, u32[]{:S(2)}, u32[]{:S(2)}) collective-permute-start(f32[2,32,1280]{2,1,0:T(8,128)S(1)} %get-tuple-element.176), channel_id=1, source_target_pairs={{0,16},{16,32},{32,48},{48,64},{64,80},{80,96},{96,112},{1,17},{17... | collective-permute-start | bytes 983048 | tf_op jit(solution)/shard_map/ppermute | solution.py:19
  158.1 9.2 %collective-permute-start.18 = (f32[32,1280]{1,0:T(8,128)S(1)}, f32[32,1280]{1,0:T(8,128)S(1)}, u32[]{:S(2)}, u32[]{:S(2)}) collective-permute-start(f32[32,1280]{1,0:T(8,128)S(1)} %get-tuple-element.175), channel_id=1, source_target_pairs={{0,2},{1,3},{2,4},{3,5},{4,6},{5,7},{6,8},{7,9},{8,10},{9,11},{10,... | collective-permute-start | bytes 491528 | tf_op jit(solution)/shard_map/ppermute | solution.py:19
  163.6 18.4 %collective-permute-start.25 = (f32[2,32,1280]{2,1,0:T(8,128)S(1)}, f32[2,32,1280]{2,1,0:T(8,128)S(1)}, u32[]{:S(2)}, u32[]{:S(2)}) collective-permute-start(f32[2,32,1280]{2,1,0:T(8,128)S(1)} %get-tuple-element.184), channel_id=1, source_target_pairs={{0,16},{16,32},{32,48},{48,64},{64,80},{80,96},{96,112},{1,17},{17... | collective-permute-start | bytes 983048 | tf_op jit(solution)/shard_map/ppermute | solution.py:19
  173.5 18.4 %collective-permute-start.23 = (f32[2,32,1280]{2,1,0:T(8,128)S(1)}, f32[2,32,1280]{2,1,0:T(8,128)S(1)}, u32[]{:S(2)}, u32[]{:S(2)}) collective-permute-start(f32[2,32,1280]{2,1,0:T(8,128)S(1)} %get-tuple-element.182), channel_id=1, source_target_pairs={{0,16},{16,32},{32,48},{48,64},{64,80},{80,96},{96,112},{1,17},{17... | collective-permute-start | bytes 983048 | tf_op jit(solution)/shard_map/ppermute | solution.py:19
  179.2 11.7 %collective-permute-start.22 = (f32[32,1280]{1,0:T(8,128)S(1)}, f32[32,1280]{1,0:T(8,128)S(1)}, u32[]{:S(2)}, u32[]{:S(2)}) collective-permute-start(f32[32,1280]{1,0:T(8,128)S(1)} %get-tuple-element.181), channel_id=1, source_target_pairs={{0,2},{1,3},{2,4},{3,5},{4,6},{5,7},{6,8},{7,9},{8,10},{9,11},{10,... | collective-permute-start | bytes 491528 | tf_op jit(solution)/shard_map/ppermute | solution.py:19
  184.7 19.9 %collective-permute-start.29 = (f32[2,32,1280]{2,1,0:T(8,128)S(1)}, f32[2,32,1280]{2,1,0:T(8,128)S(1)}, u32[]{:S(2)}, u32[]{:S(2)}) collective-permute-start(f32[2,32,1280]{2,1,0:T(8,128)S(1)} %get-tuple-element.190), channel_id=1, source_target_pairs={{0,16},{16,32},{32,48},{48,64},{64,80},{80,96},{96,112},{1,17},{17... | collective-permute-start | bytes 983048 | tf_op jit(solution)/shard_map/ppermute | solution.py:19
  195.0 17.9 %collective-permute-start.27 = (f32[2,32,1280]{2,1,0:T(8,128)S(1)}, f32[2,32,1280]{2,1,0:T(8,128)S(1)}, u32[]{:S(2)}, u32[]{:S(2)}) collective-permute-start(f32[2,32,1280]{2,1,0:T(8,128)S(1)} %get-tuple-element.188), channel_id=1, source_target_pairs={{0,16},{16,32},{32,48},{48,64},{64,80},{80,96},{96,112},{1,17},{17... | collective-permute-start | bytes 983048 | tf_op jit(solution)/shard_map/ppermute | solution.py:19
  201.8 10.8 %collective-permute-start.26 = (f32[32,1280]{1,0:T(8,128)S(1)}, f32[32,1280]{1,0:T(8,128)S(1)}, u32[]{:S(2)}, u32[]{:S(2)}) collective-permute-start(f32[32,1280]{1,0:T(8,128)S(1)} %get-tuple-element.187), channel_id=1, source_target_pairs={{0,2},{1,3},{2,4},{3,5},{4,6},{5,7},{6,8},{7,9},{8,10},{9,11},{10,... | collective-permute-start | bytes 491528 | tf_op jit(solution)/shard_map/ppermute | solution.py:19
  207.2 19.1 %collective-permute-start.33 = (f32[2,32,1280]{2,1,0:T(8,128)S(1)}, f32[2,32,1280]{2,1,0:T(8,128)S(1)}, u32[]{:S(2)}, u32[]{:S(2)}) collective-permute-start(f32[2,32,1280]{2,1,0:T(8,128)S(1)} %get-tuple-element.196), channel_id=1, source_target_pairs={{0,16},{16,32},{32,48},{48,64},{64,80},{80,96},{96,112},{1,17},{17... | collective-permute-start | bytes 983048 | tf_op jit(solution)/shard_map/ppermute | solution.py:19
  215.5 19.1 %collective-permute-start.31 = (f32[2,32,1280]{2,1,0:T(8,128)S(1)}, f32[2,32,1280]{2,1,0:T(8,128)S(1)}, u32[]{:S(2)}, u32[]{:S(2)}) collective-permute-start(f32[2,32,1280]{2,1,0:T(8,128)S(1)} %get-tuple-element.194), channel_id=1, source_target_pairs={{0,16},{16,32},{32,48},{48,64},{64,80},{80,96},{96,112},{1,17},{17... | collective-permute-start | bytes 983048 | tf_op jit(solution)/shard_map/ppermute | solution.py:19
  223.5 11.1 %collective-permute-start.30 = (f32[32,1280]{1,0:T(8,128)S(1)}, f32[32,1280]{1,0:T(8,128)S(1)}, u32[]{:S(2)}, u32[]{:S(2)}) collective-permute-start(f32[32,1280]{1,0:T(8,128)S(1)} %get-tuple-element.193), channel_id=1, source_target_pairs={{0,2},{1,3},{2,4},{3,5},{4,6},{5,7},{6,8},{7,9},{8,10},{9,11},{10,... | collective-permute-start | bytes 491528 | tf_op jit(solution)/shard_map/ppermute | solution.py:19
  226.3 22.4 %collective-permute-start.37 = (f32[2,32,1280]{2,1,0:T(8,128)S(1)}, f32[2,32,1280]{2,1,0:T(8,128)S(1)}, u32[]{:S(2)}, u32[]{:S(2)}) collective-permute-start(f32[2,32,1280]{2,1,0:T(8,128)S(1)} %get-tuple-element.202), channel_id=1, source_target_pairs={{0,16},{16,32},{32,48},{48,64},{64,80},{80,96},{96,112},{1,17},{17... | collective-permute-start | bytes 983048 | tf_op jit(solution)/shard_map/ppermute | solution.py:19
  234.6 20.5 %collective-permute-start.35 = (f32[2,32,1280]{2,1,0:T(8,128)S(1)}, f32[2,32,1280]{2,1,0:T(8,128)S(1)}, u32[]{:S(2)}, u32[]{:S(2)}) collective-permute-start(f32[2,32,1280]{2,1,0:T(8,128)S(1)} %get-tuple-element.200), channel_id=1, source_target_pairs={{0,16},{16,32},{32,48},{48,64},{64,80},{80,96},{96,112},{1,17},{17... | collective-permute-start | bytes 983048 | tf_op jit(solution)/shard_map/ppermute | solution.py:19
  245.8 9.3 %collective-permute-start.34 = (f32[32,1280]{1,0:T(8,128)S(1)}, f32[32,1280]{1,0:T(8,128)S(1)}, u32[]{:S(2)}, u32[]{:S(2)}) collective-permute-start(f32[32,1280]{1,0:T(8,128)S(1)} %get-tuple-element.199), channel_id=1, source_target_pairs={{0,2},{1,3},{2,4},{3,5},{4,6},{5,7},{6,8},{7,9},{8,10},{9,11},{10,... | collective-permute-start | bytes 491528 | tf_op jit(solution)/shard_map/ppermute | solution.py:19
  248.6 21.1 %collective-permute-start.41 = (f32[2,32,1280]{2,1,0:T(8,128)S(1)}, f32[2,32,1280]{2,1,0:T(8,128)S(1)}, u32[]{:S(2)}, u32[]{:S(2)}) collective-permute-start(f32[2,32,1280]{2,1,0:T(8,128)S(1)} %get-tuple-element.208), channel_id=1, source_target_pairs={{0,16},{16,32},{32,48},{48,64},{64,80},{80,96},{96,112},{1,17},{17... | collective-permute-start | bytes 983048 | tf_op jit(solution)/shard_map/ppermute | solution.py:19
  255.2 20.5 %collective-permute-start.39 = (f32[2,32,1280]{2,1,0:T(8,128)S(1)}, f32[2,32,1280]{2,1,0:T(8,128)S(1)}, u32[]{:S(2)}, u32[]{:S(2)}) collective-permute-start(f32[2,32,1280]{2,1,0:T(8,128)S(1)} %get-tuple-element.206), channel_id=1, source_target_pairs={{0,16},{16,32},{32,48},{48,64},{64,80},{80,96},{96,112},{1,17},{17... | collective-permute-start | bytes 983048 | tf_op jit(solution)/shard_map/ppermute | solution.py:19
  260.0 9.8 %collective-permute-start.40 = (f32[32,1280]{1,0:T(8,128)S(1)}, f32[32,1280]{1,0:T(8,128)S(1)}, u32[]{:S(2)}, u32[]{:S(2)}) collective-permute-start(f32[32,1280]{1,0:T(8,128)S(1)} %get-tuple-element.207), channel_id=1, source_target_pairs={{0,2},{1,3},{2,4},{3,5},{4,6},{5,7},{6,8},{7,9},{8,10},{9,11},{10,... | collective-permute-start | bytes 491528 | tf_op jit(solution)/shard_map/ppermute | solution.py:19
  269.8 21.5 %collective-permute-start.45 = (f32[2,32,1280]{2,1,0:T(8,128)S(1)}, f32[2,32,1280]{2,1,0:T(8,128)S(1)}, u32[]{:S(2)}, u32[]{:S(2)}) collective-permute-start(f32[2,32,1280]{2,1,0:T(8,128)S(1)} %get-tuple-element.214), channel_id=1, source_target_pairs={{0,16},{16,32},{32,48},{48,64},{64,80},{80,96},{96,112},{1,17},{17... | collective-permute-start | bytes 983048 | tf_op jit(solution)/shard_map/ppermute | solution.py:19
  275.7 21.8 %collective-permute-start.43 = (f32[2,32,1280]{2,1,0:T(8,128)S(1)}, f32[2,32,1280]{2,1,0:T(8,128)S(1)}, u32[]{:S(2)}, u32[]{:S(2)}) collective-permute-start(f32[2,32,1280]{2,1,0:T(8,128)S(1)} %get-tuple-element.212), channel_id=1, source_target_pairs={{0,16},{16,32},{32,48},{48,64},{64,80},{80,96},{96,112},{1,17},{17... | collective-permute-start | bytes 983048 | tf_op jit(solution)/shard_map/ppermute | solution.py:19
  280.1 11.2 %collective-permute-start.44 = (f32[32,1280]{1,0:T(8,128)S(1)}, f32[32,1280]{1,0:T(8,128)S(1)}, u32[]{:S(2)}, u32[]{:S(2)}) collective-permute-start(f32[32,1280]{1,0:T(8,128)S(1)} %get-tuple-element.213), channel_id=1, source_target_pairs={{0,2},{1,3},{2,4},{3,5},{4,6},{5,7},{6,8},{7,9},{8,10},{9,11},{10,... | collective-permute-start | bytes 491528 | tf_op jit(solution)/shard_map/ppermute | solution.py:19
  286.7 10.8 %collective-permute-start.42 = (f32[32,1280]{1,0:T(8,128)S(1)}, f32[32,1280]{1,0:T(8,128)S(1)}, u32[]{:S(2)}, u32[]{:S(2)}) collective-permute-start(f32[32,1280]{1,0:T(8,128)S(1)} %get-tuple-element.211), channel_id=1, source_target_pairs={{0,2},{1,3},{2,4},{3,5},{4,6},{5,7},{6,8},{7,9},{8,10},{9,11},{10,... | collective-permute-start | bytes 491528 | tf_op jit(solution)/shard_map/ppermute | solution.py:19
  291.3 20.9 %collective-permute-start.49 = (f32[2,32,1280]{2,1,0:T(8,128)S(1)}, f32[2,32,1280]{2,1,0:T(8,128)S(1)}, u32[]{:S(2)}, u32[]{:S(2)}) collective-permute-start(f32[2,32,1280]{2,1,0:T(8,128)S(1)} %get-tuple-element.220), channel_id=1, source_target_pairs={{0,16},{16,32},{32,48},{48,64},{64,80},{80,96},{96,112},{1,17},{17... | collective-permute-start | bytes 983048 | tf_op jit(solution)/shard_map/ppermute | solution.py:19
  297.5 25.4 %collective-permute-start.47 = (f32[2,32,1280]{2,1,0:T(8,128)S(1)}, f32[2,32,1280]{2,1,0:T(8,128)S(1)}, u32[]{:S(2)}, u32[]{:S(2)}) collective-permute-start(f32[2,32,1280]{2,1,0:T(8,128)S(1)} %get-tuple-element.218), channel_id=1, source_target_pairs={{0,16},{16,32},{32,48},{48,64},{64,80},{80,96},{96,112},{1,17},{17... | collective-permute-start | bytes 983048 | tf_op jit(solution)/shard_map/ppermute | solution.py:19
  304.4 12.3 %collective-permute-start.46 = (f32[32,1280]{1,0:T(8,128)S(1)}, f32[32,1280]{1,0:T(8,128)S(1)}, u32[]{:S(2)}, u32[]{:S(2)}) collective-permute-start(f32[32,1280]{1,0:T(8,128)S(1)} %get-tuple-element.217), channel_id=1, source_target_pairs={{0,2},{1,3},{2,4},{3,5},{4,6},{5,7},{6,8},{7,9},{8,10},{9,11},{10,... | collective-permute-start | bytes 491528 | tf_op jit(solution)/shard_map/ppermute | solution.py:19
  312.2 19.2 %collective-permute-start.53 = (f32[2,32,1280]{2,1,0:T(8,128)S(1)}, f32[2,32,1280]{2,1,0:T(8,128)S(1)}, u32[]{:S(2)}, u32[]{:S(2)}) collective-permute-start(f32[2,32,1280]{2,1,0:T(8,128)S(1)} %get-tuple-element.226), channel_id=1, source_target_pairs={{0,16},{16,32},{32,48},{48,64},{64,80},{80,96},{96,112},{1,17},{17... | collective-permute-start | bytes 983048 | tf_op jit(solution)/shard_map/ppermute | solution.py:19
  322.9 21.1 %collective-permute-start.51 = (f32[2,32,1280]{2,1,0:T(8,128)S(1)}, f32[2,32,1280]{2,1,0:T(8,128)S(1)}, u32[]{:S(2)}, u32[]{:S(2)}) collective-permute-start(f32[2,32,1280]{2,1,0:T(8,128)S(1)} %get-tuple-element.224), channel_id=1, source_target_pairs={{0,16},{16,32},{32,48},{48,64},{64,80},{80,96},{96,112},{1,17},{17... | collective-permute-start | bytes 983048 | tf_op jit(solution)/shard_map/ppermute | solution.py:19
  328.6 9.2 %collective-permute-start.50 = (f32[32,1280]{1,0:T(8,128)S(1)}, f32[32,1280]{1,0:T(8,128)S(1)}, u32[]{:S(2)}, u32[]{:S(2)}) collective-permute-start(f32[32,1280]{1,0:T(8,128)S(1)} %get-tuple-element.223), channel_id=1, source_target_pairs={{0,2},{1,3},{2,4},{3,5},{4,6},{5,7},{6,8},{7,9},{8,10},{9,11},{10,... | collective-permute-start | bytes 491528 | tf_op jit(solution)/shard_map/ppermute | solution.py:19
  331.4 26.4 %collective-permute-start.57 = (f32[2,32,1280]{2,1,0:T(8,128)S(1)}, f32[2,32,1280]{2,1,0:T(8,128)S(1)}, u32[]{:S(2)}, u32[]{:S(2)}) collective-permute-start(f32[2,32,1280]{2,1,0:T(8,128)S(1)} %get-tuple-element.232), channel_id=1, source_target_pairs={{0,16},{16,32},{32,48},{48,64},{64,80},{80,96},{96,112},{1,17},{17... | collective-permute-start | bytes 983048 | tf_op jit(solution)/shard_map/ppermute | solution.py:19
  343.9 21.1 %collective-permute-start.55 = (f32[2,32,1280]{2,1,0:T(8,128)S(1)}, f32[2,32,1280]{2,1,0:T(8,128)S(1)}, u32[]{:S(2)}, u32[]{:S(2)}) collective-permute-start(f32[2,32,1280]{2,1,0:T(8,128)S(1)} %get-tuple-element.230), channel_id=1, source_target_pairs={{0,16},{16,32},{32,48},{48,64},{64,80},{80,96},{96,112},{1,17},{17... | collective-permute-start | bytes 983048 | tf_op jit(solution)/shard_map/ppermute | solution.py:19
  349.7 12.7 %collective-permute-start.54 = (f32[32,1280]{1,0:T(8,128)S(1)}, f32[32,1280]{1,0:T(8,128)S(1)}, u32[]{:S(2)}, u32[]{:S(2)}) collective-permute-start(f32[32,1280]{1,0:T(8,128)S(1)} %get-tuple-element.229), channel_id=1, source_target_pairs={{0,2},{1,3},{2,4},{3,5},{4,6},{5,7},{6,8},{7,9},{8,10},{9,11},{10,... | collective-permute-start | bytes 491528 | tf_op jit(solution)/shard_map/ppermute | solution.py:19
  357.9 21.2 %collective-permute-start.61 = (f32[2,32,1280]{2,1,0:T(8,128)S(1)}, f32[2,32,1280]{2,1,0:T(8,128)S(1)}, u32[]{:S(2)}, u32[]{:S(2)}) collective-permute-start(f32[2,32,1280]{2,1,0:T(8,128)S(1)} %get-tuple-element.238), channel_id=1, source_target_pairs={{0,16},{16,32},{32,48},{48,64},{64,80},{80,96},{96,112},{1,17},{17... | collective-permute-start | bytes 983048 | tf_op jit(solution)/shard_map/ppermute | solution.py:19
  365.0 21.1 %collective-permute-start.59 = (f32[2,32,1280]{2,1,0:T(8,128)S(1)}, f32[2,32,1280]{2,1,0:T(8,128)S(1)}, u32[]{:S(2)}, u32[]{:S(2)}) collective-permute-start(f32[2,32,1280]{2,1,0:T(8,128)S(1)} %get-tuple-element.236), channel_id=1, source_target_pairs={{0,16},{16,32},{32,48},{48,64},{64,80},{80,96},{96,112},{1,17},{17... | collective-permute-start | bytes 983048 | tf_op jit(solution)/shard_map/ppermute | solution.py:19
  370.7 12.7 %collective-permute-start.58 = (f32[32,1280]{1,0:T(8,128)S(1)}, f32[32,1280]{1,0:T(8,128)S(1)}, u32[]{:S(2)}, u32[]{:S(2)}) collective-permute-start(f32[32,1280]{1,0:T(8,128)S(1)} %get-tuple-element.235), channel_id=1, source_target_pairs={{0,2},{1,3},{2,4},{3,5},{4,6},{5,7},{6,8},{7,9},{8,10},{9,11},{10,... | collective-permute-start | bytes 491528 | tf_op jit(solution)/shard_map/ppermute | solution.py:19
  379.1 21.1 %collective-permute-start.65 = (f32[2,32,1280]{2,1,0:T(8,128)S(1)}, f32[2,32,1280]{2,1,0:T(8,128)S(1)}, u32[]{:S(2)}, u32[]{:S(2)}) collective-permute-start(f32[2,32,1280]{2,1,0:T(8,128)S(1)} %get-tuple-element.244), channel_id=1, source_target_pairs={{0,16},{16,32},{32,48},{48,64},{64,80},{80,96},{96,112},{1,17},{17... | collective-permute-start | bytes 983048 | tf_op jit(solution)/shard_map/ppermute | solution.py:19
  386.2 26.0 %collective-permute-start.63 = (f32[2,32,1280]{2,1,0:T(8,128)S(1)}, f32[2,32,1280]{2,1,0:T(8,128)S(1)}, u32[]{:S(2)}, u32[]{:S(2)}) collective-permute-start(f32[2,32,1280]{2,1,0:T(8,128)S(1)} %get-tuple-element.242), channel_id=1, source_target_pairs={{0,16},{16,32},{32,48},{48,64},{64,80},{80,96},{96,112},{1,17},{17... | collective-permute-start | bytes 983048 | tf_op jit(solution)/shard_map/ppermute | solution.py:19
  392.0 12.6 %collective-permute-start.62 = (f32[32,1280]{1,0:T(8,128)S(1)}, f32[32,1280]{1,0:T(8,128)S(1)}, u32[]{:S(2)}, u32[]{:S(2)}) collective-permute-start(f32[32,1280]{1,0:T(8,128)S(1)} %get-tuple-element.241), channel_id=1, source_target_pairs={{0,2},{1,3},{2,4},{3,5},{4,6},{5,7},{6,8},{7,9},{8,10},{9,11},{10,... | collective-permute-start | bytes 491528 | tf_op jit(solution)/shard_map/ppermute | solution.py:19
  400.1 22.6 %collective-permute-start.69 = (f32[2,32,1280]{2,1,0:T(8,128)S(1)}, f32[2,32,1280]{2,1,0:T(8,128)S(1)}, u32[]{:S(2)}, u32[]{:S(2)}) collective-permute-start(f32[2,32,1280]{2,1,0:T(8,128)S(1)} %get-tuple-element.250), channel_id=1, source_target_pairs={{0,16},{16,32},{32,48},{48,64},{64,80},{80,96},{96,112},{1,17},{17... | collective-permute-start | bytes 983048 | tf_op jit(solution)/shard_map/ppermute | solution.py:19
  412.3 23.0 %collective-permute-start.67 = (f32[2,32,1280]{2,1,0:T(8,128)S(1)}, f32[2,32,1280]{2,1,0:T(8,128)S(1)}, u32[]{:S(2)}, u32[]{:S(2)}) collective-permute-start(f32[2,32,1280]{2,1,0:T(8,128)S(1)} %get-tuple-element.248), channel_id=1, source_target_pairs={{0,16},{16,32},{32,48},{48,64},{64,80},{80,96},{96,112},{1,17},{17... | collective-permute-start | bytes 983048 | tf_op jit(solution)/shard_map/ppermute | solution.py:19
  422.7 21.1 %collective-permute-start.73 = (f32[2,32,1280]{2,1,0:T(8,128)S(1)}, f32[2,32,1280]{2,1,0:T(8,128)S(1)}, u32[]{:S(2)}, u32[]{:S(2)}) collective-permute-start(f32[2,32,1280]{2,1,0:T(8,128)S(1)} %get-tuple-element.256), channel_id=1, source_target_pairs={{0,16},{16,32},{32,48},{48,64},{64,80},{80,96},{96,112},{1,17},{17... | collective-permute-start | bytes 983048 | tf_op jit(solution)/shard_map/ppermute | solution.py:19
  435.2 21.1 %collective-permute-start.71 = (f32[2,32,1280]{2,1,0:T(8,128)S(1)}, f32[2,32,1280]{2,1,0:T(8,128)S(1)}, u32[]{:S(2)}, u32[]{:S(2)}) collective-permute-start(f32[2,32,1280]{2,1,0:T(8,128)S(1)} %get-tuple-element.254), channel_id=1, source_target_pairs={{0,16},{16,32},{32,48},{48,64},{64,80},{80,96},{96,112},{1,17},{17... | collective-permute-start | bytes 983048 | tf_op jit(solution)/shard_map/ppermute | solution.py:19
  443.8 21.1 %collective-permute-start.77 = (f32[2,32,1280]{2,1,0:T(8,128)S(1)}, f32[2,32,1280]{2,1,0:T(8,128)S(1)}, u32[]{:S(2)}, u32[]{:S(2)}) collective-permute-start(f32[2,32,1280]{2,1,0:T(8,128)S(1)} %get-tuple-element.262), channel_id=1, source_target_pairs={{0,16},{16,32},{32,48},{48,64},{64,80},{80,96},{96,112},{1,17},{17... | collective-permute-start | bytes 983048 | tf_op jit(solution)/shard_map/ppermute | solution.py:19
  456.3 21.1 %collective-permute-start.75 = (f32[2,32,1280]{2,1,0:T(8,128)S(1)}, f32[2,32,1280]{2,1,0:T(8,128)S(1)}, u32[]{:S(2)}, u32[]{:S(2)}) collective-permute-start(f32[2,32,1280]{2,1,0:T(8,128)S(1)} %get-tuple-element.260), channel_id=1, source_target_pairs={{0,16},{16,32},{32,48},{48,64},{64,80},{80,96},{96,112},{1,17},{17... | collective-permute-start | bytes 983048 | tf_op jit(solution)/shard_map/ppermute | solution.py:19
  464.8 22.9 %collective-permute-start.81 = (f32[2,32,1280]{2,1,0:T(8,128)S(1)}, f32[2,32,1280]{2,1,0:T(8,128)S(1)}, u32[]{:S(2)}, u32[]{:S(2)}) collective-permute-start(f32[2,32,1280]{2,1,0:T(8,128)S(1)} %get-tuple-element.268), channel_id=1, source_target_pairs={{0,16},{16,32},{32,48},{48,64},{64,80},{80,96},{96,112},{1,17},{17... | collective-permute-start | bytes 983048 | tf_op jit(solution)/shard_map/ppermute | solution.py:19
  477.4 17.6 %collective-permute-start.79 = (f32[2,32,1280]{2,1,0:T(8,128)S(1)}, f32[2,32,1280]{2,1,0:T(8,128)S(1)}, u32[]{:S(2)}, u32[]{:S(2)}) collective-permute-start(f32[2,32,1280]{2,1,0:T(8,128)S(1)} %get-tuple-element.266), channel_id=1, source_target_pairs={{0,16},{16,32},{32,48},{48,64},{64,80},{80,96},{96,112},{1,17},{17... | collective-permute-start | bytes 983048 | tf_op jit(solution)/shard_map/ppermute | solution.py:19
  487.8 15.7 %collective-permute-start.85 = (f32[2,32,1280]{2,1,0:T(8,128)S(1)}, f32[2,32,1280]{2,1,0:T(8,128)S(1)}, u32[]{:S(2)}, u32[]{:S(2)}) collective-permute-start(f32[2,32,1280]{2,1,0:T(8,128)S(1)} %get-tuple-element.274), channel_id=1, source_target_pairs={{0,16},{16,32},{32,48},{48,64},{64,80},{80,96},{96,112},{1,17},{17... | collective-permute-start | bytes 983048 | tf_op jit(solution)/shard_map/ppermute | solution.py:19
  494.9 10.3 %collective-permute-start.83 = (f32[2,32,1280]{2,1,0:T(8,128)S(1)}, f32[2,32,1280]{2,1,0:T(8,128)S(1)}, u32[]{:S(2)}, u32[]{:S(2)}) collective-permute-start(f32[2,32,1280]{2,1,0:T(8,128)S(1)} %get-tuple-element.272), channel_id=1, source_target_pairs={{0,16},{16,32},{32,48},{48,64},{64,80},{80,96},{96,112},{1,17},{17... | collective-permute-start | bytes 983048 | tf_op jit(solution)/shard_map/ppermute | solution.py:19
  509.0 26.1 %collective-permute-start.86 = (f32[512,1280]{1,0:T(8,128)}, f32[512,1280]{1,0:T(8,128)}, u32[]{:S(2)}, u32[]{:S(2)}) collective-permute-start(f32[512,1280]{1,0:T(8,128)} %get-tuple-element.284), channel_id=1, source_target_pairs={{0,1},{1,0},{2,3},{3,2},{4,5},{5,4},{6,7},{7,6},{8,9},{9,8},{10,11... | collective-permute-start | bytes 7864328 | tf_op jit(solution)/shard_map/ppermute | solution.py:24
  525.0 42.3 %all-to-all-start = ((f32[8,2,64,512]{3,2,1,0:T(8,128)}), f32[8,2,64,512]{3,2,1,0:T(8,128)}, u32[]{:S(2)}, u32[]{:S(2)}) async-start(f32[8,2,64,512]{3,2,1,0:T(8,128)} %copy-done.22), calls=%async_computation | async-start | bytes 4194304 | tf_op jit(solution)/shard_map/all_to_all | solution.py:344
  567.3 35.3 %all-to-all-start.1 = ((f32[8,2,64,512]{3,2,1,0:T(8,128)}), f32[8,2,64,512]{3,2,1,0:T(8,128)}, u32[]{:S(2)}, u32[]{:S(2)}) async-start(f32[8,2,64,512]{3,2,1,0:T(8,128)} %copy-done.21), calls=%async_computation.1 | async-start | bytes 4194304 | tf_op jit(solution)/shard_map/all_to_all | solution.py:346
  (49 other events, 254.7 us)

commit v2 on v1

--- a/solution.py
+++ b/solution.py
@@ -11,12 +11,19 @@
 UNIT = 32
 SKEW = 2
 VMEM = pltpu.MemorySpace.VMEM
+HBM = pltpu.MemorySpace.HBM
 SMEM = pltpu.MemorySpace.SMEM
 
 
-def passed_along(value, axis, steps):
-    count = lax.axis_size(axis)
-    return lax.ppermute(value, axis, [(place, place + steps) for place in range(count - steps)])
+def passed_along(value, moved, live):
+    columns, rows = lax.axis_size("gx"), lax.axis_size("gz")
+    across, down = moved
+    pairs = []
+    for column in range(columns - across):
+        for row in range(rows - down):
+            if live(row // 2 + column):
+                pairs.append((column * rows + row, (column + across) * rows + row + down))
+    return lax.ppermute(value, ("gx", "gz"), pairs)
 
 
 def swapped(value, axis):
@@ -38,7 +45,7 @@
     return pl.pallas_call(
         pick_kernel,
         out_shape=pltpu.VMEM((count,) + sources.shape[1:], sources.dtype),
-        in_specs=[pl.BlockSpec(memory_space=SMEM), pl.BlockSpec(memory_space=pl.ANY)],
+        in_specs=[pl.BlockSpec(memory_space=SMEM), pl.BlockSpec(memory_space=HBM)],
         out_specs=pl.BlockSpec(memory_space=VMEM),
         scratch_shapes=[pltpu.SemaphoreType.DMA((count,))],
         compiler_params=pltpu.CompilerParams(vmem_limit_bytes=4 * 1024 * 1024),
@@ -110,7 +117,7 @@
     shots = sources.shape[2]
     columns = count * shots
     scalar = pl.BlockSpec(memory_space=SMEM)
-    anywhere = pl.BlockSpec(memory_space=pl.ANY)
+    anywhere = pl.BlockSpec(memory_space=HBM)
     inside = pl.BlockSpec(memory_space=VMEM)
     return pl.pallas_call(
         own_kernel,
@@ -130,7 +137,7 @@
 def other_side(core, green, theirs, pairs, inputs):
     count, trace, shots = theirs.shape
     scalar = pl.BlockSpec(memory_space=SMEM)
-    anywhere = pl.BlockSpec(memory_space=pl.ANY)
+    anywhere = pl.BlockSpec(memory_space=HBM)
     inside = pl.BlockSpec(memory_space=VMEM)
     return pl.pallas_call(
         other_kernel,
@@ -207,8 +214,8 @@
 
 
 def released(core, store):
-    shape = jax.ShapeDtypeStruct(store.shape[1:], store.dtype)
-    anywhere = pl.BlockSpec(memory_space=pl.ANY)
+    shape = pltpu.HBM(store.shape[1:], store.dtype)
+    anywhere = pl.BlockSpec(memory_space=HBM)
     return pl.pallas_call(
         release_kernel,
         out_shape=(shape, shape),
@@ -227,9 +234,9 @@
     def _():
         copy = pltpu.make_async_copy(probe, whole, sem)
         copy.start()
-        receivers = places.shape[0]
-        slots = lax.broadcasted_iota(jnp.int32, (receivers, receivers), 1)
-        chosen = jnp.where(slots == places[...], 1.0, 0.0).astype(jnp.bfloat16)
+        receivers = places.shape[1]
+        slots = lax.broadcasted_iota(jnp.int32, (receivers, receivers), 0)
+        chosen = jnp.where(slots == places[...], 1.0, 0.0).T.astype(jnp.bfloat16)
         copy.wait()
         for component in range(whole.shape[0] // receivers):
             span = pl.ds(component * receivers, receivers)
@@ -245,7 +252,7 @@
     return pl.pallas_call(
         order_kernel,
         out_shape=(shape, shape),
-        in_specs=[pl.BlockSpec(memory_space=SMEM), inside, pl.BlockSpec(memory_space=pl.ANY)] + [inside] * len(more),
+        in_specs=[pl.BlockSpec(memory_space=SMEM), inside, pl.BlockSpec(memory_space=HBM)] + [inside] * len(more),
         out_specs=(inside, inside),
         input_output_aliases={3 + number: number for number in range(len(more))},
         scratch_shapes=[pltpu.VMEM(probe.shape, jnp.float32), pltpu.SemaphoreType.DMA],
@@ -284,11 +291,11 @@
 def gathered(traces, high, low, owners):
     columns, trace = traces.shape
     inside = pl.BlockSpec(memory_space=VMEM)
-    anywhere = pl.BlockSpec(memory_space=pl.ANY)
+    anywhere = pl.BlockSpec(memory_space=HBM)
     return pl.pallas_call(
         gather_kernel,
         out_shape=(
-            jax.ShapeDtypeStruct((trace, columns), jnp.float32),
+            pltpu.HBM((trace, columns), jnp.float32),
             jax.ShapeDtypeStruct((owners, 2, high.shape[0] // (2 * owners), columns), jnp.float32),
         ),
         in_specs=[inside] * 3,
@@ -313,19 +320,22 @@
     shots = sources.shape[4]
     units = half * shots // UNIT
     steps = units + SKEW * (columns + rows // 2 - 2)
-    receivers = owner_map.shape[1]
-
+
+    here = pltpu.with_memory_space_constraint(sources[0, 0], HBM)
+    operator = pltpu.with_memory_space_constraint(operator, HBM)
+    probes = pltpu.with_memory_space_constraint(probe[0, 0], HBM)
     other_operator = swapped(operator, "gz")
     on_diag = lax.dynamic_index_in_dim(batch_pick, row + column, 1, keepdims=False).reshape(2, half)
     picks = jnp.where(core == 0, on_diag, on_diag[::-1])
-    theirs = swapped(picked(picks, sources[0, 0]), "gz")
     core_word = core.astype(jnp.int32).reshape(1)
-    pairs, inputs, store = own_side(core_word, picks, operator, sources[0, 0])
+    places = owner_map
+    late = (chip_diag < 2).astype(jnp.int32).reshape(1)
+    early = 1 - late
+    picks, places, late, early, core_word = lax.optimization_barrier((picks, places, late, early, core_word))
+    theirs = swapped(picked(picks, here), "gz")
+    pairs, inputs, store = own_side(core_word, picks, operator, here)
+    high, low = ordered(early, places, probes)
     pairs, inputs = other_side(core_word, other_operator, theirs, pairs, inputs)
-
-    places = owner_map.reshape(receivers, 1)
-    late = (chip_diag < 2).astype(jnp.int32).reshape(1)
-    high, low = ordered(1 - late, places, probe[0, 0])
 
     base = (SKEW * chip_diag).astype(jnp.int32).reshape(1)
     uppers = [jnp.zeros((UNIT, trace), jnp.float32)] * SKEW
@@ -333,10 +343,13 @@
     for step in range(steps):
         right, lower, store = swept(step, units, base, pairs, inputs, uppers[step], lefters[step], store)
         if step + SKEW < steps:
-            lefters.append(passed_along(right, "gx", 1))
-            uppers.append(passed_along(lower, "gz", 2))
+            def live(diag, step=step):
+                return 0 <= step - SKEW * diag < units
+
+            lefters.append(passed_along(right, (1, 0), live))
+            uppers.append(passed_along(lower, (0, 2), live))
         if step == steps - 4:
-            high, low = ordered(late, places, probe[0, 0], (high, low))
+            high, low = ordered(late, places, probes, (high, low))
 
     own_traces, other_traces = released(core_word, store)
     arrived = swapped(other_traces, "gz")

time: 617 us -> 822 us (1.33)
  the two profiles are of different devices: /device:TPU:0 before, /device:TPU:70 now
where the time goes in v2:
time: 822 us; the launch traced here: 812 us
  starting transfers between devices  661 us (80%)
  Pallas kernels  85 us (10%)
  waiting for transfers between devices  44.8 us (5%)
  other arithmetic  10.1 us (1%)
  local copies, waits for them, and re-layouts  8.4 us (1%)
    ppermute x84, starting transfers between devices, passed_along(): return lax.ppermute(value, ('gx', 'gz'), pairs)  584 us
    all_to_all x1, starting transfers between devices, local(): lax.all_to_all(own_partial, 'gx', split_axis=0, concat_axis=0, tiled=True)  64.9 us
    pallas_call x44, Pallas kernels, swept(): pl.pallas_call(functools.partial(sweep_kernel, step, units), out_shape=(p...  44.2 us
    all_to_all x1, waiting for transfers between devices, local(): lax.all_to_all(own_partial, 'gx', split_axis=0, concat_axis=0, tiled=True)  22.9 us
    all_to_all x1, waiting for transfers between devices, local(): lax.all_to_all(far_partial, 'gx', split_axis=0, concat_axis=0, tiled=True)  21.7 us
  transfers between devices with their start and end apart: 89, of which 2 were waited for; matrix products, arithmetic and copies ran while one was open for 1% of the time, Pallas kernels for 9%

profile of v2, /device:TPU:70, one launch (start us, length us, event | category | flops | bytes accessed | tf_op | source)
XLA Modules:
  0.0 812.2 jit_solution(15744520487190262487)
XLA Ops:
  1.6 3.8 pick.1
  5.4 9.2 %collective-permute-start.1 = (f32[4,1280,128]{2,1,0:T(8,128)}, f32[4,1280,128]{2,1,0:T(8,128)S(1)}, u32[]{:S(2)}, u32[]{:S(2)}) collective-permute-start(f32[4,1280,128]{2,1,0:T(8,128)} %pick.1), channel_id=1, source_target_pairs={{0,1},{1,0},{2,3},{3,2},{4,5},{5,4},{6,7},{7,6},{8,9},{9,8},{10,11... | collective-permute-start | bytes 7864328 | tf_op jit(solution)/shard_map/ppermute | solution.py:31
  14.6 9.6 %own.1 = (bf16[2,1280,2560]{2,1,0:T(8,128)(2,1)S(1)}, f32[2,512,1280]{2,1,0:T(8,128)S(1)}, f32[2,512,1280]{2,1,0:T(8,128)S(1)}) custom-call(s32[1]{0:T(128)} %bitcast.1.core, s32[2,4]{1,0:T(2,128)S(1)} %broadcast_select_fusion.picks, f32[1280,1280]{1,0:T(8,128)} %bitcast.15, f32[8,1280,128]{2,1,0:T(8,128)} %bitcast.11), custom_call_target="tpu_custom_call" | custom-call | tf_op jit(solution)/shard_map/own/pallas_call | solution.py:122
  24.2 8.9 %other.1 = (bf16[2,1280,2560]{2,1,0:T(8,128)(2,1)S(1)}, f32[2,512,1280]{2,1,0:T(8,128)S(1)}) custom-call(s32[1]{0:T(128)} %bitcast.1.core, f32[1280,1280]{1,0:T(8,128)} %collective-permute-done.green, f32[4,1280,128]{2,1,0:T(8,128)S(1)} %collective-permute-done.1.theirs, ...), custom_call_target="tpu_custom_call", output_to_operand_aliasing={{0}: (3, {}), {1}: (4, {})} | custom-call | tf_op jit(solution)/shard_map/other/pallas_call | solution.py:142
  44.5 60.7 %collective-permute-start.21 = (f32[2,32,1280]{2,1,0:T(8,128)S(1)}, f32[2,32,1280]{2,1,0:T(8,128)S(1)}, u32[]{:S(2)}, u32[]{:S(2)}) collective-permute-start(f32[2,32,1280]{2,1,0:T(8,128)S(1)} %get-tuple-element.185), channel_id=1, source_target_pairs={{0,16},{1,17},{2,18},{3,19},{4,20},{5,21},{6,22},{7,23},{8,24},{9,... | collective-permute-start | bytes 983048 | tf_op jit(solution)/shard_map/ppermute | solution.py:26
  105.2 9.6 %collective-permute-start.19 = (f32[2,32,1280]{2,1,0:T(8,128)S(1)}, f32[2,32,1280]{2,1,0:T(8,128)S(1)}, u32[]{:S(2)}, u32[]{:S(2)}) collective-permute-start(f32[2,32,1280]{2,1,0:T(8,128)S(1)} %get-tuple-element.183), channel_id=1, source_target_pairs={{0,16},{1,17},{2,18},{3,19},{4,20},{5,21},{6,22},{7,23},{8,24},{9,... | collective-permute-start | bytes 983048 | tf_op jit(solution)/shard_map/ppermute | solution.py:26
  116.2 19.0 %collective-permute-start.25 = (f32[2,32,1280]{2,1,0:T(8,128)S(1)}, f32[2,32,1280]{2,1,0:T(8,128)S(1)}, u32[]{:S(2)}, u32[]{:S(2)}) collective-permute-start(f32[2,32,1280]{2,1,0:T(8,128)S(1)} %get-tuple-element.191), channel_id=1, source_target_pairs={{0,16},{1,17},{2,18},{3,19},{4,20},{5,21},{6,22},{7,23},{8,24},{9,... | collective-permute-start | bytes 983048 | tf_op jit(solution)/shard_map/ppermute | solution.py:26
  135.3 9.6 %collective-permute-start.23 = (f32[2,32,1280]{2,1,0:T(8,128)S(1)}, f32[2,32,1280]{2,1,0:T(8,128)S(1)}, u32[]{:S(2)}, u32[]{:S(2)}) collective-permute-start(f32[2,32,1280]{2,1,0:T(8,128)S(1)} %get-tuple-element.189), channel_id=1, source_target_pairs={{0,16},{1,17},{2,18},{3,19},{4,20},{5,21},{6,22},{7,23},{8,24},{9,... | collective-permute-start | bytes 983048 | tf_op jit(solution)/shard_map/ppermute | solution.py:26
  144.8 9.6 %collective-permute-start.24 = (f32[32,1280]{1,0:T(8,128)S(1)}, f32[32,1280]{1,0:T(8,128)S(1)}, u32[]{:S(2)}, u32[]{:S(2)}) collective-permute-start(f32[32,1280]{1,0:T(8,128)S(1)} %get-tuple-element.190), channel_id=1, source_target_pairs={{0,2},{1,3},{2,4},{3,5},{4,6},{5,7},{6,8},{7,9},{8,10},{9,11},{10,... | collective-permute-start | bytes 491528 | tf_op jit(solution)/shard_map/ppermute | solution.py:26
  154.4 9.6 %collective-permute-start.22 = (f32[32,1280]{1,0:T(8,128)S(1)}, f32[32,1280]{1,0:T(8,128)S(1)}, u32[]{:S(2)}, u32[]{:S(2)}) collective-permute-start(f32[32,1280]{1,0:T(8,128)S(1)} %get-tuple-element.188), channel_id=1, source_target_pairs={{0,2},{1,3},{2,4},{3,5},{4,6},{5,7},{6,8},{7,9},{8,10},{9,11},{10,... | collective-permute-start | bytes 491528 | tf_op jit(solution)/shard_map/ppermute | solution.py:26
  164.0 9.6 %collective-permute-start.29 = (f32[2,32,1280]{2,1,0:T(8,128)S(1)}, f32[2,32,1280]{2,1,0:T(8,128)S(1)}, u32[]{:S(2)}, u32[]{:S(2)}) collective-permute-start(f32[2,32,1280]{2,1,0:T(8,128)S(1)} %get-tuple-element.197), channel_id=1, source_target_pairs={{0,16},{1,17},{2,18},{3,19},{4,20},{5,21},{6,22},{7,23},{8,24},{9,... | collective-permute-start | bytes 983048 | tf_op jit(solution)/shard_map/ppermute | solution.py:26
  173.7 10.3 %collective-permute-start.27 = (f32[2,32,1280]{2,1,0:T(8,128)S(1)}, f32[2,32,1280]{2,1,0:T(8,128)S(1)}, u32[]{:S(2)}, u32[]{:S(2)}) collective-permute-start(f32[2,32,1280]{2,1,0:T(8,128)S(1)} %get-tuple-element.195), channel_id=1, source_target_pairs={{0,16},{1,17},{2,18},{3,19},{4,20},{5,21},{6,22},{7,23},{8,24},{9,... | collective-permute-start | bytes 983048 | tf_op jit(solution)/shard_map/ppermute | solution.py:26
  183.9 10.0 %collective-permute-start.28 = (f32[32,1280]{1,0:T(8,128)S(1)}, f32[32,1280]{1,0:T(8,128)S(1)}, u32[]{:S(2)}, u32[]{:S(2)}) collective-permute-start(f32[32,1280]{1,0:T(8,128)S(1)} %get-tuple-element.196), channel_id=1, source_target_pairs={{0,2},{1,3},{2,4},{3,5},{4,6},{5,7},{6,8},{7,9},{8,10},{9,11},{10,... | collective-permute-start | bytes 491528 | tf_op jit(solution)/shard_map/ppermute | solution.py:26
  193.9 9.5 %collective-permute-start.26 = (f32[32,1280]{1,0:T(8,128)S(1)}, f32[32,1280]{1,0:T(8,128)S(1)}, u32[]{:S(2)}, u32[]{:S(2)}) collective-permute-start(f32[32,1280]{1,0:T(8,128)S(1)} %get-tuple-element.194), channel_id=1, source_target_pairs={{0,2},{1,3},{2,4},{3,5},{4,6},{5,7},{6,8},{7,9},{8,10},{9,11},{10,... | collective-permute-start | bytes 491528 | tf_op jit(solution)/shard_map/ppermute | solution.py:26
  206.1 8.4 %collective-permute-start.33 = (f32[2,32,1280]{2,1,0:T(8,128)S(1)}, f32[2,32,1280]{2,1,0:T(8,128)S(1)}, u32[]{:S(2)}, u32[]{:S(2)}) collective-permute-start(f32[2,32,1280]{2,1,0:T(8,128)S(1)} %get-tuple-element.203), channel_id=1, source_target_pairs={{0,16},{1,17},{2,18},{3,19},{4,20},{5,21},{6,22},{7,23},{8,24},{9,... | collective-permute-start | bytes 983048 | tf_op jit(solution)/shard_map/ppermute | solution.py:26
  217.3 8.4 %collective-permute-start.31 = (f32[2,32,1280]{2,1,0:T(8,128)S(1)}, f32[2,32,1280]{2,1,0:T(8,128)S(1)}, u32[]{:S(2)}, u32[]{:S(2)}) collective-permute-start(f32[2,32,1280]{2,1,0:T(8,128)S(1)} %get-tuple-element.201), channel_id=1, source_target_pairs={{0,16},{1,17},{2,18},{3,19},{4,20},{5,21},{6,22},{7,23},{8,24},{9,... | collective-permute-start | bytes 983048 | tf_op jit(solution)/shard_map/ppermute | solution.py:26
  225.7 8.9 %collective-permute-start.32 = (f32[32,1280]{1,0:T(8,128)S(1)}, f32[32,1280]{1,0:T(8,128)S(1)}, u32[]{:S(2)}, u32[]{:S(2)}) collective-permute-start(f32[32,1280]{1,0:T(8,128)S(1)} %get-tuple-element.202), channel_id=1, source_target_pairs={{0,2},{1,3},{2,4},{3,5},{4,6},{5,7},{6,8},{7,9},{8,10},{9,11},{10,... | collective-permute-start | bytes 491528 | tf_op jit(solution)/shard_map/ppermute | solution.py:26
  234.6 9.6 %collective-permute-start.30 = (f32[32,1280]{1,0:T(8,128)S(1)}, f32[32,1280]{1,0:T(8,128)S(1)}, u32[]{:S(2)}, u32[]{:S(2)}) collective-permute-start(f32[32,1280]{1,0:T(8,128)S(1)} %get-tuple-element.200), channel_id=1, source_target_pairs={{0,2},{1,3},{2,4},{3,5},{4,6},{5,7},{6,8},{7,9},{8,10},{9,11},{10,... | collective-permute-start | bytes 491528 | tf_op jit(solution)/shard_map/ppermute | solution.py:26
  246.8 9.1 %collective-permute-start.37 = (f32[2,32,1280]{2,1,0:T(8,128)S(1)}, f32[2,32,1280]{2,1,0:T(8,128)S(1)}, u32[]{:S(2)}, u32[]{:S(2)}) collective-permute-start(f32[2,32,1280]{2,1,0:T(8,128)S(1)} %get-tuple-element.209), channel_id=1, source_target_pairs={{2,18},{3,19},{4,20},{5,21},{6,22},{7,23},{8,24},{9,25},{10,26},{1... | collective-permute-start | bytes 983048 | tf_op jit(solution)/shard_map/ppermute | solution.py:26
  255.9 2.7 sweep.61
  258.6 8.6 %collective-permute-start.35 = (f32[2,32,1280]{2,1,0:T(8,128)S(1)}, f32[2,32,1280]{2,1,0:T(8,128)S(1)}, u32[]{:S(2)}, u32[]{:S(2)}) collective-permute-start(f32[2,32,1280]{2,1,0:T(8,128)S(1)} %get-tuple-element.207), channel_id=1, source_target_pairs={{2,18},{3,19},{4,20},{5,21},{6,22},{7,23},{8,24},{9,25},{10,26},{1... | collective-permute-start | bytes 983048 | tf_op jit(solution)/shard_map/ppermute | solution.py:26
  267.2 8.9 %collective-permute-start.36 = (f32[32,1280]{1,0:T(8,128)S(1)}, f32[32,1280]{1,0:T(8,128)S(1)}, u32[]{:S(2)}, u32[]{:S(2)}) collective-permute-start(f32[32,1280]{1,0:T(8,128)S(1)} %get-tuple-element.208), channel_id=1, source_target_pairs={{2,4},{3,5},{4,6},{5,7},{6,8},{7,9},{8,10},{9,11},{10,12},{11,13},... | collective-permute-start | bytes 491528 | tf_op jit(solution)/shard_map/ppermute | solution.py:26
  276.1 9.6 %collective-permute-start.34 = (f32[32,1280]{1,0:T(8,128)S(1)}, f32[32,1280]{1,0:T(8,128)S(1)}, u32[]{:S(2)}, u32[]{:S(2)}) collective-permute-start(f32[32,1280]{1,0:T(8,128)S(1)} %get-tuple-element.206), channel_id=1, source_target_pairs={{2,4},{3,5},{4,6},{5,7},{6,8},{7,9},{8,10},{9,11},{10,12},{11,13},... | collective-permute-start | bytes 491528 | tf_op jit(solution)/shard_map/ppermute | solution.py:26
  288.3 9.3 %collective-permute-start.41 = (f32[2,32,1280]{2,1,0:T(8,128)S(1)}, f32[2,32,1280]{2,1,0:T(8,128)S(1)}, u32[]{:S(2)}, u32[]{:S(2)}) collective-permute-start(f32[2,32,1280]{2,1,0:T(8,128)S(1)} %get-tuple-element.215), channel_id=1, source_target_pairs={{4,20},{5,21},{6,22},{7,23},{8,24},{9,25},{10,26},{11,27},{12,28},... | collective-permute-start | bytes 983048 | tf_op jit(solution)/shard_map/ppermute | solution.py:26
  297.6 2.7 sweep.63
  300.3 8.7 %collective-permute-start.39 = (f32[2,32,1280]{2,1,0:T(8,128)S(1)}, f32[2,32,1280]{2,1,0:T(8,128)S(1)}, u32[]{:S(2)}, u32[]{:S(2)}) collective-permute-start(f32[2,32,1280]{2,1,0:T(8,128)S(1)} %get-tuple-element.213), channel_id=1, source_target_pairs={{4,20},{5,21},{6,22},{7,23},{8,24},{9,25},{10,26},{11,27},{12,28},... | collective-permute-start | bytes 983048 | tf_op jit(solution)/shard_map/ppermute | solution.py:26
  308.9 8.9 %collective-permute-start.40 = (f32[32,1280]{1,0:T(8,128)S(1)}, f32[32,1280]{1,0:T(8,128)S(1)}, u32[]{:S(2)}, u32[]{:S(2)}) collective-permute-start(f32[32,1280]{1,0:T(8,128)S(1)} %get-tuple-element.214), channel_id=1, source_target_pairs={{4,6},{5,7},{6,8},{7,9},{8,10},{9,11},{10,12},{11,13},{12,14},{13,... | collective-permute-start | bytes 491528 | tf_op jit(solution)/shard_map/ppermute | solution.py:26
  317.8 9.5 %collective-permute-start.38 = (f32[32,1280]{1,0:T(8,128)S(1)}, f32[32,1280]{1,0:T(8,128)S(1)}, u32[]{:S(2)}, u32[]{:S(2)}) collective-permute-start(f32[32,1280]{1,0:T(8,128)S(1)} %get-tuple-element.212), channel_id=1, source_target_pairs={{4,6},{5,7},{6,8},{7,9},{8,10},{9,11},{10,12},{11,13},{12,14},{13,... | collective-permute-start | bytes 491528 | tf_op jit(solution)/shard_map/ppermute | solution.py:26
  330.0 10.2 %collective-permute-start.45 = (f32[2,32,1280]{2,1,0:T(8,128)S(1)}, f32[2,32,1280]{2,1,0:T(8,128)S(1)}, u32[]{:S(2)}, u32[]{:S(2)}) collective-permute-start(f32[2,32,1280]{2,1,0:T(8,128)S(1)} %get-tuple-element.221), channel_id=1, source_target_pairs={{6,22},{7,23},{8,24},{9,25},{10,26},{11,27},{12,28},{13,29},{14,30... | collective-permute-start | bytes 983048 | tf_op jit(solution)/shard_map/ppermute | solution.py:26
  342.9 10.2 %collective-permute-start.43 = (f32[2,32,1280]{2,1,0:T(8,128)S(1)}, f32[2,32,1280]{2,1,0:T(8,128)S(1)}, u32[]{:S(2)}, u32[]{:S(2)}) collective-permute-start(f32[2,32,1280]{2,1,0:T(8,128)S(1)} %get-tuple-element.219), channel_id=1, source_target_pairs={{6,22},{7,23},{8,24},{9,25},{10,26},{11,27},{12,28},{13,29},{14,30... | collective-permute-start | bytes 983048 | tf_op jit(solution)/shard_map/ppermute | solution.py:26
  353.1 9.5 %collective-permute-start.44 = (f32[32,1280]{1,0:T(8,128)S(1)}, f32[32,1280]{1,0:T(8,128)S(1)}, u32[]{:S(2)}, u32[]{:S(2)}) collective-permute-start(f32[32,1280]{1,0:T(8,128)S(1)} %get-tuple-element.220), channel_id=1, source_target_pairs={{6,8},{7,9},{8,10},{9,11},{10,12},{11,13},{12,14},{13,15},{20,22},... | collective-permute-start | bytes 491528 | tf_op jit(solution)/shard_map/ppermute | solution.py:26
  362.6 10.2 %collective-permute-start.42 = (f32[32,1280]{1,0:T(8,128)S(1)}, f32[32,1280]{1,0:T(8,128)S(1)}, u32[]{:S(2)}, u32[]{:S(2)}) collective-permute-start(f32[32,1280]{1,0:T(8,128)S(1)} %get-tuple-element.218), channel_id=1, source_target_pairs={{6,8},{7,9},{8,10},{9,11},{10,12},{11,13},{12,14},{13,15},{20,22},... | collective-permute-start | bytes 491528 | tf_op jit(solution)/shard_map/ppermute | solution.py:26
  375.4 10.9 %collective-permute-start.49 = (f32[2,32,1280]{2,1,0:T(8,128)S(1)}, f32[2,32,1280]{2,1,0:T(8,128)S(1)}, u32[]{:S(2)}, u32[]{:S(2)}) collective-permute-start(f32[2,32,1280]{2,1,0:T(8,128)S(1)} %get-tuple-element.227), channel_id=1, source_target_pairs={{8,24},{9,25},{10,26},{11,27},{12,28},{13,29},{14,30},{15,31},{22,... | collective-permute-start | bytes 983048 | tf_op jit(solution)/shard_map/ppermute | solution.py:26
  389.0 10.2 %collective-permute-start.47 = (f32[2,32,1280]{2,1,0:T(8,128)S(1)}, f32[2,32,1280]{2,1,0:T(8,128)S(1)}, u32[]{:S(2)}, u32[]{:S(2)}) collective-permute-start(f32[2,32,1280]{2,1,0:T(8,128)S(1)} %get-tuple-element.225), channel_id=1, source_target_pairs={{8,24},{9,25},{10,26},{11,27},{12,28},{13,29},{14,30},{15,31},{22,... | collective-permute-start | bytes 983048 | tf_op jit(solution)/shard_map/ppermute | solution.py:26
  399.2 9.5 %collective-permute-start.48 = (f32[32,1280]{1,0:T(8,128)S(1)}, f32[32,1280]{1,0:T(8,128)S(1)}, u32[]{:S(2)}, u32[]{:S(2)}) collective-permute-start(f32[32,1280]{1,0:T(8,128)S(1)} %get-tuple-element.226), channel_id=1, source_target_pairs={{8,10},{9,11},{10,12},{11,13},{12,14},{13,15},{22,24},{23,25},{24,... | collective-permute-start | bytes 491528 | tf_op jit(solution)/shard_map/ppermute | solution.py:26
  408.7 10.2 %collective-permute-start.46 = (f32[32,1280]{1,0:T(8,128)S(1)}, f32[32,1280]{1,0:T(8,128)S(1)}, u32[]{:S(2)}, u32[]{:S(2)}) collective-permute-start(f32[32,1280]{1,0:T(8,128)S(1)} %get-tuple-element.224), channel_id=1, source_target_pairs={{8,10},{9,11},{10,12},{11,13},{12,14},{13,15},{22,24},{23,25},{24,... | collective-permute-start | bytes 491528 | tf_op jit(solution)/shard_map/ppermute | solution.py:26
  421.5 10.9 %collective-permute-start.53 = (f32[2,32,1280]{2,1,0:T(8,128)S(1)}, f32[2,32,1280]{2,1,0:T(8,128)S(1)}, u32[]{:S(2)}, u32[]{:S(2)}) collective-permute-start(f32[2,32,1280]{2,1,0:T(8,128)S(1)} %get-tuple-element.233), channel_id=1, source_target_pairs={{10,26},{11,27},{12,28},{13,29},{14,30},{15,31},{24,40},{25,41},{2... | collective-permute-start | bytes 983048 | tf_op jit(solution)/shard_map/ppermute | solution.py:26
  435.1 10.2 %collective-permute-start.51 = (f32[2,32,1280]{2,1,0:T(8,128)S(1)}, f32[2,32,1280]{2,1,0:T(8,128)S(1)}, u32[]{:S(2)}, u32[]{:S(2)}) collective-permute-start(f32[2,32,1280]{2,1,0:T(8,128)S(1)} %get-tuple-element.231), channel_id=1, source_target_pairs={{10,26},{11,27},{12,28},{13,29},{14,30},{15,31},{24,40},{25,41},{2... | collective-permute-start | bytes 983048 | tf_op jit(solution)/shard_map/ppermute | solution.py:26
  445.3 9.5 %collective-permute-start.52 = (f32[32,1280]{1,0:T(8,128)S(1)}, f32[32,1280]{1,0:T(8,128)S(1)}, u32[]{:S(2)}, u32[]{:S(2)}) collective-permute-start(f32[32,1280]{1,0:T(8,128)S(1)} %get-tuple-element.232), channel_id=1, source_target_pairs={{10,12},{11,13},{12,14},{13,15},{24,26},{25,27},{26,28},{27,29},{2... | collective-permute-start | bytes 491528 | tf_op jit(solution)/shard_map/ppermute | solution.py:26
  454.8 10.2 %collective-permute-start.50 = (f32[32,1280]{1,0:T(8,128)S(1)}, f32[32,1280]{1,0:T(8,128)S(1)}, u32[]{:S(2)}, u32[]{:S(2)}) collective-permute-start(f32[32,1280]{1,0:T(8,128)S(1)} %get-tuple-element.230), channel_id=1, source_target_pairs={{10,12},{11,13},{12,14},{13,15},{24,26},{25,27},{26,28},{27,29},{2... | collective-permute-start | bytes 491528 | tf_op jit(solution)/shard_map/ppermute | solution.py:26
  467.6 10.9 %collective-permute-start.57 = (f32[2,32,1280]{2,1,0:T(8,128)S(1)}, f32[2,32,1280]{2,1,0:T(8,128)S(1)}, u32[]{:S(2)}, u32[]{:S(2)}) collective-permute-start(f32[2,32,1280]{2,1,0:T(8,128)S(1)} %get-tuple-element.239), channel_id=1, source_target_pairs={{12,28},{13,29},{14,30},{15,31},{26,42},{27,43},{28,44},{29,45},{3... | collective-permute-start | bytes 983048 | tf_op jit(solution)/shard_map/ppermute | solution.py:26
  481.2 10.2 %collective-permute-start.55 = (f32[2,32,1280]{2,1,0:T(8,128)S(1)}, f32[2,32,1280]{2,1,0:T(8,128)S(1)}, u32[]{:S(2)}, u32[]{:S(2)}) collective-permute-start(f32[2,32,1280]{2,1,0:T(8,128)S(1)} %get-tuple-element.237), channel_id=1, source_target_pairs={{12,28},{13,29},{14,30},{15,31},{26,42},{27,43},{28,44},{29,45},{3... | collective-permute-start | bytes 983048 | tf_op jit(solution)/shard_map/ppermute | solution.py:26
  491.4 9.5 %collective-permute-start.56 = (f32[32,1280]{1,0:T(8,128)S(1)}, f32[32,1280]{1,0:T(8,128)S(1)}, u32[]{:S(2)}, u32[]{:S(2)}) collective-permute-start(f32[32,1280]{1,0:T(8,128)S(1)} %get-tuple-element.238), channel_id=1, source_target_pairs={{12,14},{13,15},{26,28},{27,29},{28,30},{29,31},{40,42},{41,43},{4... | collective-permute-start | bytes 491528 | tf_op jit(solution)/shard_map/ppermute | solution.py:26
  500.9 10.2 %collective-permute-start.54 = (f32[32,1280]{1,0:T(8,128)S(1)}, f32[32,1280]{1,0:T(8,128)S(1)}, u32[]{:S(2)}, u32[]{:S(2)}) collective-permute-start(f32[32,1280]{1,0:T(8,128)S(1)} %get-tuple-element.236), channel_id=1, source_target_pairs={{12,14},{13,15},{26,28},{27,29},{28,30},{29,31},{40,42},{41,43},{4... | collective-permute-start | bytes 491528 | tf_op jit(solution)/shard_map/ppermute | solution.py:26
  513.7 10.9 %collective-permute-start.61 = (f32[2,32,1280]{2,1,0:T(8,128)S(1)}, f32[2,32,1280]{2,1,0:T(8,128)S(1)}, u32[]{:S(2)}, u32[]{:S(2)}) collective-permute-start(f32[2,32,1280]{2,1,0:T(8,128)S(1)} %get-tuple-element.245), channel_id=1, source_target_pairs={{14,30},{15,31},{28,44},{29,45},{30,46},{31,47},{42,58},{43,59},{4... | collective-permute-start | bytes 983048 | tf_op jit(solution)/shard_map/ppermute | solution.py:26
  527.3 10.2 %collective-permute-start.59 = (f32[2,32,1280]{2,1,0:T(8,128)S(1)}, f32[2,32,1280]{2,1,0:T(8,128)S(1)}, u32[]{:S(2)}, u32[]{:S(2)}) collective-permute-start(f32[2,32,1280]{2,1,0:T(8,128)S(1)} %get-tuple-element.243), channel_id=1, source_target_pairs={{14,30},{15,31},{28,44},{29,45},{30,46},{31,47},{42,58},{43,59},{4... | collective-permute-start | bytes 983048 | tf_op jit(solution)/shard_map/ppermute | solution.py:26
  537.5 9.5 %collective-permute-start.60 = (f32[32,1280]{1,0:T(8,128)S(1)}, f32[32,1280]{1,0:T(8,128)S(1)}, u32[]{:S(2)}, u32[]{:S(2)}) collective-permute-start(f32[32,1280]{1,0:T(8,128)S(1)} %get-tuple-element.244), channel_id=1, source_target_pairs={{28,30},{29,31},{42,44},{43,45},{44,46},{45,47},{56,58},{57,59},{5... | collective-permute-start | bytes 491528 | tf_op jit(solution)/shard_map/ppermute | solution.py:26
  547.0 10.2 %collective-permute-start.58 = (f32[32,1280]{1,0:T(8,128)S(1)}, f32[32,1280]{1,0:T(8,128)S(1)}, u32[]{:S(2)}, u32[]{:S(2)}) collective-permute-start(f32[32,1280]{1,0:T(8,128)S(1)} %get-tuple-element.242), channel_id=1, source_target_pairs={{28,30},{29,31},{42,44},{43,45},{44,46},{45,47},{56,58},{57,59},{5... | collective-permute-start | bytes 491528 | tf_op jit(solution)/shard_map/ppermute | solution.py:26
  557.2 12.8 %collective-permute-start.65 = (f32[2,32,1280]{2,1,0:T(8,128)S(1)}, f32[2,32,1280]{2,1,0:T(8,128)S(1)}, u32[]{:S(2)}, u32[]{:S(2)}) collective-permute-start(f32[2,32,1280]{2,1,0:T(8,128)S(1)} %get-tuple-element.251), channel_id=1, source_target_pairs={{30,46},{31,47},{44,60},{45,61},{46,62},{47,63},{58,74},{59,75},{6... | collective-permute-start | bytes 983048 | tf_op jit(solution)/shard_map/ppermute | solution.py:26
  570.1 12.8 %collective-permute-start.63 = (f32[2,32,1280]{2,1,0:T(8,128)S(1)}, f32[2,32,1280]{2,1,0:T(8,128)S(1)}, u32[]{:S(2)}, u32[]{:S(2)}) collective-permute-start(f32[2,32,1280]{2,1,0:T(8,128)S(1)} %get-tuple-element.249), channel_id=1, source_target_pairs={{30,46},{31,47},{44,60},{45,61},{46,62},{47,63},{58,74},{59,75},{6... | collective-permute-start | bytes 983048 | tf_op jit(solution)/shard_map/ppermute | solution.py:26
  582.9 10.2 %collective-permute-start.64 = (f32[32,1280]{1,0:T(8,128)S(1)}, f32[32,1280]{1,0:T(8,128)S(1)}, u32[]{:S(2)}, u32[]{:S(2)}) collective-permute-start(f32[32,1280]{1,0:T(8,128)S(1)} %get-tuple-element.250), channel_id=1, source_target_pairs={{44,46},{45,47},{58,60},{59,61},{60,62},{61,63},{72,74},{73,75},{7... | collective-permute-start | bytes 491528 | tf_op jit(solution)/shard_map/ppermute | solution.py:26
  593.1 10.3 %collective-permute-start.62 = (f32[32,1280]{1,0:T(8,128)S(1)}, f32[32,1280]{1,0:T(8,128)S(1)}, u32[]{:S(2)}, u32[]{:S(2)}) collective-permute-start(f32[32,1280]{1,0:T(8,128)S(1)} %get-tuple-element.248), channel_id=1, source_target_pairs={{44,46},{45,47},{58,60},{59,61},{60,62},{61,63},{72,74},{73,75},{7... | collective-permute-start | bytes 491528 | tf_op jit(solution)/shard_map/ppermute | solution.py:26
  603.5 12.8 %collective-permute-start.69 = (f32[2,32,1280]{2,1,0:T(8,128)S(1)}, f32[2,32,1280]{2,1,0:T(8,128)S(1)}, u32[]{:S(2)}, u32[]{:S(2)}) collective-permute-start(f32[2,32,1280]{2,1,0:T(8,128)S(1)} %get-tuple-element.257), channel_id=1, source_target_pairs={{46,62},{47,63},{60,76},{61,77},{62,78},{63,79},{74,90},{75,91},{7... | collective-permute-start | bytes 983048 | tf_op jit(solution)/shard_map/ppermute | solution.py:26
  616.4 12.8 %collective-permute-start.67 = (f32[2,32,1280]{2,1,0:T(8,128)S(1)}, f32[2,32,1280]{2,1,0:T(8,128)S(1)}, u32[]{:S(2)}, u32[]{:S(2)}) collective-permute-start(f32[2,32,1280]{2,1,0:T(8,128)S(1)} %get-tuple-element.255), channel_id=1, source_target_pairs={{46,62},{47,63},{60,76},{61,77},{62,78},{63,79},{74,90},{75,91},{7... | collective-permute-start | bytes 983048 | tf_op jit(solution)/shard_map/ppermute | solution.py:26
  629.2 10.2 %collective-permute-start.68 = (f32[32,1280]{1,0:T(8,128)S(1)}, f32[32,1280]{1,0:T(8,128)S(1)}, u32[]{:S(2)}, u32[]{:S(2)}) collective-permute-start(f32[32,1280]{1,0:T(8,128)S(1)} %get-tuple-element.256), channel_id=1, source_target_pairs={{60,62},{61,63},{74,76},{75,77},{76,78},{77,79},{88,90},{89,91},{9... | collective-permute-start | bytes 491528 | tf_op jit(solution)/shard_map/ppermute | solution.py:26
  639.4 10.2 %collective-permute-start.66 = (f32[32,1280]{1,0:T(8,128)S(1)}, f32[32,1280]{1,0:T(8,128)S(1)}, u32[]{:S(2)}, u32[]{:S(2)}) collective-permute-start(f32[32,1280]{1,0:T(8,128)S(1)} %get-tuple-element.254), channel_id=1, source_target_pairs={{60,62},{61,63},{74,76},{75,77},{76,78},{77,79},{88,90},{89,91},{9... | collective-permute-start | bytes 491528 | tf_op jit(solution)/shard_map/ppermute | solution.py:26
  665.0 5.5 order.2
  672.3 4.4 gather.2
  679.5 64.9 %all-to-all-start = ((f32[8,2,64,512]{3,2,1,0:T(8,128)}), f32[8,2,64,512]{3,2,1,0:T(8,128)}, u32[]{:S(2)}, u32[]{:S(2)}) async-start(f32[8,2,64,512]{3,2,1,0:T(8,128)} %copy-done.6), calls=%async_computation | async-start | bytes 4194304 | tf_op jit(solution)/shard_map/all_to_all | solution.py:357
  746.1 6.1 gather.3
  753.6 22.9 %all-to-all-done = f32[8,2,64,512]{3,2,1,0:T(8,128)} async-done(((f32[8,2,64,512]{3,2,1,0:T(8,128)}), f32[8,2,64,512]{3,2,1,0:T(8,128)}, u32[]{:S(2)}, u32[]{:S(2)}) %all-to-all-start) | async-done | bytes 2097184 | tf_op jit(solution)/shard_map/all_to_all | solution.py:357
  776.5 3.6 all-to-all-start.1
  782.0 7.2 maximum_select_fusion
  789.2 21.7 %all-to-all-done.1 = f32[8,2,64,512]{3,2,1,0:T(8,128)S(1)} async-done(((f32[8,2,64,512]{3,2,1,0:T(8,128)}), f32[8,2,64,512]{3,2,1,0:T(8,128)S(1)}, u32[]{:S(2)}, u32[]{:S(2)}) %all-to-all-start.1) | async-done | bytes 2097184 | tf_op jit(solution)/shard_map/all_to_all | solution.py:359
  (192 shorter events, 76.3 us)
Async XLA Ops:
  0.6 23.6 %collective-permute-start = (f32[1280,1280]{1,0:T(8,128)}, f32[1280,1280]{1,0:T(8,128)}, u32[]{:S(2)}, u32[]{:S(2)}) collective-permute-start(f32[1280,1280]{1,0:T(8,128)} %bitcast.14), channel_id=1, source_target_pairs={{0,1},{1,0},{2,3},{3,2},{4,5},{5,4},{6,7},{7,6},{8,9},{9,8},{10,11... | collective-permute-start | bytes 19660808 | tf_op jit(solution)/shard_map/ppermute | solution.py:31
  5.4 18.8 %collective-permute-start.1 = (f32[4,1280,128]{2,1,0:T(8,128)}, f32[4,1280,128]{2,1,0:T(8,128)S(1)}, u32[]{:S(2)}, u32[]{:S(2)}) collective-permute-start(f32[4,1280,128]{2,1,0:T(8,128)} %pick.1), channel_id=1, source_target_pairs={{0,1},{1,0},{2,3},{3,2},{4,5},{5,4},{6,7},{7,6},{8,9},{9,8},{10,11... | collective-permute-start | bytes 7864328 | tf_op jit(solution)/shard_map/ppermute | solution.py:31
  33.9 2.8 collective-permute-start.3
  36.0 2.8 collective-permute-start.9
  36.8 2.8 collective-permute-start.7
  38.8 2.8 collective-permute-start.13
  39.6 2.8 collective-permute-start.11
  42.4 62.8 %collective-permute-start.15 = (f32[2,32,1280]{2,1,0:T(8,128)S(1)}, f32[2,32,1280]{2,1,0:T(8,128)S(1)}, u32[]{:S(2)}, u32[]{:S(2)}) collective-permute-start(f32[2,32,1280]{2,1,0:T(8,128)S(1)} %get-tuple-element.177), channel_id=1, source_target_pairs={{0,16},{1,17},{2,18},{3,19},{4,20},{5,21},{6,22},{7,23},{16,32},{1... | collective-permute-start | bytes 983048 | tf_op jit(solution)/shard_map/ppermute | solution.py:26
  43.8 61.4 %collective-permute-start.14 = (f32[32,1280]{1,0:T(8,128)S(1)}, f32[32,1280]{1,0:T(8,128)S(1)}, u32[]{:S(2)}, u32[]{:S(2)}) collective-permute-start(f32[32,1280]{1,0:T(8,128)S(1)} %get-tuple-element.176), channel_id=1, source_target_pairs={{0,2},{1,3},{2,4},{3,5},{4,6},{5,7},{6,8},{7,9},{16,18},{17,19},{1... | collective-permute-start | bytes 491528 | tf_op jit(solution)/shard_map/ppermute | solution.py:26
  44.5 71.7 %collective-permute-start.21 = (f32[2,32,1280]{2,1,0:T(8,128)S(1)}, f32[2,32,1280]{2,1,0:T(8,128)S(1)}, u32[]{:S(2)}, u32[]{:S(2)}) collective-permute-start(f32[2,32,1280]{2,1,0:T(8,128)S(1)} %get-tuple-element.185), channel_id=1, source_target_pairs={{0,16},{1,17},{2,18},{3,19},{4,20},{5,21},{6,22},{7,23},{8,24},{9,... | collective-permute-start | bytes 983048 | tf_op jit(solution)/shard_map/ppermute | solution.py:26
  105.2 30.0 %collective-permute-start.19 = (f32[2,32,1280]{2,1,0:T(8,128)S(1)}, f32[2,32,1280]{2,1,0:T(8,128)S(1)}, u32[]{:S(2)}, u32[]{:S(2)}) collective-permute-start(f32[2,32,1280]{2,1,0:T(8,128)S(1)} %get-tuple-element.183), channel_id=1, source_target_pairs={{0,16},{1,17},{2,18},{3,19},{4,20},{5,21},{6,22},{7,23},{8,24},{9,... | collective-permute-start | bytes 983048 | tf_op jit(solution)/shard_map/ppermute | solution.py:26
  115.5 19.8 %collective-permute-start.18 = (f32[32,1280]{1,0:T(8,128)S(1)}, f32[32,1280]{1,0:T(8,128)S(1)}, u32[]{:S(2)}, u32[]{:S(2)}) collective-permute-start(f32[32,1280]{1,0:T(8,128)S(1)} %get-tuple-element.182), channel_id=1, source_target_pairs={{0,2},{1,3},{2,4},{3,5},{4,6},{5,7},{6,8},{7,9},{8,10},{9,11},{16,... | collective-permute-start | bytes 491528 | tf_op jit(solution)/shard_map/ppermute | solution.py:26
  116.2 47.8 %collective-permute-start.25 = (f32[2,32,1280]{2,1,0:T(8,128)S(1)}, f32[2,32,1280]{2,1,0:T(8,128)S(1)}, u32[]{:S(2)}, u32[]{:S(2)}) collective-permute-start(f32[2,32,1280]{2,1,0:T(8,128)S(1)} %get-tuple-element.191), channel_id=1, source_target_pairs={{0,16},{1,17},{2,18},{3,19},{4,20},{5,21},{6,22},{7,23},{8,24},{9,... | collective-permute-start | bytes 983048 | tf_op jit(solution)/shard_map/ppermute | solution.py:26
  135.3 38.4 %collective-permute-start.23 = (f32[2,32,1280]{2,1,0:T(8,128)S(1)}, f32[2,32,1280]{2,1,0:T(8,128)S(1)}, u32[]{:S(2)}, u32[]{:S(2)}) collective-permute-start(f32[2,32,1280]{2,1,0:T(8,128)S(1)} %get-tuple-element.189), channel_id=1, source_target_pairs={{0,16},{1,17},{2,18},{3,19},{4,20},{5,21},{6,22},{7,23},{8,24},{9,... | collective-permute-start | bytes 983048 | tf_op jit(solution)/shard_map/ppermute | solution.py:26
  144.8 19.1 %collective-permute-start.24 = (f32[32,1280]{1,0:T(8,128)S(1)}, f32[32,1280]{1,0:T(8,128)S(1)}, u32[]{:S(2)}, u32[]{:S(2)}) collective-permute-start(f32[32,1280]{1,0:T(8,128)S(1)} %get-tuple-element.190), channel_id=1, source_target_pairs={{0,2},{1,3},{2,4},{3,5},{4,6},{5,7},{6,8},{7,9},{8,10},{9,11},{10,... | collective-permute-start | bytes 491528 | tf_op jit(solution)/shard_map/ppermute | solution.py:26
  154.4 19.2 %collective-permute-start.22 = (f32[32,1280]{1,0:T(8,128)S(1)}, f32[32,1280]{1,0:T(8,128)S(1)}, u32[]{:S(2)}, u32[]{:S(2)}) collective-permute-start(f32[32,1280]{1,0:T(8,128)S(1)} %get-tuple-element.188), channel_id=1, source_target_pairs={{0,2},{1,3},{2,4},{3,5},{4,6},{5,7},{6,8},{7,9},{8,10},{9,11},{10,... | collective-permute-start | bytes 491528 | tf_op jit(solution)/shard_map/ppermute | solution.py:26
  164.0 39.5 %collective-permute-start.29 = (f32[2,32,1280]{2,1,0:T(8,128)S(1)}, f32[2,32,1280]{2,1,0:T(8,128)S(1)}, u32[]{:S(2)}, u32[]{:S(2)}) collective-permute-start(f32[2,32,1280]{2,1,0:T(8,128)S(1)} %get-tuple-element.197), channel_id=1, source_target_pairs={{0,16},{1,17},{2,18},{3,19},{4,20},{5,21},{6,22},{7,23},{8,24},{9,... | collective-permute-start | bytes 983048 | tf_op jit(solution)/shard_map/ppermute | solution.py:26
  173.7 40.9 %collective-permute-start.27 = (f32[2,32,1280]{2,1,0:T(8,128)S(1)}, f32[2,32,1280]{2,1,0:T(8,128)S(1)}, u32[]{:S(2)}, u32[]{:S(2)}) collective-permute-start(f32[2,32,1280]{2,1,0:T(8,128)S(1)} %get-tuple-element.195), channel_id=1, source_target_pairs={{0,16},{1,17},{2,18},{3,19},{4,20},{5,21},{6,22},{7,23},{8,24},{9,... | collective-permute-start | bytes 983048 | tf_op jit(solution)/shard_map/ppermute | solution.py:26
  183.9 19.6 %collective-permute-start.28 = (f32[32,1280]{1,0:T(8,128)S(1)}, f32[32,1280]{1,0:T(8,128)S(1)}, u32[]{:S(2)}, u32[]{:S(2)}) collective-permute-start(f32[32,1280]{1,0:T(8,128)S(1)} %get-tuple-element.196), channel_id=1, source_target_pairs={{0,2},{1,3},{2,4},{3,5},{4,6},{5,7},{6,8},{7,9},{8,10},{9,11},{10,... | collective-permute-start | bytes 491528 | tf_op jit(solution)/shard_map/ppermute | solution.py:26
  193.9 20.6 %collective-permute-start.26 = (f32[32,1280]{1,0:T(8,128)S(1)}, f32[32,1280]{1,0:T(8,128)S(1)}, u32[]{:S(2)}, u32[]{:S(2)}) collective-permute-start(f32[32,1280]{1,0:T(8,128)S(1)} %get-tuple-element.194), channel_id=1, source_target_pairs={{0,2},{1,3},{2,4},{3,5},{4,6},{5,7},{6,8},{7,9},{8,10},{9,11},{10,... | collective-permute-start | bytes 491528 | tf_op jit(solution)/shard_map/ppermute | solution.py:26
  206.1 38.0 %collective-permute-start.33 = (f32[2,32,1280]{2,1,0:T(8,128)S(1)}, f32[2,32,1280]{2,1,0:T(8,128)S(1)}, u32[]{:S(2)}, u32[]{:S(2)}) collective-permute-start(f32[2,32,1280]{2,1,0:T(8,128)S(1)} %get-tuple-element.203), channel_id=1, source_target_pairs={{0,16},{1,17},{2,18},{3,19},{4,20},{5,21},{6,22},{7,23},{8,24},{9,... | collective-permute-start | bytes 983048 | tf_op jit(solution)/shard_map/ppermute | solution.py:26
  217.3 38.6 %collective-permute-start.31 = (f32[2,32,1280]{2,1,0:T(8,128)S(1)}, f32[2,32,1280]{2,1,0:T(8,128)S(1)}, u32[]{:S(2)}, u32[]{:S(2)}) collective-permute-start(f32[2,32,1280]{2,1,0:T(8,128)S(1)} %get-tuple-element.201), channel_id=1, source_target_pairs={{0,16},{1,17},{2,18},{3,19},{4,20},{5,21},{6,22},{7,23},{8,24},{9,... | collective-permute-start | bytes 983048 | tf_op jit(solution)/shard_map/ppermute | solution.py:26
  225.7 18.5 %collective-permute-start.32 = (f32[32,1280]{1,0:T(8,128)S(1)}, f32[32,1280]{1,0:T(8,128)S(1)}, u32[]{:S(2)}, u32[]{:S(2)}) collective-permute-start(f32[32,1280]{1,0:T(8,128)S(1)} %get-tuple-element.202), channel_id=1, source_target_pairs={{0,2},{1,3},{2,4},{3,5},{4,6},{5,7},{6,8},{7,9},{8,10},{9,11},{10,... | collective-permute-start | bytes 491528 | tf_op jit(solution)/shard_map/ppermute | solution.py:26
  234.6 21.3 %collective-permute-start.30 = (f32[32,1280]{1,0:T(8,128)S(1)}, f32[32,1280]{1,0:T(8,128)S(1)}, u32[]{:S(2)}, u32[]{:S(2)}) collective-permute-start(f32[32,1280]{1,0:T(8,128)S(1)} %get-tuple-element.200), channel_id=1, source_target_pairs={{0,2},{1,3},{2,4},{3,5},{4,6},{5,7},{6,8},{7,9},{8,10},{9,11},{10,... | collective-permute-start | bytes 491528 | tf_op jit(solution)/shard_map/ppermute | solution.py:26
  246.8 38.8 %collective-permute-start.37 = (f32[2,32,1280]{2,1,0:T(8,128)S(1)}, f32[2,32,1280]{2,1,0:T(8,128)S(1)}, u32[]{:S(2)}, u32[]{:S(2)}) collective-permute-start(f32[2,32,1280]{2,1,0:T(8,128)S(1)} %get-tuple-element.209), channel_id=1, source_target_pairs={{2,18},{3,19},{4,20},{5,21},{6,22},{7,23},{8,24},{9,25},{10,26},{1... | collective-permute-start | bytes 983048 | tf_op jit(solution)/shard_map/ppermute | solution.py:26
  258.6 39.0 %collective-permute-start.35 = (f32[2,32,1280]{2,1,0:T(8,128)S(1)}, f32[2,32,1280]{2,1,0:T(8,128)S(1)}, u32[]{:S(2)}, u32[]{:S(2)}) collective-permute-start(f32[2,32,1280]{2,1,0:T(8,128)S(1)} %get-tuple-element.207), channel_id=1, source_target_pairs={{2,18},{3,19},{4,20},{5,21},{6,22},{7,23},{8,24},{9,25},{10,26},{1... | collective-permute-start | bytes 983048 | tf_op jit(solution)/shard_map/ppermute | solution.py:26
  267.2 18.5 %collective-permute-start.36 = (f32[32,1280]{1,0:T(8,128)S(1)}, f32[32,1280]{1,0:T(8,128)S(1)}, u32[]{:S(2)}, u32[]{:S(2)}) collective-permute-start(f32[32,1280]{1,0:T(8,128)S(1)} %get-tuple-element.208), channel_id=1, source_target_pairs={{2,4},{3,5},{4,6},{5,7},{6,8},{7,9},{8,10},{9,11},{10,12},{11,13},... | collective-permute-start | bytes 491528 | tf_op jit(solution)/shard_map/ppermute | solution.py:26
  276.1 21.5 %collective-permute-start.34 = (f32[32,1280]{1,0:T(8,128)S(1)}, f32[32,1280]{1,0:T(8,128)S(1)}, u32[]{:S(2)}, u32[]{:S(2)}) collective-permute-start(f32[32,1280]{1,0:T(8,128)S(1)} %get-tuple-element.206), channel_id=1, source_target_pairs={{2,4},{3,5},{4,6},{5,7},{6,8},{7,9},{8,10},{9,11},{10,12},{11,13},... | collective-permute-start | bytes 491528 | tf_op jit(solution)/shard_map/ppermute | solution.py:26
  288.3 39.1 %collective-permute-start.41 = (f32[2,32,1280]{2,1,0:T(8,128)S(1)}, f32[2,32,1280]{2,1,0:T(8,128)S(1)}, u32[]{:S(2)}, u32[]{:S(2)}) collective-permute-start(f32[2,32,1280]{2,1,0:T(8,128)S(1)} %get-tuple-element.215), channel_id=1, source_target_pairs={{4,20},{5,21},{6,22},{7,23},{8,24},{9,25},{10,26},{11,27},{12,28},... | collective-permute-start | bytes 983048 | tf_op jit(solution)/shard_map/ppermute | solution.py:26
  300.3 40.0 %collective-permute-start.39 = (f32[2,32,1280]{2,1,0:T(8,128)S(1)}, f32[2,32,1280]{2,1,0:T(8,128)S(1)}, u32[]{:S(2)}, u32[]{:S(2)}) collective-permute-start(f32[2,32,1280]{2,1,0:T(8,128)S(1)} %get-tuple-element.213), channel_id=1, source_target_pairs={{4,20},{5,21},{6,22},{7,23},{8,24},{9,25},{10,26},{11,27},{12,28},... | collective-permute-start | bytes 983048 | tf_op jit(solution)/shard_map/ppermute | solution.py:26
  308.9 18.4 %collective-permute-start.40 = (f32[32,1280]{1,0:T(8,128)S(1)}, f32[32,1280]{1,0:T(8,128)S(1)}, u32[]{:S(2)}, u32[]{:S(2)}) collective-permute-start(f32[32,1280]{1,0:T(8,128)S(1)} %get-tuple-element.214), channel_id=1, source_target_pairs={{4,6},{5,7},{6,8},{7,9},{8,10},{9,11},{10,12},{11,13},{12,14},{13,... | collective-permute-start | bytes 491528 | tf_op jit(solution)/shard_map/ppermute | solution.py:26
  317.8 22.4 %collective-permute-start.38 = (f32[32,1280]{1,0:T(8,128)S(1)}, f32[32,1280]{1,0:T(8,128)S(1)}, u32[]{:S(2)}, u32[]{:S(2)}) collective-permute-start(f32[32,1280]{1,0:T(8,128)S(1)} %get-tuple-element.212), channel_id=1, source_target_pairs={{4,6},{5,7},{6,8},{7,9},{8,10},{9,11},{10,12},{11,13},{12,14},{13,... | collective-permute-start | bytes 491528 | tf_op jit(solution)/shard_map/ppermute | solution.py:26
  330.0 42.8 %collective-permute-start.45 = (f32[2,32,1280]{2,1,0:T(8,128)S(1)}, f32[2,32,1280]{2,1,0:T(8,128)S(1)}, u32[]{:S(2)}, u32[]{:S(2)}) collective-permute-start(f32[2,32,1280]{2,1,0:T(8,128)S(1)} %get-tuple-element.221), channel_id=1, source_target_pairs={{6,22},{7,23},{8,24},{9,25},{10,26},{11,27},{12,28},{13,29},{14,30... | collective-permute-start | bytes 983048 | tf_op jit(solution)/shard_map/ppermute | solution.py:26
  342.9 43.4 %collective-permute-start.43 = (f32[2,32,1280]{2,1,0:T(8,128)S(1)}, f32[2,32,1280]{2,1,0:T(8,128)S(1)}, u32[]{:S(2)}, u32[]{:S(2)}) collective-permute-start(f32[2,32,1280]{2,1,0:T(8,128)S(1)} %get-tuple-element.219), channel_id=1, source_target_pairs={{6,22},{7,23},{8,24},{9,25},{10,26},{11,27},{12,28},{13,29},{14,30... | collective-permute-start | bytes 983048 | tf_op jit(solution)/shard_map/ppermute | solution.py:26
  353.1 19.7 %collective-permute-start.44 = (f32[32,1280]{1,0:T(8,128)S(1)}, f32[32,1280]{1,0:T(8,128)S(1)}, u32[]{:S(2)}, u32[]{:S(2)}) collective-permute-start(f32[32,1280]{1,0:T(8,128)S(1)} %get-tuple-element.220), channel_id=1, source_target_pairs={{6,8},{7,9},{8,10},{9,11},{10,12},{11,13},{12,14},{13,15},{20,22},... | collective-permute-start | bytes 491528 | tf_op jit(solution)/shard_map/ppermute | solution.py:26
  362.6 23.7 %collective-permute-start.42 = (f32[32,1280]{1,0:T(8,128)S(1)}, f32[32,1280]{1,0:T(8,128)S(1)}, u32[]{:S(2)}, u32[]{:S(2)}) collective-permute-start(f32[32,1280]{1,0:T(8,128)S(1)} %get-tuple-element.218), channel_id=1, source_target_pairs={{6,8},{7,9},{8,10},{9,11},{10,12},{11,13},{12,14},{13,15},{20,22},... | collective-permute-start | bytes 491528 | tf_op jit(solution)/shard_map/ppermute | solution.py:26
  375.4 43.5 %collective-permute-start.49 = (f32[2,32,1280]{2,1,0:T(8,128)S(1)}, f32[2,32,1280]{2,1,0:T(8,128)S(1)}, u32[]{:S(2)}, u32[]{:S(2)}) collective-permute-start(f32[2,32,1280]{2,1,0:T(8,128)S(1)} %get-tuple-element.227), channel_id=1, source_target_pairs={{8,24},{9,25},{10,26},{11,27},{12,28},{13,29},{14,30},{15,31},{22,... | collective-permute-start | bytes 983048 | tf_op jit(solution)/shard_map/ppermute | solution.py:26
  389.0 43.4 %collective-permute-start.47 = (f32[2,32,1280]{2,1,0:T(8,128)S(1)}, f32[2,32,1280]{2,1,0:T(8,128)S(1)}, u32[]{:S(2)}, u32[]{:S(2)}) collective-permute-start(f32[2,32,1280]{2,1,0:T(8,128)S(1)} %get-tuple-element.225), channel_id=1, source_target_pairs={{8,24},{9,25},{10,26},{11,27},{12,28},{13,29},{14,30},{15,31},{22,... | collective-permute-start | bytes 983048 | tf_op jit(solution)/shard_map/ppermute | solution.py:26
  399.2 19.7 %collective-permute-start.48 = (f32[32,1280]{1,0:T(8,128)S(1)}, f32[32,1280]{1,0:T(8,128)S(1)}, u32[]{:S(2)}, u32[]{:S(2)}) collective-permute-start(f32[32,1280]{1,0:T(8,128)S(1)} %get-tuple-element.226), channel_id=1, source_target_pairs={{8,10},{9,11},{10,12},{11,13},{12,14},{13,15},{22,24},{23,25},{24,... | collective-permute-start | bytes 491528 | tf_op jit(solution)/shard_map/ppermute | solution.py:26
  408.7 23.7 %collective-permute-start.46 = (f32[32,1280]{1,0:T(8,128)S(1)}, f32[32,1280]{1,0:T(8,128)S(1)}, u32[]{:S(2)}, u32[]{:S(2)}) collective-permute-start(f32[32,1280]{1,0:T(8,128)S(1)} %get-tuple-element.224), channel_id=1, source_target_pairs={{8,10},{9,11},{10,12},{11,13},{12,14},{13,15},{22,24},{23,25},{24,... | collective-permute-start | bytes 491528 | tf_op jit(solution)/shard_map/ppermute | solution.py:26
  421.5 43.4 %collective-permute-start.53 = (f32[2,32,1280]{2,1,0:T(8,128)S(1)}, f32[2,32,1280]{2,1,0:T(8,128)S(1)}, u32[]{:S(2)}, u32[]{:S(2)}) collective-permute-start(f32[2,32,1280]{2,1,0:T(8,128)S(1)} %get-tuple-element.233), channel_id=1, source_target_pairs={{10,26},{11,27},{12,28},{13,29},{14,30},{15,31},{24,40},{25,41},{2... | collective-permute-start | bytes 983048 | tf_op jit(solution)/shard_map/ppermute | solution.py:26
  435.1 43.4 %collective-permute-start.51 = (f32[2,32,1280]{2,1,0:T(8,128)S(1)}, f32[2,32,1280]{2,1,0:T(8,128)S(1)}, u32[]{:S(2)}, u32[]{:S(2)}) collective-permute-start(f32[2,32,1280]{2,1,0:T(8,128)S(1)} %get-tuple-element.231), channel_id=1, source_target_pairs={{10,26},{11,27},{12,28},{13,29},{14,30},{15,31},{24,40},{25,41},{2... | collective-permute-start | bytes 983048 | tf_op jit(solution)/shard_map/ppermute | solution.py:26
  445.3 19.7 %collective-permute-start.52 = (f32[32,1280]{1,0:T(8,128)S(1)}, f32[32,1280]{1,0:T(8,128)S(1)}, u32[]{:S(2)}, u32[]{:S(2)}) collective-permute-start(f32[32,1280]{1,0:T(8,128)S(1)} %get-tuple-element.232), channel_id=1, source_target_pairs={{10,12},{11,13},{12,14},{13,15},{24,26},{25,27},{26,28},{27,29},{2... | collective-permute-start | bytes 491528 | tf_op jit(solution)/shard_map/ppermute | solution.py:26
  454.8 23.7 %collective-permute-start.50 = (f32[32,1280]{1,0:T(8,128)S(1)}, f32[32,1280]{1,0:T(8,128)S(1)}, u32[]{:S(2)}, u32[]{:S(2)}) collective-permute-start(f32[32,1280]{1,0:T(8,128)S(1)} %get-tuple-element.230), channel_id=1, source_target_pairs={{10,12},{11,13},{12,14},{13,15},{24,26},{25,27},{26,28},{27,29},{2... | collective-permute-start | bytes 491528 | tf_op jit(solution)/shard_map/ppermute | solution.py:26
  467.6 43.5 %collective-permute-start.57 = (f32[2,32,1280]{2,1,0:T(8,128)S(1)}, f32[2,32,1280]{2,1,0:T(8,128)S(1)}, u32[]{:S(2)}, u32[]{:S(2)}) collective-permute-start(f32[2,32,1280]{2,1,0:T(8,128)S(1)} %get-tuple-element.239), channel_id=1, source_target_pairs={{12,28},{13,29},{14,30},{15,31},{26,42},{27,43},{28,44},{29,45},{3... | collective-permute-start | bytes 983048 | tf_op jit(solution)/shard_map/ppermute | solution.py:26
  481.2 43.4 %collective-permute-start.55 = (f32[2,32,1280]{2,1,0:T(8,128)S(1)}, f32[2,32,1280]{2,1,0:T(8,128)S(1)}, u32[]{:S(2)}, u32[]{:S(2)}) collective-permute-start(f32[2,32,1280]{2,1,0:T(8,128)S(1)} %get-tuple-element.237), channel_id=1, source_target_pairs={{12,28},{13,29},{14,30},{15,31},{26,42},{27,43},{28,44},{29,45},{3... | collective-permute-start | bytes 983048 | tf_op jit(solution)/shard_map/ppermute | solution.py:26
  491.4 19.7 %collective-permute-start.56 = (f32[32,1280]{1,0:T(8,128)S(1)}, f32[32,1280]{1,0:T(8,128)S(1)}, u32[]{:S(2)}, u32[]{:S(2)}) collective-permute-start(f32[32,1280]{1,0:T(8,128)S(1)} %get-tuple-element.238), channel_id=1, source_target_pairs={{12,14},{13,15},{26,28},{27,29},{28,30},{29,31},{40,42},{41,43},{4... | collective-permute-start | bytes 491528 | tf_op jit(solution)/shard_map/ppermute | solution.py:26
  500.9 23.7 %collective-permute-start.54 = (f32[32,1280]{1,0:T(8,128)S(1)}, f32[32,1280]{1,0:T(8,128)S(1)}, u32[]{:S(2)}, u32[]{:S(2)}) collective-permute-start(f32[32,1280]{1,0:T(8,128)S(1)} %get-tuple-element.236), channel_id=1, source_target_pairs={{12,14},{13,15},{26,28},{27,29},{28,30},{29,31},{40,42},{41,43},{4... | collective-permute-start | bytes 491528 | tf_op jit(solution)/shard_map/ppermute | solution.py:26
  513.7 43.5 %collective-permute-start.61 = (f32[2,32,1280]{2,1,0:T(8,128)S(1)}, f32[2,32,1280]{2,1,0:T(8,128)S(1)}, u32[]{:S(2)}, u32[]{:S(2)}) collective-permute-start(f32[2,32,1280]{2,1,0:T(8,128)S(1)} %get-tuple-element.245), channel_id=1, source_target_pairs={{14,30},{15,31},{28,44},{29,45},{30,46},{31,47},{42,58},{43,59},{4... | collective-permute-start | bytes 983048 | tf_op jit(solution)/shard_map/ppermute | solution.py:26
  527.3 42.8 %collective-permute-start.59 = (f32[2,32,1280]{2,1,0:T(8,128)S(1)}, f32[2,32,1280]{2,1,0:T(8,128)S(1)}, u32[]{:S(2)}, u32[]{:S(2)}) collective-permute-start(f32[2,32,1280]{2,1,0:T(8,128)S(1)} %get-tuple-element.243), channel_id=1, source_target_pairs={{14,30},{15,31},{28,44},{29,45},{30,46},{31,47},{42,58},{43,59},{4... | collective-permute-start | bytes 983048 | tf_op jit(solution)/shard_map/ppermute | solution.py:26
  537.5 19.7 %collective-permute-start.60 = (f32[32,1280]{1,0:T(8,128)S(1)}, f32[32,1280]{1,0:T(8,128)S(1)}, u32[]{:S(2)}, u32[]{:S(2)}) collective-permute-start(f32[32,1280]{1,0:T(8,128)S(1)} %get-tuple-element.244), channel_id=1, source_target_pairs={{28,30},{29,31},{42,44},{43,45},{44,46},{45,47},{56,58},{57,59},{5... | collective-permute-start | bytes 491528 | tf_op jit(solution)/shard_map/ppermute | solution.py:26
  547.0 23.1 %collective-permute-start.58 = (f32[32,1280]{1,0:T(8,128)S(1)}, f32[32,1280]{1,0:T(8,128)S(1)}, u32[]{:S(2)}, u32[]{:S(2)}) collective-permute-start(f32[32,1280]{1,0:T(8,128)S(1)} %get-tuple-element.242), channel_id=1, source_target_pairs={{28,30},{29,31},{42,44},{43,45},{44,46},{45,47},{56,58},{57,59},{5... | collective-permute-start | bytes 491528 | tf_op jit(solution)/shard_map/ppermute | solution.py:26
  557.2 46.2 %collective-permute-start.65 = (f32[2,32,1280]{2,1,0:T(8,128)S(1)}, f32[2,32,1280]{2,1,0:T(8,128)S(1)}, u32[]{:S(2)}, u32[]{:S(2)}) collective-permute-start(f32[2,32,1280]{2,1,0:T(8,128)S(1)} %get-tuple-element.251), channel_id=1, source_target_pairs={{30,46},{31,47},{44,60},{45,61},{46,62},{47,63},{58,74},{59,75},{6... | collective-permute-start | bytes 983048 | tf_op jit(solution)/shard_map/ppermute | solution.py:26
  570.1 46.2 %collective-permute-start.63 = (f32[2,32,1280]{2,1,0:T(8,128)S(1)}, f32[2,32,1280]{2,1,0:T(8,128)S(1)}, u32[]{:S(2)}, u32[]{:S(2)}) collective-permute-start(f32[2,32,1280]{2,1,0:T(8,128)S(1)} %get-tuple-element.249), channel_id=1, source_target_pairs={{30,46},{31,47},{44,60},{45,61},{46,62},{47,63},{58,74},{59,75},{6... | collective-permute-start | bytes 983048 | tf_op jit(solution)/shard_map/ppermute | solution.py:26
  582.9 20.5 %collective-permute-start.64 = (f32[32,1280]{1,0:T(8,128)S(1)}, f32[32,1280]{1,0:T(8,128)S(1)}, u32[]{:S(2)}, u32[]{:S(2)}) collective-permute-start(f32[32,1280]{1,0:T(8,128)S(1)} %get-tuple-element.250), channel_id=1, source_target_pairs={{44,46},{45,47},{58,60},{59,61},{60,62},{61,63},{72,74},{73,75},{7... | collective-permute-start | bytes 491528 | tf_op jit(solution)/shard_map/ppermute | solution.py:26
  593.1 23.2 %collective-permute-start.62 = (f32[32,1280]{1,0:T(8,128)S(1)}, f32[32,1280]{1,0:T(8,128)S(1)}, u32[]{:S(2)}, u32[]{:S(2)}) collective-permute-start(f32[32,1280]{1,0:T(8,128)S(1)} %get-tuple-element.248), channel_id=1, source_target_pairs={{44,46},{45,47},{58,60},{59,61},{60,62},{61,63},{72,74},{73,75},{7... | collective-permute-start | bytes 491528 | tf_op jit(solution)/shard_map/ppermute | solution.py:26
  603.5 46.1 %collective-permute-start.69 = (f32[2,32,1280]{2,1,0:T(8,128)S(1)}, f32[2,32,1280]{2,1,0:T(8,128)S(1)}, u32[]{:S(2)}, u32[]{:S(2)}) collective-permute-start(f32[2,32,1280]{2,1,0:T(8,128)S(1)} %get-tuple-element.257), channel_id=1, source_target_pairs={{46,62},{47,63},{60,76},{61,77},{62,78},{63,79},{74,90},{75,91},{7... | collective-permute-start | bytes 983048 | tf_op jit(solution)/shard_map/ppermute | solution.py:26
  616.4 33.9 %collective-permute-start.67 = (f32[2,32,1280]{2,1,0:T(8,128)S(1)}, f32[2,32,1280]{2,1,0:T(8,128)S(1)}, u32[]{:S(2)}, u32[]{:S(2)}) collective-permute-start(f32[2,32,1280]{2,1,0:T(8,128)S(1)} %get-tuple-element.255), channel_id=1, source_target_pairs={{46,62},{47,63},{60,76},{61,77},{62,78},{63,79},{74,90},{75,91},{7... | collective-permute-start | bytes 983048 | tf_op jit(solution)/shard_map/ppermute | solution.py:26
  629.2 20.4 %collective-permute-start.68 = (f32[32,1280]{1,0:T(8,128)S(1)}, f32[32,1280]{1,0:T(8,128)S(1)}, u32[]{:S(2)}, u32[]{:S(2)}) collective-permute-start(f32[32,1280]{1,0:T(8,128)S(1)} %get-tuple-element.256), channel_id=1, source_target_pairs={{60,62},{61,63},{74,76},{75,77},{76,78},{77,79},{88,90},{89,91},{9... | collective-permute-start | bytes 491528 | tf_op jit(solution)/shard_map/ppermute | solution.py:26
  639.4 10.9 %collective-permute-start.66 = (f32[32,1280]{1,0:T(8,128)S(1)}, f32[32,1280]{1,0:T(8,128)S(1)}, u32[]{:S(2)}, u32[]{:S(2)}) collective-permute-start(f32[32,1280]{1,0:T(8,128)S(1)} %get-tuple-element.254), channel_id=1, source_target_pairs={{60,62},{61,63},{74,76},{75,77},{76,78},{77,79},{88,90},{89,91},{9... | collective-permute-start | bytes 491528 | tf_op jit(solution)/shard_map/ppermute | solution.py:26
  658.8 2.9 collective-permute-start.83
  664.8 79.6 %collective-permute-start.86 = (f32[512,1280]{1,0:T(8,128)}, f32[512,1280]{1,0:T(8,128)}, u32[]{:S(2)}, u32[]{:S(2)}) collective-permute-start(f32[512,1280]{1,0:T(8,128)} %get-tuple-element.294), channel_id=1, source_target_pairs={{0,1},{1,0},{2,3},{3,2},{4,5},{5,4},{6,7},{7,6},{8,9},{9,8},{10,11... | collective-permute-start | bytes 7864328 | tf_op jit(solution)/shard_map/ppermute | solution.py:31
  679.5 97.0 %all-to-all-start = ((f32[8,2,64,512]{3,2,1,0:T(8,128)}), f32[8,2,64,512]{3,2,1,0:T(8,128)}, u32[]{:S(2)}, u32[]{:S(2)}) async-start(f32[8,2,64,512]{3,2,1,0:T(8,128)} %copy-done.6), calls=%async_computation | async-start | bytes 4194304 | tf_op jit(solution)/shard_map/all_to_all | solution.py:357
  776.5 34.4 %all-to-all-start.1 = ((f32[8,2,64,512]{3,2,1,0:T(8,128)}), f32[8,2,64,512]{3,2,1,0:T(8,128)S(1)}, u32[]{:S(2)}, u32[]{:S(2)}) async-start(f32[8,2,64,512]{3,2,1,0:T(8,128)} %copy-done.5), calls=%async_computation.1 | async-start | bytes 4194304 | tf_op jit(solution)/shard_map/all_to_all | solution.py:359
  (33 other events, 88.4 us)
